TPU v7x, 256 devices: a whole 4x4x8 slice. The times are simulated.
256 devices in a mesh: section: 2 (over core), fsdp: 8 (over y, x_hi), tp: 16 (over z, x_lo).
Axes of the slice: x: 4 (x_hi: 2, x_lo: 2; x = x_hi * 2 + x_lo), y: 4, z: 8, core: 2. Of those that a mesh axis runs over, the one named last changes fastest.
Arguments:
- saved_inputs: bfloat16 [2, 8, 512, 2560], P('section', None, 'fsdp', 'tp'), may hold values from -6 to 6
- top_grad: bfloat16 [8, 512, 2560], P(None, 'fsdp', 'tp'), may hold values from -6 to 6
- norm_gain: float32 [2, 2560], P('section'), may hold values from 0.5 to 1.5
- gate_weight: bfloat16 [2, 2560, 6912], P('section', 'fsdp', 'tp'), may hold values from -0.125 to 0.125
- up_weight: bfloat16 [2, 2560, 6912], P('section', 'fsdp', 'tp'), may hold values from -0.125 to 0.125
- down_weight: bfloat16 [2, 6912, 2560], P('section', 'tp', 'fsdp'), may hold values from -0.078125 to 0.078125
Outputs:
- input_grads: bfloat16 [2, 8, 512, 2560], P('section', None, 'fsdp', 'tp')
- gate_grad: float32 [2, 2560, 6912], P('section', 'fsdp', 'tp')
- up_grad: float32 [2, 2560, 6912], P('section', 'fsdp', 'tp')
- down_grad: float32 [2, 6912, 2560], P('section', 'tp', 'fsdp')
- gain_grad: float32 [2, 2560], P('section', 'tp')
All inputs are finite; a program needn't handle non-finite values.
Results may differ from a plain program's by a relative error of at most 0.0055.
Values may be sent and summed in bfloat16 or wider, within the bound.
A program may use at most 128 MiB of HBM per device.

v0:
```python
import jax
import jax.numpy as jnp
from jax import lax
from jax.sharding import Mesh
from jax.sharding import PartitionSpec as P

TP = ("tp_0", "tp_1")


epsilon = 1e-05


def joined_along(tiles, dim):
    shape = list(tiles.shape[1:])
    shape[dim] *= tiles.shape[0]
    return jnp.moveaxis(tiles, 0, dim).reshape(shape)


def one_gather(arrays, axis, dims):
    vector = jnp.concatenate([a.reshape(-1) for a in arrays])
    lines, at, finished = lax.all_gather(vector, axis), 0, []
    for a, dim in zip(arrays, dims):
        tiles = lines[:, at : at + a.size].reshape(-1, *a.shape)
        finished.append(joined_along(tiles, dim))
        at += a.size
    return tuple(finished)


def gathered_by_axis(x, axes, dim):
    for axis in reversed(axes):
        x = lax.all_gather(x, axis, axis=dim, tiled=True)
    return x


def as_sent(x):
    def short(part):
        return part.astype(jnp.bfloat16) if part.dtype == jnp.float32 else part

    return jax.tree.map(short, x)


def sum_by_axis(x, axes, dim):
    if not axes:
        return x
    nearer = lax.psum_scatter(x, axes[0], scatter_dimension=dim, tiled=True)
    return sum_by_axis(nearer, axes[1:], dim)


def passed_along(value, axis, steps):
    count = lax.axis_size(axis)
    initial, last = max(0, -steps), min(count, count - steps)
    return lax.ppermute(value, axis, [(source, source + steps) for source in range(initial, last)])


def select_micro(buffer, micro_index):
    return lax.dynamic_index_in_dim(buffer, micro_index, 0, keepdims=False)


def store_micro(buffer, micro_index, update, condition):
    previous = select_micro(buffer, micro_index)
    return lax.dynamic_update_index_in_dim(
        buffer, jnp.where(condition, update, previous), micro_index, 0
    )


def contract_rows(left, right):
    return lax.dot_general(
        left, right, (((0,), (0,)), ((), ())), preferred_element_type=jnp.float32
    )


def contract_cols(left, right):
    return lax.dot_general(
        left, right, (((1,), (1,)), ((), ())), preferred_element_type=jnp.float32
    )


def body(saved_inputs, top_grad, norm_gain, gate_weight, up_weight, down_weight):
    section_count = lax.axis_size("section")
    section_index = lax.axis_index("section")
    tp_count = lax.axis_size(TP)
    micro_count = saved_inputs.shape[1]
    row_count = saved_inputs.shape[2]
    local_width = saved_inputs.shape[3]
    full_width = local_width * tp_count
    w_gate, w_up, w_down = one_gather(
        (gate_weight[0], up_weight[0], down_weight[0]), "fsdp", (0, 0, 1)
    )
    hidden_width = w_gate.shape[1]
    gain_full = norm_gain[0]
    column_start = lax.axis_index(TP) * local_width
    gain_local = lax.dynamic_slice_in_dim(gain_full, column_start, local_width)
    inputs_local = saved_inputs[0]
    inputs_full = gathered_by_axis(inputs_local, TP, 2)
    inputs_wide = inputs_full.astype(jnp.float32)
    row_scale = lax.rsqrt(jnp.mean(inputs_wide * inputs_wide, axis=-1, keepdims=True) + epsilon)
    normed = (inputs_wide * row_scale * gain_full).astype(jnp.bfloat16)
    gate_pre = jnp.einsum("mtd,df->mtf", normed, w_gate, preferred_element_type=jnp.float32)
    upward = jnp.einsum("mtd,df->mtf", normed, w_up, preferred_element_type=jnp.float32)
    gate_sigmoid = jax.nn.sigmoid(gate_pre)
    silu_out = gate_pre * gate_sigmoid
    hidden = (silu_out * upward).astype(jnp.bfloat16)
    last_section = section_index == section_count - 1

    def one_tick(tick_number, loop_state):
        received, grads_out, gain_total, stored = loop_state
        micro_raw = tick_number - (section_count - 1 - section_index)
        is_valid = (micro_raw >= 0) & (micro_raw < micro_count)
        micro_index = jnp.clip(micro_raw, 0, micro_count - 1)
        top_piece = select_micro(top_grad, micro_index)
        cotangent = jnp.where(last_section, top_piece, received)
        full_cotangent = gathered_by_axis(as_sent(cotangent), TP, 1).astype(cotangent.dtype)
        gate_now = select_micro(gate_pre, micro_index)
        upward_now = select_micro(upward, micro_index)
        sigmoid_now = select_micro(gate_sigmoid, micro_index)
        silu_now = select_micro(silu_out, micro_index)
        d_hidden = contract_cols(full_cotangent, w_down)
        d_gate = (
            d_hidden * upward_now * sigmoid_now * (1.0 + gate_now * (1.0 - sigmoid_now))
        ).astype(jnp.bfloat16)
        d_up = (d_hidden * silu_now).astype(jnp.bfloat16)
        partial_value = contract_cols(d_gate, w_gate) + contract_cols(d_up, w_up)
        scale_now = select_micro(row_scale, micro_index)
        unit_local = select_micro(inputs_local, micro_index).astype(jnp.float32) * scale_now
        unit_full = select_micro(inputs_wide, micro_index) * scale_now
        stat_part = jnp.sum(partial_value * gain_full * unit_full, axis=-1, keepdims=True)
        blocks = partial_value.reshape(row_count, tp_count, local_width)
        stat_blocks = jnp.broadcast_to(stat_part[:, :, None], (row_count, tp_count, 1))
        joined = jnp.concatenate([blocks, stat_blocks], axis=2).reshape(
            row_count, tp_count * (local_width + 1)
        )
        combined = sum_by_axis(joined, TP, 1)
        d_normed = combined[:, :local_width]
        norm_stat = combined[:, local_width:] / full_width
        scaled = d_normed * gain_local
        d_inputs = (
            cotangent.astype(jnp.float32) + scale_now * (scaled - unit_local * norm_stat)
        ).astype(jnp.bfloat16)
        grads_out = store_micro(grads_out, micro_index, d_inputs, is_valid)
        valid_float = is_valid.astype(jnp.float32)
        gain_total = gain_total + valid_float * jnp.sum(d_normed * unit_local, axis=0)
        stored = (
            store_micro(stored[0], micro_index, d_gate, is_valid),
            store_micro(stored[1], micro_index, d_up, is_valid),
            store_micro(stored[2], micro_index, full_cotangent, is_valid),
        )
        handed = passed_along(d_inputs, "section", -1)
        return (handed, grads_out, gain_total, stored)

    stored_init = (
        jnp.zeros((micro_count, row_count, hidden_width), jnp.bfloat16),
        jnp.zeros((micro_count, row_count, hidden_width), jnp.bfloat16),
        jnp.zeros((micro_count, row_count, full_width), jnp.bfloat16),
    )
    initial = (
        jnp.zeros((row_count, local_width), jnp.bfloat16),
        jnp.zeros((micro_count, row_count, local_width), jnp.bfloat16),
        jnp.zeros((local_width,), jnp.float32),
        stored_init,
    )
    handed_last, grads_out, gain_total, stored = lax.fori_loop(
        0, micro_count + section_count - 1, one_tick, initial
    )
    flat_rows = micro_count * row_count
    normed_flat = normed.reshape(flat_rows, full_width)
    hidden_flat = hidden.reshape(flat_rows, hidden_width)
    gate_flat = stored[0].reshape(flat_rows, hidden_width)
    up_flat = stored[1].reshape(flat_rows, hidden_width)
    cotangent_flat = stored[2].reshape(flat_rows, full_width)

    def grad_rows():
        normed_cols = lax.slice_in_dim(
            normed_flat, 0, full_width // lax.axis_size("fsdp") * lax.axis_size("fsdp"), axis=1
        )
        cotangent_cols = lax.slice_in_dim(
            cotangent_flat, 0, full_width // lax.axis_size("fsdp") * lax.axis_size("fsdp"), axis=1
        )
        return jnp.concatenate(
            [
                contract_rows(normed_cols, gate_flat),
                contract_rows(normed_cols, up_flat),
                contract_rows(cotangent_cols, hidden_flat),
            ],
            axis=1,
        )

    stacked = lax.psum_scatter(grad_rows(), "fsdp", scatter_dimension=0, tiled=True)
    gate_share = stacked[:, :hidden_width]
    up_share = stacked[:, hidden_width : 2 * hidden_width]
    down_share = stacked[:, 2 * hidden_width :]
    gain_share = lax.psum(gain_total, "fsdp")
    return (grads_out[None], gate_share[None], up_share[None], down_share.T[None], gain_share[None])


def solution(mesh):
    split = Mesh(
        mesh.devices.reshape(mesh.shape["section"], mesh.shape["fsdp"], 8, 2),
        ("section", "fsdp", "tp_0", "tp_1"),
    )
    return jax.shard_map(
        body,
        mesh=split,
        in_specs=(
            P("section", None, "fsdp", TP),
            P(None, "fsdp", TP),
            P("section", None),
            P("section", "fsdp", TP),
            P("section", "fsdp", TP),
            P("section", TP, "fsdp"),
        ),
        out_specs=(
            P("section", None, "fsdp", TP),
            P("section", "fsdp", TP),
            P("section", "fsdp", TP),
            P("section", TP, "fsdp"),
            P("section", TP),
        ),
        check_vma=False,
    )
```

profile of v0, /device:TPU:2, one launch (start us, length us, event | category | flops | bytes accessed | tf_op | source)
XLA Modules:
  0.0 1865.0 jit_solution(10509474963267189827)
XLA Ops:
  8.5 10.2 all-gather
  22.9 63.3 %all-gather.14.cloned.1.call-done = bf16[1,8,64,2560]{2,1,0,3:T(8,128)(2,1)} async-done(((bf16[1,8,64,320]{2,1,0,3:T(8,128)(2,1)}), bf16[1,8,64,2560]{2,1,0,3:T(8,128)(2,1)}) %all-gather.14.cloned.1.call-update) | async-done | bytes 2621456 | tf_op jit(solution)/shard_map/all_gather | solution.py:31
  86.3 5.6 copy.63
  95.5 87.5 %all-gather.16.cloned.1.call-done = bf16[3317760]{0:T(1024)(128)(2,1)} async-done(((bf16[414720]{0:T(1024)(128)(2,1)}), bf16[3317760]{0:T(1024)(128)(2,1)}) %all-gather.16.cloned.1.call-update) | async-done | bytes 6635536 | tf_op jit(solution)/shard_map/all_gather | solution.py:21
  183.0 8.4 reshape.74
  191.4 4.5 fusion.25
  198.3 6.7 reshape_reshape.7
  205.1 4.1 reshape.105
  209.1 7.5 reshape_reshape.6
  216.6 4.0 reshape.103
  220.6 5.6 reshape.69
  226.2 3.9 copy.65
  230.0 5.2 reshape.70
  235.2 5.2 fusion.18
  247.9 1404.9 %while.26 = (s32[]{:T(128)}, bf16[64,160]{1,0:T(8,128)(2,1)S(1)}, bf16[8,64,160]{2,1,0:T(8,128)(2,1)}, f32[160]{0:T(256)S(1)}, bf16[8,64,432]{2,1,0:T(8,128)(2,1...) while((s32[]{:T(128)}, bf16[64,160]{1,0:T(8,128)(2,1)S(1)}, ...), condition=%wide.region_6.7_spmd.clone, body=%wide.region_1.6_spmd.clone.sunk | while | flops 426474944 | bytes 50044748 | solution.py:161
  248.7 4.6 all-gather.9
  253.5 26.5 %all-gather.10 = bf16[8,320,64]{1,2,0:T(8,128)(2,1)S(1)} all-gather(bf16[1,320,64]{1,2,0:T(8,128)(2,1)S(1)} %reshape.113), channel_id=1, replica_groups=mesh['section'=2,'fsdp'=8,'tp_0'=8,'tp_1'=2] {'tp_0'}, dimensions={0}, use_global_device_ids=true | all-gather | bytes 368640 | tf_op jit(solution)/shard_map/while/body/eval_jaxpr/all_gather | solution.py:31
  281.4 3.4 bitcast_dynamic-update-slice_fusion.7
  294.5 68.0 %all-reduce.9.cloned.1.call-done = f32[64,2576]{1,0:T(8,128)} async-done(((f32[64,2576]{1,0:T(8,128)}), f32[64,2576]{1,0:T(8,128)}) %all-reduce.9.cloned.1.call-update) | async-done | bytes 659472 | tf_op jit(solution)/shard_map/while
  364.9 31.0 %all-reduce.11.cloned.1.call-done = f32[64,322]{1,0:T(8,128)} async-done(((f32[64,322]{1,0:T(8,128)}), f32[64,322]{1,0:T(8,128)}) %all-reduce.11.cloned.1.call-update) | async-done | bytes 82448 | tf_op jit(solution)/shard_map/while
  402.4 4.6 all-gather.9
  407.2 26.5 %all-gather.10 = bf16[8,320,64]{1,2,0:T(8,128)(2,1)S(1)} all-gather(bf16[1,320,64]{1,2,0:T(8,128)(2,1)S(1)} %reshape.113), channel_id=1, replica_groups=mesh['section'=2,'fsdp'=8,'tp_0'=8,'tp_1'=2] {'tp_0'}, dimensions={0}, use_global_device_ids=true | all-gather | bytes 368640 | tf_op jit(solution)/shard_map/while/body/eval_jaxpr/all_gather | solution.py:31
  435.1 3.4 bitcast_dynamic-update-slice_fusion.7
  448.2 70.7 %all-reduce.9.cloned.1.call-done = f32[64,2576]{1,0:T(8,128)} async-done(((f32[64,2576]{1,0:T(8,128)}), f32[64,2576]{1,0:T(8,128)}) %all-reduce.9.cloned.1.call-update) | async-done | bytes 659472 | tf_op jit(solution)/shard_map/while
  521.3 31.0 %all-reduce.11.cloned.1.call-done = f32[64,322]{1,0:T(8,128)} async-done(((f32[64,322]{1,0:T(8,128)}), f32[64,322]{1,0:T(8,128)}) %all-reduce.11.cloned.1.call-update) | async-done | bytes 82448 | tf_op jit(solution)/shard_map/while
  558.8 4.6 all-gather.9
  563.5 26.5 %all-gather.10 = bf16[8,320,64]{1,2,0:T(8,128)(2,1)S(1)} all-gather(bf16[1,320,64]{1,2,0:T(8,128)(2,1)S(1)} %reshape.113), channel_id=1, replica_groups=mesh['section'=2,'fsdp'=8,'tp_0'=8,'tp_1'=2] {'tp_0'}, dimensions={0}, use_global_device_ids=true | all-gather | bytes 368640 | tf_op jit(solution)/shard_map/while/body/eval_jaxpr/all_gather | solution.py:31
  591.5 3.4 bitcast_dynamic-update-slice_fusion.7
  604.5 70.7 %all-reduce.9.cloned.1.call-done = f32[64,2576]{1,0:T(8,128)} async-done(((f32[64,2576]{1,0:T(8,128)}), f32[64,2576]{1,0:T(8,128)}) %all-reduce.9.cloned.1.call-update) | async-done | bytes 659472 | tf_op jit(solution)/shard_map/while
  677.7 31.2 %all-reduce.11.cloned.1.call-done = f32[64,322]{1,0:T(8,128)} async-done(((f32[64,322]{1,0:T(8,128)}), f32[64,322]{1,0:T(8,128)}) %all-reduce.11.cloned.1.call-update) | async-done | bytes 82448 | tf_op jit(solution)/shard_map/while
  715.3 4.6 all-gather.9
  720.1 26.5 %all-gather.10 = bf16[8,320,64]{1,2,0:T(8,128)(2,1)S(1)} all-gather(bf16[1,320,64]{1,2,0:T(8,128)(2,1)S(1)} %reshape.113), channel_id=1, replica_groups=mesh['section'=2,'fsdp'=8,'tp_0'=8,'tp_1'=2] {'tp_0'}, dimensions={0}, use_global_device_ids=true | all-gather | bytes 368640 | tf_op jit(solution)/shard_map/while/body/eval_jaxpr/all_gather | solution.py:31
  761.1 70.7 %all-reduce.9.cloned.1.call-done = f32[64,2576]{1,0:T(8,128)} async-done(((f32[64,2576]{1,0:T(8,128)}), f32[64,2576]{1,0:T(8,128)}) %all-reduce.9.cloned.1.call-update) | async-done | bytes 659472 | tf_op jit(solution)/shard_map/while
  834.2 31.0 %all-reduce.11.cloned.1.call-done = f32[64,322]{1,0:T(8,128)} async-done(((f32[64,322]{1,0:T(8,128)}), f32[64,322]{1,0:T(8,128)}) %all-reduce.11.cloned.1.call-update) | async-done | bytes 82448 | tf_op jit(solution)/shard_map/while
  871.7 4.6 all-gather.9
  876.4 26.5 %all-gather.10 = bf16[8,320,64]{1,2,0:T(8,128)(2,1)S(1)} all-gather(bf16[1,320,64]{1,2,0:T(8,128)(2,1)S(1)} %reshape.113), channel_id=1, replica_groups=mesh['section'=2,'fsdp'=8,'tp_0'=8,'tp_1'=2] {'tp_0'}, dimensions={0}, use_global_device_ids=true | all-gather | bytes 368640 | tf_op jit(solution)/shard_map/while/body/eval_jaxpr/all_gather | solution.py:31
  904.4 3.4 bitcast_dynamic-update-slice_fusion.7
  917.4 70.7 %all-reduce.9.cloned.1.call-done = f32[64,2576]{1,0:T(8,128)} async-done(((f32[64,2576]{1,0:T(8,128)}), f32[64,2576]{1,0:T(8,128)}) %all-reduce.9.cloned.1.call-update) | async-done | bytes 659472 | tf_op jit(solution)/shard_map/while
  990.6 31.0 %all-reduce.11.cloned.1.call-done = f32[64,322]{1,0:T(8,128)} async-done(((f32[64,322]{1,0:T(8,128)}), f32[64,322]{1,0:T(8,128)}) %all-reduce.11.cloned.1.call-update) | async-done | bytes 82448 | tf_op jit(solution)/shard_map/while
  1028.1 4.6 all-gather.9
  1032.8 26.5 %all-gather.10 = bf16[8,320,64]{1,2,0:T(8,128)(2,1)S(1)} all-gather(bf16[1,320,64]{1,2,0:T(8,128)(2,1)S(1)} %reshape.113), channel_id=1, replica_groups=mesh['section'=2,'fsdp'=8,'tp_0'=8,'tp_1'=2] {'tp_0'}, dimensions={0}, use_global_device_ids=true | all-gather | bytes 368640 | tf_op jit(solution)/shard_map/while/body/eval_jaxpr/all_gather | solution.py:31
  1060.8 3.4 bitcast_dynamic-update-slice_fusion.7
  1073.8 70.7 %all-reduce.9.cloned.1.call-done = f32[64,2576]{1,0:T(8,128)} async-done(((f32[64,2576]{1,0:T(8,128)}), f32[64,2576]{1,0:T(8,128)}) %all-reduce.9.cloned.1.call-update) | async-done | bytes 659472 | tf_op jit(solution)/shard_map/while
  1147.0 31.0 %all-reduce.11.cloned.1.call-done = f32[64,322]{1,0:T(8,128)} async-done(((f32[64,322]{1,0:T(8,128)}), f32[64,322]{1,0:T(8,128)}) %all-reduce.11.cloned.1.call-update) | async-done | bytes 82448 | tf_op jit(solution)/shard_map/while
  1184.5 4.6 all-gather.9
  1189.2 26.5 %all-gather.10 = bf16[8,320,64]{1,2,0:T(8,128)(2,1)S(1)} all-gather(bf16[1,320,64]{1,2,0:T(8,128)(2,1)S(1)} %reshape.113), channel_id=1, replica_groups=mesh['section'=2,'fsdp'=8,'tp_0'=8,'tp_1'=2] {'tp_0'}, dimensions={0}, use_global_device_ids=true | all-gather | bytes 368640 | tf_op jit(solution)/shard_map/while/body/eval_jaxpr/all_gather | solution.py:31
  1217.2 3.4 bitcast_dynamic-update-slice_fusion.7
  1230.3 70.7 %all-reduce.9.cloned.1.call-done = f32[64,2576]{1,0:T(8,128)} async-done(((f32[64,2576]{1,0:T(8,128)}), f32[64,2576]{1,0:T(8,128)}) %all-reduce.9.cloned.1.call-update) | async-done | bytes 659472 | tf_op jit(solution)/shard_map/while
  1303.4 31.0 %all-reduce.11.cloned.1.call-done = f32[64,322]{1,0:T(8,128)} async-done(((f32[64,322]{1,0:T(8,128)}), f32[64,322]{1,0:T(8,128)}) %all-reduce.11.cloned.1.call-update) | async-done | bytes 82448 | tf_op jit(solution)/shard_map/while
  1340.8 4.6 all-gather.9
  1345.6 26.5 %all-gather.10 = bf16[8,320,64]{1,2,0:T(8,128)(2,1)S(1)} all-gather(bf16[1,320,64]{1,2,0:T(8,128)(2,1)S(1)} %reshape.113), channel_id=1, replica_groups=mesh['section'=2,'fsdp'=8,'tp_0'=8,'tp_1'=2] {'tp_0'}, dimensions={0}, use_global_device_ids=true | all-gather | bytes 368640 | tf_op jit(solution)/shard_map/while/body/eval_jaxpr/all_gather | solution.py:31
  1373.5 3.4 bitcast_dynamic-update-slice_fusion.7
  1386.6 70.7 %all-reduce.9.cloned.1.call-done = f32[64,2576]{1,0:T(8,128)} async-done(((f32[64,2576]{1,0:T(8,128)}), f32[64,2576]{1,0:T(8,128)}) %all-reduce.9.cloned.1.call-update) | async-done | bytes 659472 | tf_op jit(solution)/shard_map/while
  1459.7 31.0 %all-reduce.11.cloned.1.call-done = f32[64,322]{1,0:T(8,128)} async-done(((f32[64,322]{1,0:T(8,128)}), f32[64,322]{1,0:T(8,128)}) %all-reduce.11.cloned.1.call-update) | async-done | bytes 82448 | tf_op jit(solution)/shard_map/while
  1497.2 4.6 all-gather.9
  1501.9 26.5 %all-gather.10 = bf16[8,320,64]{1,2,0:T(8,128)(2,1)S(1)} all-gather(bf16[1,320,64]{1,2,0:T(8,128)(2,1)S(1)} %reshape.113), channel_id=1, replica_groups=mesh['section'=2,'fsdp'=8,'tp_0'=8,'tp_1'=2] {'tp_0'}, dimensions={0}, use_global_device_ids=true | all-gather | bytes 368640 | tf_op jit(solution)/shard_map/while/body/eval_jaxpr/all_gather | solution.py:31
  1529.9 3.4 bitcast_dynamic-update-slice_fusion.7
  1543.0 70.7 %all-reduce.9.cloned.1.call-done = f32[64,2576]{1,0:T(8,128)} async-done(((f32[64,2576]{1,0:T(8,128)}), f32[64,2576]{1,0:T(8,128)}) %all-reduce.9.cloned.1.call-update) | async-done | bytes 659472 | tf_op jit(solution)/shard_map/while
  1616.1 31.0 %all-reduce.11.cloned.1.call-done = f32[64,322]{1,0:T(8,128)} async-done(((f32[64,322]{1,0:T(8,128)}), f32[64,322]{1,0:T(8,128)}) %all-reduce.11.cloned.1.call-update) | async-done | bytes 82448 | tf_op jit(solution)/shard_map/while
  1652.8 3.5 convolution_bitcast_fusion.1
  1660.1 5.3 pad_maximum_fusion.1
  1665.4 14.5 copy.75
  1679.9 24.2 %psum.7 = f32[1,160]{1,0:T(1,128)} all-reduce(f32[1,160]{1,0:T(1,128)S(1)} %bitcast.180), channel_id=1, replica_groups=mesh['section'=2,'fsdp'=8,'tp_0'=8,'tp_1'=2] {'fsdp'}, use_global_device_ids=true, to_apply=%region_8.9 | all-reduce | flops 160 | bytes 1280 | tf_op jit(solution)/shard_map/psum | solution.py:191
  1704.1 148.0 %reduce-scatter.6.cloned.1.call-done = f32[320,1296]{1,0:T(8,128)} async-done(((f32[2560,1296]{1,0:T(8,128)}), f32[320,1296]{1,0:T(8,128)}) %reduce-scatter.6.cloned.1.call-update) | async-done | bytes 1658896
  (383 shorter events, 201.9 us)
Async XLA Ops:
  7.2 13.3 copy-start.12
  7.2 14.0 copy-start.11
  7.2 79.1 %all-gather.14.cloned.1.call-start = ((), (), s32[]{:S(2)}) async-start(), calls=%async_computation.1 | async-start | bytes 5898240 | tf_op jit(solution)/shard_map/all_gather | solution.py:31
  18.7 4.1 copy-start.10
  18.7 164.2 %all-gather.16.cloned.1.call-start = ((), (), s32[]{:S(2)}) async-start(), calls=%async_computation.2 | async-start | bytes 7464960 | tf_op jit(solution)/shard_map/all_gather | solution.py:21
  91.9 3.6 copy-start.3
  235.2 5.2 copy-start.4
  243.7 4.1 copy-start.13
  243.7 4.1 copy-start.14
  247.9 36.9 %copy-start = (bf16[2560,432]{1,0:T(8,128)(2,1)}, bf16[2560,432]{1,0:T(8,128)(2,1)S(1)}, u32[]{:S(2)}) copy-start(bf16[2560,432]{1,0:T(8,128)(2,1)S(1)} %get-tuple-element.941) | copy-start | bytes 6635524 | tf_op jit(solution)/shard_map/while
  247.9 114.6 %all-reduce.9.cloned.1.call-start = ((), (), s32[]{:S(2)}) async-start(), calls=%async_computation.4 | async-start | bytes 1376256 | tf_op jit(solution)/shard_map/while
  281.4 4.3 copy-start.2
  290.2 111.4 %copy-start.1 = (bf16[2560,432]{1,0:T(8,128)(2,1)S(1)}, bf16[2560,432]{1,0:T(8,128)(2,1)}, u32[]{:S(2)}) copy-start(bf16[2560,432]{1,0:T(8,128)(2,1)} %copy-done) | copy-start | bytes 6635524 | tf_op jit(solution)/shard_map/while
  290.2 105.7 %all-reduce.11.cloned.1.call-start = ((), (), s32[]{:S(2)}) async-start(), calls=%async_computation.5 | async-start | bytes 196608 | tf_op jit(solution)/shard_map/while
  398.5 3.1 collective-permute-start
  401.6 36.9 %copy-start = (bf16[2560,432]{1,0:T(8,128)(2,1)}, bf16[2560,432]{1,0:T(8,128)(2,1)S(1)}, u32[]{:S(2)}) copy-start(bf16[2560,432]{1,0:T(8,128)(2,1)S(1)} %get-tuple-element.941) | copy-start | bytes 6635524 | tf_op jit(solution)/shard_map/while
  401.6 117.3 %all-reduce.9.cloned.1.call-start = ((), (), s32[]{:S(2)}) async-start(), calls=%async_computation.4 | async-start | bytes 1376256 | tf_op jit(solution)/shard_map/while
  435.1 4.3 copy-start.2
  443.9 114.0 %copy-start.1 = (bf16[2560,432]{1,0:T(8,128)(2,1)S(1)}, bf16[2560,432]{1,0:T(8,128)(2,1)}, u32[]{:S(2)}) copy-start(bf16[2560,432]{1,0:T(8,128)(2,1)} %copy-done) | copy-start | bytes 6635524 | tf_op jit(solution)/shard_map/while
  443.9 108.4 %all-reduce.11.cloned.1.call-start = ((), (), s32[]{:S(2)}) async-start(), calls=%async_computation.5 | async-start | bytes 196608 | tf_op jit(solution)/shard_map/while
  554.8 3.1 collective-permute-start
  557.9 36.9 %copy-start = (bf16[2560,432]{1,0:T(8,128)(2,1)}, bf16[2560,432]{1,0:T(8,128)(2,1)S(1)}, u32[]{:S(2)}) copy-start(bf16[2560,432]{1,0:T(8,128)(2,1)S(1)} %get-tuple-element.941) | copy-start | bytes 6635524 | tf_op jit(solution)/shard_map/while
  557.9 117.3 %all-reduce.9.cloned.1.call-start = ((), (), s32[]{:S(2)}) async-start(), calls=%async_computation.4 | async-start | bytes 1376256 | tf_op jit(solution)/shard_map/while
  591.5 4.3 copy-start.2
  600.2 114.2 %copy-start.1 = (bf16[2560,432]{1,0:T(8,128)(2,1)S(1)}, bf16[2560,432]{1,0:T(8,128)(2,1)}, u32[]{:S(2)}) copy-start(bf16[2560,432]{1,0:T(8,128)(2,1)} %copy-done) | copy-start | bytes 6635524 | tf_op jit(solution)/shard_map/while
  600.3 108.6 %all-reduce.11.cloned.1.call-start = ((), (), s32[]{:S(2)}) async-start(), calls=%async_computation.5 | async-start | bytes 196608 | tf_op jit(solution)/shard_map/while
  711.4 3.1 collective-permute-start
  714.5 36.9 %copy-start = (bf16[2560,432]{1,0:T(8,128)(2,1)}, bf16[2560,432]{1,0:T(8,128)(2,1)S(1)}, u32[]{:S(2)}) copy-start(bf16[2560,432]{1,0:T(8,128)(2,1)S(1)} %get-tuple-element.941) | copy-start | bytes 6635524 | tf_op jit(solution)/shard_map/while
  714.5 117.3 %all-reduce.9.cloned.1.call-start = ((), (), s32[]{:S(2)}) async-start(), calls=%async_computation.4 | async-start | bytes 1376256 | tf_op jit(solution)/shard_map/while
  748.0 4.3 copy-start.2
  756.8 114.0 %copy-start.1 = (bf16[2560,432]{1,0:T(8,128)(2,1)S(1)}, bf16[2560,432]{1,0:T(8,128)(2,1)}, u32[]{:S(2)}) copy-start(bf16[2560,432]{1,0:T(8,128)(2,1)} %copy-done) | copy-start | bytes 6635524 | tf_op jit(solution)/shard_map/while
  756.8 108.4 %all-reduce.11.cloned.1.call-start = ((), (), s32[]{:S(2)}) async-start(), calls=%async_computation.5 | async-start | bytes 196608 | tf_op jit(solution)/shard_map/while
  867.7 3.1 collective-permute-start
  870.8 36.9 %copy-start = (bf16[2560,432]{1,0:T(8,128)(2,1)}, bf16[2560,432]{1,0:T(8,128)(2,1)S(1)}, u32[]{:S(2)}) copy-start(bf16[2560,432]{1,0:T(8,128)(2,1)S(1)} %get-tuple-element.941) | copy-start | bytes 6635524 | tf_op jit(solution)/shard_map/while
  870.8 117.3 %all-reduce.9.cloned.1.call-start = ((), (), s32[]{:S(2)}) async-start(), calls=%async_computation.4 | async-start | bytes 1376256 | tf_op jit(solution)/shard_map/while
  904.4 4.3 copy-start.2
  913.1 114.1 %copy-start.1 = (bf16[2560,432]{1,0:T(8,128)(2,1)S(1)}, bf16[2560,432]{1,0:T(8,128)(2,1)}, u32[]{:S(2)}) copy-start(bf16[2560,432]{1,0:T(8,128)(2,1)} %copy-done) | copy-start | bytes 6635524 | tf_op jit(solution)/shard_map/while
  913.2 108.4 %all-reduce.11.cloned.1.call-start = ((), (), s32[]{:S(2)}) async-start(), calls=%async_computation.5 | async-start | bytes 196608 | tf_op jit(solution)/shard_map/while
  1024.1 3.1 collective-permute-start
  1027.2 36.9 %copy-start = (bf16[2560,432]{1,0:T(8,128)(2,1)}, bf16[2560,432]{1,0:T(8,128)(2,1)S(1)}, u32[]{:S(2)}) copy-start(bf16[2560,432]{1,0:T(8,128)(2,1)S(1)} %get-tuple-element.941) | copy-start | bytes 6635524 | tf_op jit(solution)/shard_map/while
  1027.2 117.3 %all-reduce.9.cloned.1.call-start = ((), (), s32[]{:S(2)}) async-start(), calls=%async_computation.4 | async-start | bytes 1376256 | tf_op jit(solution)/shard_map/while
  1060.8 4.3 copy-start.2
  1069.6 114.1 %copy-start.1 = (bf16[2560,432]{1,0:T(8,128)(2,1)S(1)}, bf16[2560,432]{1,0:T(8,128)(2,1)}, u32[]{:S(2)}) copy-start(bf16[2560,432]{1,0:T(8,128)(2,1)} %copy-done) | copy-start | bytes 6635524 | tf_op jit(solution)/shard_map/while
  1069.6 108.4 %all-reduce.11.cloned.1.call-start = ((), (), s32[]{:S(2)}) async-start(), calls=%async_computation.5 | async-start | bytes 196608 | tf_op jit(solution)/shard_map/while
  1180.6 3.1 collective-permute-start
  1183.6 36.9 %copy-start = (bf16[2560,432]{1,0:T(8,128)(2,1)}, bf16[2560,432]{1,0:T(8,128)(2,1)S(1)}, u32[]{:S(2)}) copy-start(bf16[2560,432]{1,0:T(8,128)(2,1)S(1)} %get-tuple-element.941) | copy-start | bytes 6635524 | tf_op jit(solution)/shard_map/while
  1183.7 117.3 %all-reduce.9.cloned.1.call-start = ((), (), s32[]{:S(2)}) async-start(), calls=%async_computation.4 | async-start | bytes 1376256 | tf_op jit(solution)/shard_map/while
  1217.2 4.3 copy-start.2
  1226.0 114.0 %copy-start.1 = (bf16[2560,432]{1,0:T(8,128)(2,1)S(1)}, bf16[2560,432]{1,0:T(8,128)(2,1)}, u32[]{:S(2)}) copy-start(bf16[2560,432]{1,0:T(8,128)(2,1)} %copy-done) | copy-start | bytes 6635524 | tf_op jit(solution)/shard_map/while
  1226.0 108.4 %all-reduce.11.cloned.1.call-start = ((), (), s32[]{:S(2)}) async-start(), calls=%async_computation.5 | async-start | bytes 196608 | tf_op jit(solution)/shard_map/while
  1336.9 3.1 collective-permute-start
  1340.0 36.9 %copy-start = (bf16[2560,432]{1,0:T(8,128)(2,1)}, bf16[2560,432]{1,0:T(8,128)(2,1)S(1)}, u32[]{:S(2)}) copy-start(bf16[2560,432]{1,0:T(8,128)(2,1)S(1)} %get-tuple-element.941) | copy-start | bytes 6635524 | tf_op jit(solution)/shard_map/while
  1340.0 117.3 %all-reduce.9.cloned.1.call-start = ((), (), s32[]{:S(2)}) async-start(), calls=%async_computation.4 | async-start | bytes 1376256 | tf_op jit(solution)/shard_map/while
  1373.5 4.3 copy-start.2
  1382.3 114.0 %copy-start.1 = (bf16[2560,432]{1,0:T(8,128)(2,1)S(1)}, bf16[2560,432]{1,0:T(8,128)(2,1)}, u32[]{:S(2)}) copy-start(bf16[2560,432]{1,0:T(8,128)(2,1)} %copy-done) | copy-start | bytes 6635524 | tf_op jit(solution)/shard_map/while
  1382.3 108.4 %all-reduce.11.cloned.1.call-start = ((), (), s32[]{:S(2)}) async-start(), calls=%async_computation.5 | async-start | bytes 196608 | tf_op jit(solution)/shard_map/while
  1493.3 3.1 collective-permute-start
  1496.4 36.9 %copy-start = (bf16[2560,432]{1,0:T(8,128)(2,1)}, bf16[2560,432]{1,0:T(8,128)(2,1)S(1)}, u32[]{:S(2)}) copy-start(bf16[2560,432]{1,0:T(8,128)(2,1)S(1)} %get-tuple-element.941) | copy-start | bytes 6635524 | tf_op jit(solution)/shard_map/while
  1496.4 117.3 %all-reduce.9.cloned.1.call-start = ((), (), s32[]{:S(2)}) async-start(), calls=%async_computation.4 | async-start | bytes 1376256 | tf_op jit(solution)/shard_map/while
  1529.9 4.3 copy-start.2
  1538.7 114.1 %copy-start.1 = (bf16[2560,432]{1,0:T(8,128)(2,1)S(1)}, bf16[2560,432]{1,0:T(8,128)(2,1)}, u32[]{:S(2)}) copy-start(bf16[2560,432]{1,0:T(8,128)(2,1)} %copy-done) | copy-start | bytes 6635524 | tf_op jit(solution)/shard_map/while
  1538.7 108.4 %all-reduce.11.cloned.1.call-start = ((), (), s32[]{:S(2)}) async-start(), calls=%async_computation.5 | async-start | bytes 196608 | tf_op jit(solution)/shard_map/while
  1649.7 3.1 collective-permute-start
  1652.8 199.3 %reduce-scatter.6.cloned.1.call-start = ((), (), s32[]{:S(2)}) async-start(), calls=%async_computation.3 | async-start | bytes 16220160
  (5 other events, 13.1 us)
Sparse Core Ops, SparseCore 0:
  18.8 67.4 all-gather.13
  88.9 94.0 all-gather.15
  290.3 72.1 all-reduce.8
  365.5 30.4 all-reduce.10
  444.0 74.7 all-reduce.8
  521.8 30.4 all-reduce.10
  600.4 74.8 all-reduce.8
  678.4 30.4 all-reduce.10
  756.9 74.7 all-reduce.8
  834.7 30.4 all-reduce.10
  913.3 74.8 all-reduce.8
  991.1 30.4 all-reduce.10
  1069.7 74.8 all-reduce.8
  1147.5 30.4 all-reduce.10
  1226.1 74.7 all-reduce.8
  1303.9 30.4 all-reduce.10
  1382.5 74.7 all-reduce.8
  1460.3 30.4 all-reduce.10
  1538.8 74.8 all-reduce.8
  1616.7 30.4 all-reduce.10
  1680.0 172.0 reduce-scatter.5
where the time goes:
time: 1870 us; the launch traced here: 1860 us
  waiting for transfers between devices  1220 us (65%)
  blocking collectives  314 us (17%)
  local copies, waits for them, and re-layouts  162 us (9%)
  matrix products  72.4 us (4%)
  other arithmetic  58.2 us (3%)
    while x36, waiting for transfers between devices  913 us
    all_gather x19, blocking collectives, gathered_by_axis(): x = lax.all_gather(x, axis, axis=dim, tiled=True)  290 us
    unnamed x4, waiting for transfers between devices  148 us
    all_gather x1, waiting for transfers between devices, one_gather(): lines, at, finished = (lax.all_gather(vector, axis), 0, [])  87.5 us
    all_gather x1, waiting for transfers between devices, gathered_by_axis(): x = lax.all_gather(x, axis, axis=dim, tiled=True)  63.3 us
    dot_general x27, matrix products, contract_cols(): lax.dot_general(left, right, (((1,), (1,)), ((), ())), preferred_element_...  57.4 us
  transfers between devices with their start and end apart: 30, of which 30 were waited for; matrix products, arithmetic and copies ran while one was open for 3% of the time, Pallas kernels for 0%

commit v1 on v0

v1 whole, which is shorter than its diff:
```python
import functools

import jax
import jax.numpy as jnp
from jax import lax
from jax.experimental import pallas as pl
from jax.experimental.pallas import tpu as pltpu
from jax.sharding import PartitionSpec as P

EPS = 1e-05
MESH = pl.DeviceIdType.MESH
F32 = jnp.float32
BF16 = jnp.bfloat16

NY, NXH, NZ, NXL = 4, 2, 8, 2
NF, NT = NY * NXH, NZ * NXL
MICRO = 8
ROWS = 64
T = MICRO * ROWS
W = 160
PW = NXL * W
FL = 432
GU = 2 * FL
D = W * NT


def dot(a, b, ca, cb, precision=None):
    return lax.dot_general(
        a, b, (((ca,), (cb,)), ((), ())), preferred_element_type=F32, precision=precision
    )


def fused_kernel(
    x_ref,
    tg_ref,
    gain_ref,
    wg_ref,
    wu_ref,
    wd_ref,
    dx_ref,
    gg_ref,
    ug_ref,
    dg_ref,
    gn_ref,
    wgu,
    wd,
    n_all,
    dy_all,
    gu,
    dh,
    dgu,
    hid,
    unit,
    scale,
    stat,
    ssq_in,
    stat_in,
    gain_in,
    pdn,
    rdn,
    xs,
    xr,
    pgu,
    rgu,
    pd,
    rd,
    ssem,
    rsem,
):
    s = lax.axis_index("section")
    f = lax.axis_index("fsdp")
    t = lax.axis_index("tp")
    y, xh = lax.div(f, NXH), lax.rem(f, NXH)
    z, xl = lax.div(t, NXL), lax.rem(t, NXL)

    def at_y(step, col=None):
        return (s, lax.rem(y + step + NY, NY) * NXH + xh, t)

    def at_z(step):
        return (s, f, lax.rem(z + step + NZ, NZ) * NXL + xl)

    yp, ym, zp, zm = at_y(1), at_y(-1), at_z(1), at_z(-1)
    xhp = (s, y * NXH + (1 - xh), t)
    xlp = (s, f, z * NXL + (1 - xl))
    core = (1 - s, f, t)
    tp_peers = [(s, f, lax.rem(t + k, NT)) for k in range(1, NT)]
    fs_peers = [(s, lax.rem(f + k, NF), t) for k in range(1, NF)]

    count = [0]
    started = []

    def message():
        count[0] += 1
        return count[0] - 1

    def copy(src, dst, m, dev):
        return pltpu.make_async_remote_copy(
            src_ref=src,
            dst_ref=dst,
            send_sem=ssem.at[m],
            recv_sem=rsem.at[m],
            device_id=dev,
            device_id_type=MESH,
        )

    def send(src, dst, m, dev):
        copy(src, dst, m, dev).start()

    def sent(buf, lead, m):
        started.append((buf, lead, m))

    def arrived(dst, m):
        copy(dst, dst, m, core).wait_recv()

    def rows(n, step, fn):
        def body(i, c):
            fn(pl.multiple_of(i * step, step))
            return c

        lax.fori_loop(0, n // step, body, 0)

    barrier = pltpu.get_barrier_semaphore()
    for dev in tp_peers + fs_peers + [core]:
        pl.semaphore_signal(barrier, inc=1, device_id=dev, device_id_type=MESH)

    eye = (
        lax.broadcasted_iota(jnp.int32, (W, W), 0) == lax.broadcasted_iota(jnp.int32, (W, W), 1)
    ).astype(BF16)

    def pack(r):
        wgu[f, pl.ds(r, 32), 0:FL] = wg_ref[pl.ds(r, 32), :]
        wgu[f, pl.ds(r, 32), FL:GU] = wu_ref[pl.ds(r, 32), :]

    rows(PW, 32, pack)

    def pack_down(r):
        wd[f, pl.ds(r, 48), :] = wd_ref[pl.ds(r, 48), :]

    rows(FL, 48, pack_down)
    xt = dot(eye, x_ref[...], 1, 1)
    ssq_in[t] = jnp.sum(xt * xt, axis=0, keepdims=True)
    unit[...] = xt

    @pl.when(s == 1)
    def _():
        dy_all[z, xl] = dot(eye, tg_ref[...], 1, 1).astype(BF16)

    pl.semaphore_wait(barrier, NT - 1 + NF - 1 + 1)

    def weights_own():
        for arr in (wgu, wd):
            for dev in (yp, ym, xhp):
                m = message()
                send(arr.at[f], arr.at[f], m, dev)
                sent(arr, 1, m)

    mark_w = count[0]
    weights_own()

    def left_block(col):
        return lax.rem(y + NY - 1, NY) * NXH + col

    def right_block(col):
        return lax.rem(y + 1, NY) * NXH + col

    far = lax.rem(y + 2, NY) * NXH

    m_ssq = count[0]
    for k, dev in enumerate(tp_peers):
        m = message()
        send(ssq_in.at[t], ssq_in.at[t], m, dev)
        sent(ssq_in, 1, m)

    def gather_steps(buf):
        ms = [message() for _ in range(9)]

        def start():
            send(buf.at[z, xl], buf.at[z, xl], ms[0], xlp)
            sent(buf, 2, ms[0])

        def step(k):
            fwd = lax.rem(z + NZ - (k - 1), NZ)
            bwd = lax.rem(z + (k - 1), NZ)
            if k == 1:
                arrived(buf.at[z, 1 - xl], ms[0])
            else:
                arrived(buf.at[fwd], ms[2 * k - 3])
                arrived(buf.at[bwd], ms[2 * k - 2])
            a = buf.at[fwd] if k < 4 else buf.at[fwd, 0]
            b = buf.at[bwd] if k < 4 else buf.at[bwd, 1]
            send(a, a, ms[2 * k - 1], zp)
            send(b, b, ms[2 * k], zm)
            like = (buf, 1) if k < 4 else (buf, 2)
            sent(*like, ms[2 * k - 1])
            sent(*like, ms[2 * k])

        def finish():
            opp = lax.rem(z + 4, NZ)
            arrived(buf.at[opp, 0], ms[7])
            arrived(buf.at[opp, 1], ms[8])

        return start, step, finish

    n_start, n_step, n_finish = gather_steps(n_all)
    d_start, d_step, d_finish = gather_steps(dy_all)
    m_core = message()

    @pl.when(s == 1)
    def _():
        d_start()

    for k in range(1, NT):
        arrived(ssq_in.at[lax.rem(t + NT - k, NT)], m_ssq + k - 1)
    total = ssq_in[0]
    for k in range(1, NT):
        total = total + ssq_in[k]
    row_scale = lax.rsqrt(total / D + EPS)
    scale[...] = row_scale
    u = unit[...] * row_scale
    unit[...] = u
    n_all[z, xl] = (u * gain_ref[:, 0:1]).astype(BF16)
    n_start()

    m_pass = count[0]
    for _ in range(8):
        message()

    def weights_partner():
        for j, arr in enumerate((wgu, wd)):
            blk = arr.at[y * NXH + (1 - xh)]
            arrived(blk, mark_w + 3 * j + 2)
            for q, dev in enumerate((yp, ym)):
                send(blk, blk, m_pass + 4 * j + q, dev)
                sent(arr, 1, m_pass + 4 * j + q)

    def weights_far():
        for j, arr in enumerate((wgu, wd)):
            arrived(arr.at[left_block(xh)], mark_w + 3 * j + 0)
            arrived(arr.at[right_block(xh)], mark_w + 3 * j + 1)
            arrived(arr.at[left_block(1 - xh)], m_pass + 4 * j + 0)
            arrived(arr.at[right_block(1 - xh)], m_pass + 4 * j + 1)
            a, b = arr.at[left_block(0)], arr.at[right_block(1)]
            send(a, a, m_pass + 4 * j + 2, yp)
            send(b, b, m_pass + 4 * j + 3, ym)
            sent(arr, 1, m_pass + 4 * j + 2)
            sent(arr, 1, m_pass + 4 * j + 3)

    def weights_last():
        for j, arr in enumerate((wgu, wd)):
            arrived(arr.at[far], m_pass + 4 * j + 2)
            arrived(arr.at[far + 1], m_pass + 4 * j + 3)

    @pl.when(s == 1)
    def _():
        d_step(1)
        n_step(1)
        d_step(2)
        n_step(2)
        weights_partner()
        d_step(3)
        n_step(3)
        d_step(4)
        n_step(4)
        weights_far()
        d_finish()
        n_finish()
        weights_last()

    mid = list(started)
    del started[:]

    @pl.when(s == 0)
    def _():
        n_step(1)
        n_step(2)
        weights_partner()
        n_step(3)
        n_step(4)
        weights_far()
        n_finish()
        weights_last()

    del started[:]

    gu[...] = jnp.zeros_like(gu)

    def fwd(i, c):
        gu[...] += dot(wgu[i], n_all[i].reshape(PW, T), 0, 0)
        return c

    lax.fori_loop(0, NF, fwd, 0)

    @pl.when(s == 0)
    def _():
        arrived(dy_all.at[z, xl], m_core)
        d_start()
        for k in range(1, 5):
            d_step(k)
        d_finish()

    del started[:]

    dh[...] = jnp.zeros_like(dh)

    def dhid(i, c):
        dh[...] += dot(wd[i], dy_all[i].reshape(PW, T), 1, 0)
        return c

    lax.fori_loop(0, NF, dhid, 0)

    stat[...] = jnp.zeros_like(stat)

    def elementwise(r):
        gate = gu[pl.ds(r, 16), :]
        up = gu[pl.ds(pl.multiple_of(FL + r, 16), 16), :]
        dd = dh[pl.ds(r, 16), :]
        sig = jax.nn.sigmoid(gate)
        silu = gate * sig
        hid[pl.ds(r, 16), :] = (silu * up).astype(BF16)
        d_gate = (dd * up * sig * (1.0 + gate * (1.0 - sig))).astype(BF16)
        d_up = (dd * silu).astype(BF16)
        dgu[pl.ds(r, 16), :] = d_gate
        dgu[pl.ds(pl.multiple_of(FL + r, 16), 16), :] = d_up
        both = d_gate.astype(F32) * gate + d_up.astype(F32) * up
        stat[...] += both[0:8] + both[8:16]

    rows(FL, 16, elementwise)

    stat_in[t] = jnp.sum(stat[...], axis=0, keepdims=True)
    m_stat = count[0]
    for k, dev in enumerate(tp_peers):
        m = message()
        send(stat_in.at[t], stat_in.at[t], m, dev)
        sent(stat_in, 1, m)

    def dnormed(i, c):
        blk = lax.rem(z + 4 + i, NZ)
        pdn[blk] = dot(wgu[blk], dgu[...], 1, 0).astype(BF16).reshape(NXL, W, T)
        return c

    def add(dst, at, src, at_src, n, step):
        def body(r):
            a = dst[(*at, pl.ds(r, step), slice(None))].astype(F32)
            b = src[(*at_src, pl.ds(r, step), slice(None))].astype(F32)
            dst[(*at, pl.ds(r, step), slice(None))] = (a + b).astype(BF16)

        rows(n, step, body)

    ms = [message() for _ in range(9)]
    lax.fori_loop(0, 1, dnormed, 0)
    opp = lax.rem(z + 4, NZ)
    send(pdn.at[opp, 0], rdn.at[0, 0, 0], ms[0], zp)
    send(pdn.at[opp, 1], rdn.at[1, 0, 1], ms[1], zm)
    sent(pdn, 2, ms[0])
    sent(pdn, 2, ms[1])
    lax.fori_loop(1, NZ, dnormed, 0)
    for k in range(2, 5):
        fwd_blk = lax.rem(z + 5 - k, NZ)
        bwd_blk = lax.rem(z + NZ - 5 + k, NZ)
        for way, blk, dev in ((0, fwd_blk, zp), (1, bwd_blk, zm)):
            m_in = ms[2 * (k - 2) + way]
            halves = (way,) if k == 2 else (0, 1)
            if k == 2:
                arrived(rdn.at[way, 0, way], m_in)
            else:
                arrived(rdn.at[way, k - 2], m_in)
            for hf in halves:
                add(pdn, (blk, hf), rdn, (way, k - 2, hf), W, 32)
            m = ms[2 * (k - 1) + way]
            send(pdn.at[blk], rdn.at[way, k - 1], m, dev)
            sent(pdn, 1, m)
    arrived(rdn.at[0, 3], ms[6])
    arrived(rdn.at[1, 3], ms[7])
    for q in (1 - xl,):
        xs[...] = (
            pdn[z, q].astype(F32) + rdn[0, 3, q].astype(F32) + rdn[1, 3, q].astype(F32)
        ).astype(BF16)
    send(xs, xr, ms[8], xlp)
    sent(xs, 0, ms[8])

    for k in range(1, NT):
        arrived(stat_in.at[lax.rem(t + NT - k, NT)], m_stat + k - 1)
    norm_stat = stat_in[0]
    for k in range(1, NT):
        norm_stat = norm_stat + stat_in[k]
    norm_stat = norm_stat / D
    arrived(xr, ms[8])
    d_normed = (
        pdn[z, xl].astype(F32)
        + rdn[0, 3, xl].astype(F32)
        + rdn[1, 3, xl].astype(F32)
        + xr[...].astype(F32)
    )
    u = unit[...]
    dx = (
        dy_all[z, xl].astype(F32) + scale[...] * (d_normed * gain_ref[:, 0:1] - u * norm_stat)
    ).astype(BF16)
    xs_out = dx

    @pl.when(s == 1)
    def _():
        xr[...] = xs_out
        send(xr, dy_all.at[z, xl], m_core, core)

    gain_part = dot(jnp.ones((8, T), F32), d_normed * u, 1, 1, lax.Precision.HIGHEST)
    gain_in[f] = gain_part
    m_gain = count[0]
    for k, dev in enumerate(fs_peers):
        m = message()
        send(gain_in.at[f], gain_in.at[f], m, dev)
        sent(gain_in, 1, m)
    dx_ref[...] = dot(xs_out, eye, 0, 0).astype(BF16)

    def wgrad(i, c):
        pgu[i] = dot(n_all[i].reshape(PW, T), dgu[...], 1, 1).astype(BF16)
        pd[i] = dot(hid[...], dy_all[i].reshape(PW, T), 1, 1).astype(BF16)
        return c

    lax.fori_loop(0, NF, wgrad, 0)

    m_g = count[0]
    for _ in range(14):
        message()
    groups = ((pgu, rgu, PW, 32, m_g), (pd, rd, FL, 48, m_g + 7))
    for p, r, n, st, m0 in groups:
        send(p.at[far], r.at[0], m0, yp)
        send(p.at[far + 1], r.at[1], m0 + 1, ym)
        sent(p, 1, m0)
        sent(p, 1, m0 + 1)
    for p, r, n, st, m0 in groups:
        right, left = right_block(0), left_block(0)
        send(p.at[right + 1], r.at[3], m0 + 3, yp)
        sent(p, 1, m0 + 3)
        send(p.at[left], r.at[4], m0 + 4, ym)
        sent(p, 1, m0 + 4)
        arrived(r.at[0], m0)
        add(p, (right,), r, (0,), n, st)
        send(p.at[right], r.at[2], m0 + 2, yp)
        sent(p, 1, m0 + 2)
        arrived(r.at[1], m0 + 1)
        add(p, (left + 1,), r, (1,), n, st)
        send(p.at[left + 1], r.at[5], m0 + 5, ym)
        sent(p, 1, m0 + 5)
    for p, r, n, st, m0 in groups:
        for q in range(2, 6):
            arrived(r.at[q], m0 + q)
        other = y * NXH + (1 - xh)

        def partner(rr, p=p, r=r, st=st, other=other):
            p[other, pl.ds(rr, st), :] = (
                p[other, pl.ds(rr, st), :].astype(F32)
                + r[2 + (1 - xh), pl.ds(rr, st), :].astype(F32)
                + r[4 + (1 - xh), pl.ds(rr, st), :].astype(F32)
            ).astype(BF16)

        rows(n, st, partner)
        send(p.at[other], r.at[6], m0 + 6, xhp)
        sent(p, 1, m0 + 6)
    for p, r, n, st, m0 in groups:
        arrived(r.at[6], m0 + 6)

        def final(rr, p=p, r=r, st=st):
            v = (
                p[f, pl.ds(rr, st), :].astype(F32)
                + r[2 + xh, pl.ds(rr, st), :].astype(F32)
                + r[4 + xh, pl.ds(rr, st), :].astype(F32)
                + r[6, pl.ds(rr, st), :].astype(F32)
            )
            if p is pgu:
                gg_ref[pl.ds(rr, st), :] = v[:, 0:FL]
                ug_ref[pl.ds(rr, st), :] = v[:, FL:GU]
            else:
                dg_ref[pl.ds(rr, st), :] = v

        rows(n, st, final)

    for k in range(1, NF):
        arrived(gain_in.at[lax.rem(f + NF - k, NF)], m_gain + k - 1)
    gsum = gain_in[0]
    for k in range(1, NF):
        gsum = gsum + gain_in[k]
    gn_ref[...] = gsum

    for buf, lead, m in mid + started:
        like = buf.at[(0,) * lead] if lead else buf
        copy(like, like, m, core).wait_send()

    @pl.when(s == 1)
    def _():
        copy(xr, xr, m_core, core).wait_send()

    assert count[0] <= ssem.shape[0], count[0]


NSEM = 120


def body(saved_inputs, top_grad, norm_gain, gate_weight, up_weight, down_weight):
    x = saved_inputs.reshape(T, W)
    tg = top_grad.reshape(T, W)
    gain = lax.dynamic_slice_in_dim(norm_gain[0], lax.axis_index("tp") * W, W)
    gain = jnp.broadcast_to(gain[:, None], (W, 128))
    vm = pl.BlockSpec(memory_space=pltpu.VMEM)
    out = pl.pallas_call(
        fused_kernel,
        name="fused",
        out_shape=(
            jax.ShapeDtypeStruct((T, W), BF16),
            jax.ShapeDtypeStruct((PW, FL), F32),
            jax.ShapeDtypeStruct((PW, FL), F32),
            jax.ShapeDtypeStruct((FL, PW), F32),
            jax.ShapeDtypeStruct((8, W), F32),
        ),
        in_specs=[vm] * 6,
        out_specs=[vm] * 5,
        scratch_shapes=[
            pltpu.VMEM((NF, PW, GU), BF16),
            pltpu.VMEM((NF, FL, PW), BF16),
            pltpu.VMEM((NZ, NXL, W, T), BF16),
            pltpu.VMEM((NZ, NXL, W, T), BF16),
            pltpu.VMEM((GU, T), F32),
            pltpu.VMEM((FL, T), F32),
            pltpu.VMEM((GU, T), BF16),
            pltpu.VMEM((FL, T), BF16),
            pltpu.VMEM((W, T), F32),
            pltpu.VMEM((1, T), F32),
            pltpu.VMEM((8, T), F32),
            pltpu.VMEM((NT, 1, T), F32),
            pltpu.VMEM((NT, 1, T), F32),
            pltpu.VMEM((NF, 8, W), F32),
            pltpu.VMEM((NZ, NXL, W, T), BF16),
            pltpu.VMEM((2, 4, NXL, W, T), BF16),
            pltpu.VMEM((W, T), BF16),
            pltpu.VMEM((W, T), BF16),
            pltpu.VMEM((NF, PW, GU), BF16),
            pltpu.VMEM((7, PW, GU), BF16),
            pltpu.VMEM((NF, FL, PW), BF16),
            pltpu.VMEM((7, FL, PW), BF16),
            pltpu.SemaphoreType.DMA((NSEM,)),
            pltpu.SemaphoreType.DMA((NSEM,)),
        ],
        compiler_params=pltpu.CompilerParams(
            collective_id=0, has_side_effects=True, vmem_limit_bytes=62 * 2**20
        ),
    )(x, tg, gain, gate_weight[0], up_weight[0], down_weight[0])
    dx, gg, ug, dg, gn = out
    return (
        dx.reshape(1, MICRO, ROWS, W),
        gg[None],
        ug[None],
        dg[None],
        gn[0:1],
    )


def solution(mesh):
    return jax.shard_map(
        body,
        mesh=mesh,
        in_specs=(
            P("section", None, "fsdp", "tp"),
            P(None, "fsdp", "tp"),
            P("section", None),
            P("section", "fsdp", "tp"),
            P("section", "fsdp", "tp"),
            P("section", "tp", "fsdp"),
        ),
        out_specs=(
            P("section", None, "fsdp", "tp"),
            P("section", "fsdp", "tp"),
            P("section", "fsdp", "tp"),
            P("section", "tp", "fsdp"),
            P("section", "tp"),
        ),
        check_vma=False,
    )
```

time: 1870 us -> 246 us (0.13)
  waiting for transfers between devices: 1220 us -> 0 us
  blocking collectives: 314 us -> 0 us
  Pallas kernels: 0 us -> 235 us
  local copies, waits for them, and re-layouts: 162 us -> 9.76 us
  matrix products: 72.4 us -> 0 us
  other arithmetic: 58.2 us -> 0 us
    while x36 -> x0, waiting for transfers between devices: 913 us -> none
    all_gather x19 -> x0, blocking collectives: 290 us -> none  [gathered_by_axis(): x = lax.all_gather(x, axis, axis=dim, tiled=True)]
    pallas_call x0 -> x1, Pallas kernels: none -> 235 us  [body(): pl.pallas_call(fused_kernel, name='fused', out_shape=(jax.ShapeDtypeStruc...]
    all_gather x2 -> x0, waiting for transfers between devices: 151 us -> none  [the longest x1 87.5 us: one_gather(): lines, at, finished = (lax.all_gather(vector, axis), 0, [])]
    unnamed x4 -> x0, waiting for transfers between devices: 148 us -> none
    dot_general x32 -> x0, matrix products: 72.4 us -> none  [the longest x27 57.4 us: contract_cols(): lax.dot_general(left, right, (((1,), (1,)), ((), ())), preferred_element_...]
    reshape x20 -> x0, local copies, waits for them, and re-layouts: 28.9 us -> none  [the longest x9 12.9 us: one_tick(): jnp.concatenate([blocks, stat_blocks], axis=2)]
    while x99 -> x0, local copies, waits for them, and re-layouts: 28.8 us -> none
  transfers between devices with their start and end apart: 30 -> 0, of which waited for: 30 -> 0; matrix products, arithmetic and copies ran while one was open for 3% -> 0% of each run, Pallas kernels for 0% -> 0%
where the time goes in v1:
time: 246 us; the launch traced here: 245 us
  Pallas kernels  235 us (96%)
  local copies, waits for them, and re-layouts  9.76 us (4%)
    pallas_call x1, Pallas kernels, body(): pl.pallas_call(fused_kernel, name='fused', out_shape=(jax.ShapeDtypeStruc...  235 us
    unnamed x13, local copies, waits for them, and re-layouts  7.7 us

profile of v1, /device:TPU:2, one launch (start us, length us, event | category | flops | bytes accessed | tf_op | source)
XLA Modules:
  0.0 245.3 jit_solution(1786939140875519007)
XLA Ops:
  0.6 0.0 copy-start
  0.7 0.7 copy-done
  1.3 0.1 constant_dynamic-slice_fusion
  1.4 0.7 broadcast_in_dim.18.gain_ref
  2.1 1.9 copy.11
  4.0 234.9 %fused.1 = (bf16[512,160]{1,0:T(8,128)(2,1)}, f32[320,432]{1,0:T(8,128)}, f32[320,432]{1,0:T(8,128)}, f32[432,320]{1,0:T(8,128)}, f32[8,160]{1,0:T(8,128)}) custom-call(bf16[512,160]{1,0:T(8,128)(2,1)} %bitcast.16, bf16[512,160]{1,0:T(8,128)(2,1)} %bitcast.17, f32[160,128]{1,0:T(8,128)} %broadcast_in_dim.18.gain_ref, bf16[320,432]{1,0:T(8,128)(2,1)} %bitcast.14, ...), custom_call_target="tpu_custom_call" | custom-call | tf_op jit(solution)/shard_map/fused/pallas_call | solution.py:504
  238.9 1.3 slice.3
  240.2 0.0 copy-start.3
  240.2 0.0 copy-start.2
  240.2 2.3 copy.12
  242.4 0.0 copy-done.3
  242.4 0.7 copy.16
  243.1 0.0 copy-done.2
  243.1 0.0 copy-start.1
  243.1 0.8 copy.17
  244.0 0.5 copy-done.1
  244.5 0.8 copy.18
Async XLA Ops:
  0.6 0.7 copy-start
  240.2 2.3 copy-start.3
  240.2 3.0 %copy-start.2 = (f32[320,432]{1,0:T(8,128)S(1)}, f32[320,432]{1,0:T(8,128)}, u32[]{:S(2)}) copy-start(f32[320,432]{1,0:T(8,128)} %get-tuple-element.11) | copy-start | bytes 1658884
  243.1 1.3 copy-start.1

commit v2 on v0

v2 whole, which is shorter than its diff:
```python
import jax
import jax.numpy as jnp
from jax import lax
from jax.experimental import pallas as pl
from jax.experimental.pallas import tpu as pltpu
from jax.sharding import PartitionSpec as P

EPS = 1e-05
MESH = pl.DeviceIdType.MESH
F32 = jnp.float32
BF16 = jnp.bfloat16

NY, NXH, NZ, NXL = 4, 2, 8, 2
NF, NT = NY * NXH, NZ * NXL
MICRO = 8
ROWS = 64
T = MICRO * ROWS
H = 2
TH = T // H
W = 160
PW = NXL * W
FL = 432
GU = 2 * FL
D = W * NT
NSEM = 200


def scope(name):
    return jax.named_scope(name)


def dot(a, b, ca, cb, precision=None):
    return lax.dot_general(
        a, b, (((ca,), (cb,)), ((), ())), preferred_element_type=F32, precision=precision
    )


def fused_kernel(
    x_ref,
    tg_ref,
    gain_ref,
    wg_ref,
    wu_ref,
    wd_ref,
    dx_ref,
    gg_ref,
    ug_ref,
    dg_ref,
    gn_ref,
    wgu,
    wd,
    n_all,
    dy_all,
    gu,
    dh,
    dgu,
    hid,
    unit,
    scale,
    stat,
    ssq_in,
    stat_in,
    gain_in,
    pdn,
    rdn,
    pf,
    pown,
    xs,
    xr,
    dxs,
    sgu,
    rgu,
    fgu,
    sgd,
    rgd,
    fgd,
    ssem,
    rsem,
    go,
):
    s = lax.axis_index("section")
    f = lax.axis_index("fsdp")
    t = lax.axis_index("tp")
    y, xh = lax.div(f, NXH), lax.rem(f, NXH)
    z, xl = lax.div(t, NXL), lax.rem(t, NXL)
    oh, ol = 1 - xh, 1 - xl

    def at_y(step):
        return (s, lax.rem(y + step + NY, NY) * NXH + xh, t)

    def at_z(step):
        return (s, f, lax.rem(z + step + NZ, NZ) * NXL + xl)

    dev = {
        "y+": at_y(1),
        "y-": at_y(-1),
        "z+": at_z(1),
        "z-": at_z(-1),
        "xh": (s, y * NXH + oh, t),
        "xl": (s, f, z * NXL + ol),
        "core": (1 - s, f, t),
    }
    tp_peers = [(s, f, lax.rem(t + k, NT)) for k in range(1, NT)]
    fs_peers = [(s, lax.rem(f + k, NF), t) for k in range(1, NF)]
    zblk = [lax.rem(z + k, NZ) for k in range(NZ)]
    own, left, right, far = (
        {"c": lax.rem(y + k, NY) * NXH + xh, "o": lax.rem(y + k, NY) * NXH + oh} for k in (0, 3, 1, 2)
    )

    ids = {}
    size = [0]
    ctx = [None]
    outgoing = {None: {}, 0: {}, 1: {}}

    def ident(name, n=1):
        if name not in ids:
            ids[name] = size[0]
            size[0] += n
        return ids[name]

    def copy(src, dst, m, to):
        return pltpu.make_async_remote_copy(
            src_ref=src,
            dst_ref=dst,
            send_sem=ssem.at[m],
            recv_sem=rsem.at[m],
            device_id=to,
            device_id_type=MESH,
        )

    def static(idx):
        return tuple(i if isinstance(i, (int, pl.Slice)) else 0 for i in idx)

    def send(src, si, dst, di, name, to, q=None):
        m = ident(name, 1 if q is None else 2)
        copy(src.at[si], dst.at[di], m if q is None else m + q, to).start()
        parts = outgoing[ctx[0]].setdefault(name, [])
        parts.append((q if isinstance(q, int) else len(parts), src, static(si)))

    def arrived(dst, di, name, q=None):
        m = ident(name, 1 if q is None else 2)
        r = dst.at[di]
        copy(r, r, m if q is None else m + q, dev["core"]).wait_recv()

    def wait_sent(which):
        for name, parts in outgoing[which].items():
            for k, src, si in parts:
                r = src.at[si]
                copy(r, r, ids[name] + k, dev["core"]).wait_send()

    def rows(n, step, fn):
        def body(i, c):
            fn(pl.multiple_of(i * step, step))
            return c

        lax.fori_loop(0, n // step, body, 0)

    barrier = pltpu.get_barrier_semaphore()
    for to in tp_peers + fs_peers + [dev["core"]]:
        pl.semaphore_signal(barrier, inc=1, device_id=to, device_id_type=MESH)

    with scope("prep"):
        eye = (
            lax.broadcasted_iota(jnp.int32, (W, W), 0) == lax.broadcasted_iota(jnp.int32, (W, W), 1)
        ).astype(BF16)
        xt = dot(eye, x_ref[...], 1, 1)
        ssq_in[t] = jnp.sum(xt * xt, axis=0, keepdims=True)
        unit[...] = xt

        @pl.when(s == 1)
        def _():
            top = dot(eye, tg_ref[...], 1, 1).astype(BF16)
            for h in range(H):
                dy_all[z, xl, h] = top[:, h * TH : (h + 1) * TH]

        def pack(r):
            wgu[f, pl.ds(r, 32), 0:FL] = wg_ref[pl.ds(r, 32), :]
            wgu[f, pl.ds(r, 32), FL:GU] = wu_ref[pl.ds(r, 32), :]

        rows(PW, 32, pack)

        def pack_down(r):
            wd[f, pl.ds(r, 48), :] = wd_ref[pl.ds(r, 48), :]

        rows(FL, 48, pack_down)

    with scope("barrier"):
        pl.semaphore_wait(barrier, NT - 1 + NF - 1 + 1)

    def spread(buf, name):
        for k, to in enumerate(tp_peers):
            send(buf, (t,), buf, (t,), (name, k), to)

    def collect(buf, name):
        for k in range(1, NT):
            arrived(buf, (lax.rem(t + NT - k, NT),), (name, k - 1))
        total = buf[0]
        for k in range(1, NT):
            total = total + buf[k]
        return total

    spread(ssq_in, "ssq")

    halves = {"u": ((0, 160), (160, 160)), "d": ((0, 208), (208, 224))}
    full = {"u": wgu, "d": wd}

    def w_own(a, dirs):
        for d in dirs:
            send(full[a], (f,), full[a], (f,), ("w", a, "own", d), dev[d])

    def w_fwd(a):
        arr = full[a]
        for d, blk, k in (("y+", left["c"], 0), ("y-", right["c"], 1)):
            arrived(arr, (blk,), ("w", a, "own", d))
            part = pl.ds(*halves[a][k])
            send(arr, (blk, part), arr, (blk, part), ("w", a, "fwd", d), dev[d])

    def w_pass(a):
        arr, blk = full[a], own["o"]
        arrived(arr, (blk,), ("w", a, "own", "xh"))
        for d in ("y+", "y-"):
            send(arr, (blk,), arr, (blk,), ("w", a, "pass", d), dev[d])

    def w_far(a):
        arr, blk = full[a], far["c"]
        for d, k in (("y+", 0), ("y-", 1)):
            arrived(arr, (blk, pl.ds(*halves[a][k])), ("w", a, "fwd", d))
        send(arr, (blk,), arr, (blk,), ("w", a, "far"), dev["xh"])

    def w_last(a):
        arr = full[a]
        arrived(arr, (left["o"],), ("w", a, "pass", "y+"))
        arrived(arr, (right["o"],), ("w", a, "pass", "y-"))
        arrived(arr, (far["o"],), ("w", a, "far"))

    def ag_own(buf, nm, hh=()):
        own_at = (z, xl, *hh)
        send(buf, own_at, buf, own_at, (nm, "xl", *hh), dev["xl"])
        send(buf, own_at, buf, own_at, (nm, "z+", 1, 0, *hh), dev["z+"])
        send(buf, own_at, buf, own_at, (nm, "z-", 1, 0, *hh), dev["z-"])

    def ag_partner(buf, nm, hh=()):
        at = (z, ol, *hh)
        arrived(buf, at, (nm, "xl", *hh))
        send(buf, at, buf, at, (nm, "z+", 1, 1, *hh), dev["z+"])
        send(buf, at, buf, at, (nm, "z-", 1, 1, *hh), dev["z-"])

    def ag_fwd(buf, nm, k, j, hh=()):
        q = (xl, ol)[j]
        for d, blk in (("z+", zblk[NZ - k]), ("z-", zblk[k])):
            at = (blk, q, *hh)
            arrived(buf, at, (nm, d, k, j, *hh))
            send(buf, at, buf, at, (nm, d, k + 1, j, *hh), dev[d])

    def ag_fwd3(buf, nm, hh=()):
        for d, blk, q in (("z+", zblk[5], 0), ("z-", zblk[3], 1)):
            for j in range(2):
                arrived(buf, (blk, (xl, ol)[j], *hh), (nm, d, 3, j, *hh))
            send(buf, (blk, q, *hh), buf, (blk, q, *hh), (nm, d, 4, *hh), dev[d])

    def ag_last(buf, nm, hh=()):
        arrived(buf, (zblk[4], 0, *hh), (nm, "z+", 4, *hh))
        arrived(buf, (zblk[4], 1, *hh), (nm, "z-", 4, *hh))

    def act(buf, i):
        return jnp.concatenate([buf[i, :, h].reshape(PW, TH) for h in range(H)], axis=1)

    def pick(i, table):
        v = table[0]
        for k in range(1, len(table)):
            v = jnp.where(i == k, table[k], v)
        return v

    order = [own["c"], left["c"], right["c"], own["o"], far["c"], left["o"], right["o"], far["o"]]

    def forward(a, b):
        def body(i, c):
            blk = pick(i, order)
            part = dot(wgu[blk], n_all[blk].reshape(PW, T), 0, 0)
            gu[...] = jnp.where(i == 0, part, gu[...] + part)
            return c

        lax.fori_loop(a, b, body, 0)

    dy_order = [zblk[k] for k in (0, 1, 7, 2, 6, 3, 5, 4)]

    def dhidden(a, b):
        def body(i, c):
            blk = pick(i, dy_order)
            part = dot(wd[blk], act(dy_all, blk), 1, 0)
            dh[...] = jnp.where(i == 0, part, dh[...] + part)
            return c

        lax.fori_loop(a, b, body, 0)

    def normalize():
        row_scale = lax.rsqrt(collect(ssq_in, "ssq") / D + EPS)
        scale[...] = row_scale
        u = unit[...] * row_scale
        unit[...] = u
        n_all[z, xl] = (u * gain_ref[:, 0:1]).astype(BF16)

    @pl.when(s == 1)
    def _():
        ctx[0] = 1
        with scope("a_own"):
            ag_own(dy_all, "dy")
            w_own("d", ("y+", "y-", "xh"))
            w_own("u", ("y+", "y-"))
        with scope("a_norm"):
            normalize()
            ag_own(n_all, "n")
            w_own("u", ("xh",))
        with scope("a_dyp"):
            ag_partner(dy_all, "dy")
        with scope("a_np"):
            ag_partner(n_all, "n")
        with scope("a_wfd"):
            w_fwd("d")
        for k in (1, 2):
            with scope(f"a_n{k}"):
                ag_fwd(n_all, "n", k, 0)
                ag_fwd(n_all, "n", k, 1)
            if k == 1:
                with scope("a_wfu"):
                    w_fwd("u")
        with scope("a_wpd"):
            w_pass("d")
        with scope("a_n3"):
            ag_fwd3(n_all, "n")
        with scope("a_dy1"):
            ag_fwd(dy_all, "dy", 1, 0)
            ag_fwd(dy_all, "dy", 1, 1)
        with scope("a_wpu"):
            w_pass("u")
        with scope("a_wxd"):
            w_far("d")
        with scope("a_dy2"):
            ag_fwd(dy_all, "dy", 2, 0)
            ag_fwd(dy_all, "dy", 2, 1)
        with scope("a_nl"):
            ag_last(n_all, "n")
        with scope("a_wxu"):
            w_far("u")
        with scope("a_f5"):
            forward(0, 5)
        with scope("a_dy3"):
            ag_fwd3(dy_all, "dy")
        pl.semaphore_signal(go, inc=1, device_id=dev["core"], device_id_type=MESH)
        with scope("a_wld"):
            w_last("d")
        with scope("a_h7"):
            dhidden(0, 7)
        with scope("a_dyl"):
            ag_last(dy_all, "dy")
            dhidden(7, 8)
        with scope("a_wlu"):
            w_last("u")
        with scope("a_f8"):
            forward(5, 8)
        ctx[0] = None

    @pl.when(s == 0)
    def _():
        ctx[0] = 0
        with scope("b_norm"):
            normalize()
        with scope("b_go"):
            pl.semaphore_wait(go, 1)
        with scope("b_own"):
            ag_own(n_all, "n")
            w_own("d", ("y+", "y-", "xh"))
            w_own("u", ("y+", "y-", "xh"))
        with scope("b_np"):
            ag_partner(n_all, "n")
        with scope("b_n1"):
            ag_fwd(n_all, "n", 1, 0)
            ag_fwd(n_all, "n", 1, 1)
        with scope("b_wfd"):
            w_fwd("d")
        with scope("b_n2"):
            ag_fwd(n_all, "n", 2, 0)
            ag_fwd(n_all, "n", 2, 1)
        with scope("b_wfu"):
            w_fwd("u")
        with scope("b_n3"):
            ag_fwd3(n_all, "n")
        with scope("b_wpd"):
            w_pass("d")
            w_pass("u")
        with scope("b_nl"):
            ag_last(n_all, "n")
        with scope("b_wxd"):
            w_far("d")
        with scope("b_wxu"):
            w_far("u")
        with scope("b_f5"):
            forward(0, 5)
        with scope("b_wl"):
            w_last("d")
            w_last("u")
        with scope("b_f8"):
            forward(5, 8)
        with scope("b_core"):
            for h in range(H):
                arrived(dy_all, (z, xl, h), ("core", h))
                ag_own(dy_all, "e", (h,))
        with scope("b_dyp"):
            for h in range(H):
                ag_partner(dy_all, "e", (h,))
        for k in (1, 2):
            with scope(f"b_dy{k}"):
                for h in range(H):
                    for j in range(2):
                        ag_fwd(dy_all, "e", k, j, (h,))
        with scope("b_dy3"):
            for h in range(H):
                ag_fwd3(dy_all, "e", (h,))
        with scope("b_h7"):
            dhidden(0, 7)
        with scope("b_dyl"):
            for h in range(H):
                ag_last(dy_all, "e", (h,))
            dhidden(7, 8)
        ctx[0] = None

    with scope("elem"):
        stat[...] = jnp.zeros_like(stat)

        def elementwise(r):
            gate = gu[pl.ds(r, 16), :]
            up = gu[pl.ds(pl.multiple_of(FL + r, 16), 16), :]
            dd = dh[pl.ds(r, 16), :]
            sig = jax.nn.sigmoid(gate)
            silu = gate * sig
            hid[pl.ds(r, 16), :] = (silu * up).astype(BF16)
            d_gate = (dd * up * sig * (1.0 + gate * (1.0 - sig))).astype(BF16)
            d_up = (dd * silu).astype(BF16)
            dgu[pl.ds(r, 16), :] = d_gate
            dgu[pl.ds(pl.multiple_of(FL + r, 16), 16), :] = d_up
            both = d_gate.astype(F32) * gate + d_up.astype(F32) * up
            stat[...] += both[0:8] + both[8:16]

        rows(FL, 16, elementwise)
        stat_in[t] = jnp.sum(stat[...], axis=0, keepdims=True)
        spread(stat_in, "stat")

    def partial(blk, h):
        return dot(wgu[blk], dgu[:, h * TH : (h + 1) * TH], 1, 0).reshape(NXL, W, TH)

    ways = (("z+", 0), ("z-", 1))

    def rs_first():
        def body(h, c):
            part = dot(wgu[zblk[4]], dgu[...], 1, 0).reshape(NXL, W, T)
            for hh in range(H):
                pdn[0, hh] = part[:, :, hh * TH : (hh + 1) * TH].astype(BF16)
            return c

        lax.fori_loop(0, 1, body, 0)
        for h in range(H):
            for d, w in ways:
                send(pdn, (0, h, w), rdn, (w, 0, h, w), ("rs", d, 1, h), dev[d], q=w)

    def rs_compute(k):
        def body(w, c):
            blk = jnp.where(w == 0, zblk[5 - k], zblk[3 + k])
            part = dot(wgu[blk], dgu[...], 1, 0).reshape(NXL, W, T)
            for hh in range(H):
                pf[w, hh] = part[:, :, hh * TH : (hh + 1) * TH]
            return c

        lax.fori_loop(0, 2, body, 0)

    def rs_step(k):
        slot = 2 * k - 3
        if k == 2:
            for h in range(H):
                for d, w in ways:
                    q = 1 - w
                    pdn[slot + w, h, q] = pf[w, h, q].astype(BF16)
                    send(pdn, (slot + w, h, q), rdn, (w, k - 1, h, q), ("rs", d, k, h), dev[d], q=q)
        for h in range(H):
            for j in range(2):
                for d, w in ways:
                    if k == 2:
                        q = w
                        if j:
                            continue
                    else:
                        q = (ol, xl)[j]
                    arrived(rdn, (w, k - 2, h, q), ("rs", d, k - 1, h), q=q)
                    pdn[slot + w, h, q] = (pf[w, h, q] + rdn[w, k - 2, h, q].astype(F32)).astype(BF16)
                    send(pdn, (slot + w, h, q), rdn, (w, k - 1, h, q), ("rs", d, k, h), dev[d], q=q)

    def rs_own():
        def body(h, c):
            part = dot(wgu[z], dgu[...], 1, 0).reshape(NXL, W, T)
            for hh in range(H):
                pown[hh] = part[:, :, hh * TH : (hh + 1) * TH]
            return c

        lax.fori_loop(0, 1, body, 0)

    def rs_last():
        for h in range(H):
            for q in (ol, xl):
                for d, w in ways:
                    arrived(rdn, (w, 3, h, q), ("rs", d, 4, h), q=q)
                if q is ol:
                    xs[h] = (
                        pown[h, q] + rdn[0, 3, h, q].astype(F32) + rdn[1, 3, h, q].astype(F32)
                    ).astype(BF16)
                    send(xs, (h,), xr, (h,), ("rx", h), dev["xl"])

    def dx_part(h, norm_stat):
        arrived(xr, (h,), ("rx", h))
        cols = slice(h * TH, (h + 1) * TH)
        d_normed = (
            pown[h, xl]
            + rdn[0, 3, h, xl].astype(F32)
            + rdn[1, 3, h, xl].astype(F32)
            + xr[h].astype(F32)
        )
        u = unit[:, cols]
        dx = dy_all[z, xl, h].astype(F32) + scale[:, cols] * (
            d_normed * gain_ref[:, 0:1] - u * norm_stat[:, cols]
        )
        dxs[h] = dx.astype(BF16)
        return d_normed * u

    def gain_dx(parts):
        total = dot(
            jnp.ones((8, T), F32), jnp.concatenate(parts, axis=1), 1, 1, lax.Precision.HIGHEST
        )
        gain_in[f] = total
        for k, to in enumerate(fs_peers):
            send(gain_in, (f,), gain_in, (f,), ("gain", k), to)
        for h in range(H):
            dx_ref[h * TH : (h + 1) * TH, :] = dot(dxs[h], eye, 0, 0).astype(BF16)

    sg, rg, fg = {"u": sgu, "d": sgd}, {"u": rgu, "d": rgd}, {"u": fgu, "d": fgd}
    size_of = {"u": (PW, 32), "d": (FL, 48)}

    def wgrad(a, blk):
        if a == "u":
            return dot(n_all[blk].reshape(PW, T), dgu[...], 1, 1)
        return dot(hid[...], act(dy_all, blk), 1, 1)

    direct = [far["o"], right["o"], left["o"]]
    kept = [far["c"], right["c"], left["c"], own["o"], own["c"]]

    def g_first(a):
        def body(i, c):
            sg[a][i] = wgrad(a, pick(i, direct)).astype(BF16)
            return c

        lax.fori_loop(0, 3, body, 0)
        for i, d in enumerate(("xh", "y+", "y-")):
            send(sg[a], (i,), rg[a], (i,), ("g", a, i), dev[d])

    def g_kept(a):
        def body(i, c):
            fg[a][i] = wgrad(a, pick(i, kept))
            return c

        lax.fori_loop(0, 5, body, 0)

    def g_sum(a, slot, own_i, recv, span=None):
        n, st = size_of[a]
        lo, n = span if span else (0, n)
        st = 16 if span else st

        def body(r):
            r = pl.multiple_of(r + lo, 16)
            v = fg[a][own_i, pl.ds(r, st), :]
            for k in recv:
                v = v + rg[a][k, pl.ds(r, st), :].astype(F32)
            sg[a][slot, pl.ds(r, st), :] = v.astype(BF16)

        rows(n, st, body)

    def g_far(a):
        arrived(rg[a], (0,), ("g", a, 0))
        g_sum(a, 3, 0, (0,))
        for d, k in (("y+", 0), ("y-", 1)):
            part = pl.ds(*halves[a][k])
            send(sg[a], (3, part), rg[a], (3, part), ("g", a, 3, d), dev[d])

    def g_near(a):
        for d, k, slot in (("y+", 0, 4), ("y-", 1, 5)):
            part = pl.ds(*halves[a][k])
            arrived(rg[a], (3, part), ("g", a, 3, d))
            g_sum(a, slot, 1 + k, (3,), halves[a][k])
            g_sum(a, slot, 1 + k, (), halves[a][1 - k])
            send(sg[a], (slot,), rg[a], (slot,), ("g", a, slot), dev[d])

    def g_partner(a):
        arrived(rg[a], (1,), ("g", a, 1))
        arrived(rg[a], (2,), ("g", a, 2))
        g_sum(a, 6, 3, (1, 2))
        send(sg[a], (6,), rg[a], (6,), ("g", a, 6), dev["xh"])

    def g_last(a):
        for k in (4, 5, 6):
            arrived(rg[a], (k,), ("g", a, k))
        n, st = size_of[a]

        def body(r):
            at = pl.ds(r, st)
            v = fg[a][4, at, :]
            for k in (4, 5, 6):
                v = v + rg[a][k, at, :].astype(F32)
            if a == "u":
                gg_ref[at, :] = v[:, 0:FL]
                ug_ref[at, :] = v[:, FL:GU]
            else:
                dg_ref[at, :] = v

        rows(n, st, body)

    @pl.when(s == 1)
    def _():
        ctx[0] = 1
        with scope("c_r1"):
            rs_first()
            rs_compute(2)
        for k in (2, 3, 4):
            with scope(f"c_r{k}"):
                rs_step(k)
                if k < 4:
                    rs_compute(k + 1)
                else:
                    rs_own()
        with scope("c_rl"):
            rs_last()
        with scope("c_stat"):
            norm_stat = collect(stat_in, "stat") / D
        with scope("c_dx"):
            parts = []
            for h in range(H):
                parts.append(dx_part(h, norm_stat))
                send(dxs, (h,), dy_all, (z, xl, h), ("core", h), dev["core"])
        with scope("c_gain"):
            gain_dx(parts)
        with scope("c_g1"):
            g_first("d")
            g_first("u")
        with scope("c_gk"):
            g_kept("d")
            g_kept("u")
        with scope("c_gfd"):
            g_far("d")
        with scope("c_gpd"):
            g_partner("d")
        with scope("c_gfu"):
            g_far("u")
        with scope("c_gnd"):
            g_near("d")
        with scope("c_gpu"):
            g_partner("u")
        with scope("c_gnu"):
            g_near("u")
        with scope("c_gld"):
            g_last("d")
        with scope("c_glu"):
            g_last("u")
        wait_sent(1)
        ctx[0] = None

    @pl.when(s == 0)
    def _():
        ctx[0] = 0
        with scope("d_r1"):
            rs_first()
        with scope("d_g1"):
            g_first("d")
            g_first("u")
        with scope("d_r2"):
            rs_compute(2)
            rs_step(2)
        with scope("d_gkd"):
            g_kept("d")
        with scope("d_r3"):
            rs_compute(3)
            rs_step(3)
        with scope("d_gku"):
            g_kept("u")
        with scope("d_gfd"):
            g_far("d")
        with scope("d_r4"):
            rs_compute(4)
            rs_step(4)
        with scope("d_gfu"):
            g_far("u")
        with scope("d_gpd"):
            g_partner("d")
        with scope("d_gnd"):
            g_near("d")
        with scope("d_gpu"):
            g_partner("u")
        with scope("d_gnu"):
            g_near("u")
        with scope("d_rl"):
            rs_own()
            rs_last()
            norm_stat = collect(stat_in, "stat") / D
        with scope("d_dx"):
            parts = [dx_part(h, norm_stat) for h in range(H)]
            gain_dx(parts)
        with scope("d_gld"):
            g_last("d")
        with scope("d_glu"):
            g_last("u")
        wait_sent(0)
        ctx[0] = None

    for k in range(1, NF):
        arrived(gain_in, (lax.rem(f + NF - k, NF),), ("gain", k - 1))
    gsum = gain_in[0]
    for k in range(1, NF):
        gsum = gsum + gain_in[k]
    gn_ref[...] = gsum
    wait_sent(None)
    assert size[0] <= NSEM, size[0]


def body(saved_inputs, top_grad, norm_gain, gate_weight, up_weight, down_weight):
    x = saved_inputs.reshape(T, W)
    tg = top_grad.reshape(T, W)
    gain = lax.dynamic_slice_in_dim(norm_gain[0], lax.axis_index("tp") * W, W)
    gain = jnp.broadcast_to(gain[:, None], (W, 128))
    vm = pl.BlockSpec(memory_space=pltpu.VMEM)
    out = pl.pallas_call(
        fused_kernel,
        name="fused",
        out_shape=(
            jax.ShapeDtypeStruct((T, W), BF16),
            jax.ShapeDtypeStruct((PW, FL), F32),
            jax.ShapeDtypeStruct((PW, FL), F32),
            jax.ShapeDtypeStruct((FL, PW), F32),
            jax.ShapeDtypeStruct((8, W), F32),
        ),
        in_specs=[vm] * 6,
        out_specs=[vm] * 5,
        scratch_shapes=[
            pltpu.VMEM((NF, PW, GU), BF16),
            pltpu.VMEM((NF, FL, PW), BF16),
            pltpu.VMEM((NZ, NXL, W, T), BF16),
            pltpu.VMEM((NZ, NXL, H, W, TH), BF16),
            pltpu.VMEM((GU, T), F32),
            pltpu.VMEM((FL, T), F32),
            pltpu.VMEM((GU, T), BF16),
            pltpu.VMEM((FL, T), BF16),
            pltpu.VMEM((W, T), F32),
            pltpu.VMEM((1, T), F32),
            pltpu.VMEM((8, T), F32),
            pltpu.VMEM((NT, 1, T), F32),
            pltpu.VMEM((NT, 1, T), F32),
            pltpu.VMEM((NF, 8, W), F32),
            pltpu.VMEM((7, H, NXL, W, TH), BF16),
            pltpu.VMEM((2, 4, H, NXL, W, TH), BF16),
            pltpu.VMEM((2, H, NXL, W, TH), F32),
            pltpu.VMEM((H, NXL, W, TH), F32),
            pltpu.VMEM((H, W, TH), BF16),
            pltpu.VMEM((H, W, TH), BF16),
            pltpu.VMEM((H, W, TH), BF16),
            pltpu.VMEM((7, PW, GU), BF16),
            pltpu.VMEM((7, PW, GU), BF16),
            pltpu.VMEM((5, PW, GU), F32),
            pltpu.VMEM((7, FL, PW), BF16),
            pltpu.VMEM((7, FL, PW), BF16),
            pltpu.VMEM((5, FL, PW), F32),
            pltpu.SemaphoreType.DMA((NSEM,)),
            pltpu.SemaphoreType.DMA((NSEM,)),
            pltpu.SemaphoreType.REGULAR,
        ],
        compiler_params=pltpu.CompilerParams(
            collective_id=0, has_side_effects=True, vmem_limit_bytes=62 * 2**20
        ),
    )(x, tg, gain, gate_weight[0], up_weight[0], down_weight[0])
    dx, gg, ug, dg, gn = out
    return (
        dx.reshape(1, MICRO, ROWS, W),
        gg[None],
        ug[None],
        dg[None],
        gn[0:1],
    )


def solution(mesh):
    return jax.shard_map(
        body,
        mesh=mesh,
        in_specs=(
            P("section", None, "fsdp", "tp"),
            P(None, "fsdp", "tp"),
            P("section", None),
            P("section", "fsdp", "tp"),
            P("section", "fsdp", "tp"),
            P("section", "tp", "fsdp"),
        ),
        out_specs=(
            P("section", None, "fsdp", "tp"),
            P("section", "fsdp", "tp"),
            P("section", "fsdp", "tp"),
            P("section", "tp", "fsdp"),
            P("section", "tp"),
        ),
        check_vma=False,
    )
```

time: 1870 us -> 168 us (0.09)
  waiting for transfers between devices: 1220 us -> 0 us
  blocking collectives: 314 us -> 0 us
  Pallas kernels: 0 us -> 156 us
  local copies, waits for them, and re-layouts: 162 us -> 9.76 us
  matrix products: 72.4 us -> 0 us
  other arithmetic: 58.2 us -> 0 us
    while x36 -> x0, waiting for transfers between devices: 913 us -> none
    all_gather x19 -> x0, blocking collectives: 290 us -> none  [gathered_by_axis(): x = lax.all_gather(x, axis, axis=dim, tiled=True)]
    pallas_call x0 -> x1, Pallas kernels: none -> 156 us  [body(): pl.pallas_call(fused_kernel, name='fused', out_shape=(jax.ShapeDtypeStruc...]
    all_gather x2 -> x0, waiting for transfers between devices: 151 us -> none  [the longest x1 87.5 us: one_gather(): lines, at, finished = (lax.all_gather(vector, axis), 0, [])]
    unnamed x4 -> x0, waiting for transfers between devices: 148 us -> none
    dot_general x32 -> x0, matrix products: 72.4 us -> none  [the longest x27 57.4 us: contract_cols(): lax.dot_general(left, right, (((1,), (1,)), ((), ())), preferred_element_...]
    reshape x20 -> x0, local copies, waits for them, and re-layouts: 28.9 us -> none  [the longest x9 12.9 us: one_tick(): jnp.concatenate([blocks, stat_blocks], axis=2)]
    while x99 -> x0, local copies, waits for them, and re-layouts: 28.8 us -> none
  transfers between devices with their start and end apart: 30 -> 0, of which waited for: 30 -> 0; matrix products, arithmetic and copies ran while one was open for 3% -> 0% of each run, Pallas kernels for 0% -> 0%
where the time goes in v2:
time: 168 us; the launch traced here: 167 us
  Pallas kernels  156 us (93%)
  local copies, waits for them, and re-layouts  9.76 us (6%)
    pallas_call x1, Pallas kernels, body(): pl.pallas_call(fused_kernel, name='fused', out_shape=(jax.ShapeDtypeStruc...  156 us
    unnamed x13, local copies, waits for them, and re-layouts  7.7 us

profile of v2, /device:TPU:2, one launch (start us, length us, event | category | flops | bytes accessed | tf_op | source)
XLA Modules:
  0.0 166.8 jit_solution(4766575512848118872)
XLA Ops:
  0.6 0.0 copy-start
  0.7 0.7 copy-done
  1.3 0.1 constant_dynamic-slice_fusion
  1.4 0.7 broadcast_in_dim.18.gain_ref
  2.1 1.9 %copy.11 = bf16[1,432,320]{2,1,0:T(8,128)(2,1)} copy(bf16[1,432,320]{1,2,0:T(8,128)(2,1)} %param.11) | data formatting | bytes 552960 | tf_op args[5]
  4.0 156.4 %fused.1 = (bf16[512,160]{1,0:T(8,128)(2,1)}, f32[320,432]{1,0:T(8,128)}, f32[320,432]{1,0:T(8,128)}, f32[432,320]{1,0:T(8,128)}, f32[8,160]{1,0:T(8,128)}) custom-call(bf16[512,160]{1,0:T(8,128)(2,1)} %bitcast.16, bf16[512,160]{1,0:T(8,128)(2,1)} %bitcast.17, f32[160,128]{1,0:T(8,128)} %broadcast_in_dim.18.gain_ref, bf16[320,432]{1,0:T(8,128)(2,1)} %bitcast.14, ...), custom_call_target="tpu_custom_call" | custom-call | tf_op jit(solution)/shard_map/fused/pallas_call | solution.py:734
  160.4 1.3 slice.3
  161.6 0.0 copy-start.3
  161.6 0.0 copy-start.2
  161.6 2.3 %copy.12 = f32[1,432,320]{1,2,0:T(8,128)} copy(f32[1,432,320]{2,1,0:T(8,128)} %bitcast.11) | data formatting | bytes 1105920
  163.9 0.0 copy-done.3
  163.9 0.7 copy.16
  164.6 0.0 copy-done.2
  164.6 0.0 copy-start.1
  164.6 0.8 copy.17
  165.5 0.5 copy-done.1
  165.9 0.8 copy.18
Async XLA Ops:
  0.6 0.7 copy-start
  161.6 2.3 %copy-start.3 = (bf16[512,160]{1,0:T(8,128)(2,1)S(1)}, bf16[512,160]{1,0:T(8,128)(2,1)}, u32[]{:S(2)}) copy-start(bf16[512,160]{1,0:T(8,128)(2,1)} %get-tuple-element.10) | copy-start | bytes 491524
  161.6 3.0 %copy-start.2 = (f32[320,432]{1,0:T(8,128)S(1)}, f32[320,432]{1,0:T(8,128)}, u32[]{:S(2)}) copy-start(f32[320,432]{1,0:T(8,128)} %get-tuple-element.11) | copy-start | bytes 1658884
  164.6 1.3 copy-start.1

commit v3 on v2

--- a/solution.py
+++ b/solution.py
@@ -22,7 +22,10 @@
 FL = 432
 GU = 2 * FL
 D = W * NT
-NSEM = 200
+UW = 896
+DH = 384
+DR = PW + 16
+NSEM = 180
 
 
 def scope(name):
@@ -36,9 +39,20 @@
 
 
 def fused_kernel(
+    x_hbm,
+    tg_hbm,
+    gain_hbm,
+    wg_hbm,
+    wu_hbm,
+    wd_hbm,
+    dx_hbm,
+    gg_hbm,
+    ug_hbm,
+    dg_hbm,
+    gn_hbm,
     x_ref,
     tg_ref,
-    gain_ref,
+    gain_row,
     wg_ref,
     wu_ref,
     wd_ref,
@@ -47,6 +61,7 @@
     ug_ref,
     dg_ref,
     gn_ref,
+    gain,
     wgu,
     wd,
     n_all,
@@ -55,6 +70,7 @@
     dh,
     dgu,
     hid,
+    hid_mid,
     unit,
     scale,
     stat,
@@ -76,6 +92,7 @@
     fgd,
     ssem,
     rsem,
+    lsem,
     go,
 ):
     s = lax.axis_index("section")
@@ -159,13 +176,30 @@
     for to in tp_peers + fs_peers + [dev["core"]]:
         pl.semaphore_signal(barrier, inc=1, device_id=to, device_id_type=MESH)
 
+    loads = [
+        pltpu.make_async_copy(src, dst, lsem.at[k])
+        for k, (src, dst) in enumerate(
+            (
+                (x_hbm, x_ref),
+                (tg_hbm, tg_ref),
+                (gain_hbm, gain_row),
+                (wd_hbm, wd_ref),
+                (wg_hbm, wg_ref),
+                (wu_hbm, wu_ref),
+            )
+        )
+    ]
+    for c in loads:
+        c.start()
     with scope("prep"):
         eye = (
             lax.broadcasted_iota(jnp.int32, (W, W), 0) == lax.broadcasted_iota(jnp.int32, (W, W), 1)
         ).astype(BF16)
+        loads[0].wait()
         xt = dot(eye, x_ref[...], 1, 1)
         ssq_in[t] = jnp.sum(xt * xt, axis=0, keepdims=True)
         unit[...] = xt
+        loads[1].wait()
 
         @pl.when(s == 1)
         def _():
@@ -173,16 +207,38 @@
             for h in range(H):
                 dy_all[z, xl, h] = top[:, h * TH : (h + 1) * TH]
 
+        loads[3].wait()
+
+        def pack_down(r):
+            wd[f, pl.ds(r, 32), :] = wd_ref[pl.ds(r, 32), 0:DH]
+            wgu[f, pl.ds(r, 32), GU:UW] = wd_ref[pl.ds(r, 32), DH : DH + 32]
+
+        rows(PW, 32, pack_down)
+        last = (
+            lax.broadcasted_iota(jnp.int32, (16, FL), 0) + (FL - 16)
+            == lax.broadcasted_iota(jnp.int32, (16, FL), 1)
+        ).astype(BF16)
+        wd[f, PW:DR, 0:PW] = dot(last, wd_ref[...], 1, 1).astype(BF16)
+        loads[4].wait()
+        loads[5].wait()
+
         def pack(r):
             wgu[f, pl.ds(r, 32), 0:FL] = wg_ref[pl.ds(r, 32), :]
             wgu[f, pl.ds(r, 32), FL:GU] = wu_ref[pl.ds(r, 32), :]
 
         rows(PW, 32, pack)
-
-        def pack_down(r):
-            wd[f, pl.ds(r, 48), :] = wd_ref[pl.ds(r, 48), :]
-
-        rows(FL, 48, pack_down)
+        loads[2].wait()
+
+        def gains(r):
+            mine = lax.broadcasted_iota(jnp.int32, (32, D), 1) == (
+                lax.broadcasted_iota(jnp.int32, (32, D), 0) + (t * W + r)
+            )
+            row = jnp.broadcast_to(gain_row[...], (32, D))
+            gain[pl.ds(r, 32), :] = jnp.broadcast_to(
+                jnp.sum(jnp.where(mine, row, 0.0), axis=1, keepdims=True), (32, 128)
+            )
+
+        rows(W, 32, gains)
 
     with scope("barrier"):
         pl.semaphore_wait(barrier, NT - 1 + NF - 1 + 1)
@@ -201,7 +257,7 @@
 
     spread(ssq_in, "ssq")
 
-    halves = {"u": ((0, 160), (160, 160)), "d": ((0, 208), (208, 224))}
+    halves = {"u": ((0, 160), (160, 160)), "d": ((0, 160), (160, 176))}
     full = {"u": wgu, "d": wd}
 
     def w_own(a, dirs):
@@ -262,6 +318,31 @@
         arrived(buf, (zblk[4], 0, *hh), (nm, "z+", 4, *hh))
         arrived(buf, (zblk[4], 1, *hh), (nm, "z-", 4, *hh))
 
+    def agz_pair(buf, nm, k, blk):
+        send(buf, (blk, xl), buf, (blk, xl), (nm, "pair", k), dev["xl"])
+
+    def agz_own(buf, nm):
+        for d in ("z+", "z-"):
+            send(buf, (z, xl), buf, (z, xl), (nm, d, 1), dev[d])
+        agz_pair(buf, nm, 0, z)
+
+    def agz_fwd(buf, nm, k):
+        for d, blk in (("z+", zblk[NZ - k]), ("z-", zblk[k])):
+            arrived(buf, (blk, xl), (nm, d, k))
+            part = () if k < 3 else (pl.ds(0, 80),) if d == "z+" else (pl.ds(80, 80),)
+            send(buf, (blk, xl, *part), buf, (blk, xl, *part), (nm, d, k + 1), dev[d])
+        agz_pair(buf, nm, NZ - k, zblk[NZ - k])
+        agz_pair(buf, nm, k, zblk[k])
+
+    def agz_far(buf, nm):
+        for d, lo in (("z+", 0), ("z-", 80)):
+            arrived(buf, (zblk[4], xl, pl.ds(lo, 80)), (nm, d, 4))
+        agz_pair(buf, nm, 4, zblk[4])
+
+    def agz_last(buf, nm):
+        for k in range(NZ):
+            arrived(buf, (zblk[k], ol), (nm, "pair", k))
+
     def act(buf, i):
         return jnp.concatenate([buf[i, :, h].reshape(PW, TH) for h in range(H)], axis=1)
 
@@ -271,34 +352,55 @@
             v = jnp.where(i == k, table[k], v)
         return v
 
-    order = [own["c"], left["c"], right["c"], own["o"], far["c"], left["o"], right["o"], far["o"]]
-
-    def forward(a, b):
-        def body(i, c):
-            blk = pick(i, order)
-            part = dot(wgu[blk], n_all[blk].reshape(PW, T), 0, 0)
-            gu[...] = jnp.where(i == 0, part, gu[...] + part)
-            return c
-
-        lax.fori_loop(a, b, body, 0)
-
-    dy_order = [zblk[k] for k in (0, 1, 7, 2, 6, 3, 5, 4)]
-
-    def dhidden(a, b):
-        def body(i, c):
-            blk = pick(i, dy_order)
-            part = dot(wd[blk], act(dy_all, blk), 1, 0)
-            dh[...] = jnp.where(i == 0, part, dh[...] + part)
-            return c
-
-        lax.fori_loop(a, b, body, 0)
+    groups = ((0, 1, 7), (2, 6), (3, 5, 4))
+
+    def together(parts):
+        return jnp.concatenate(parts, axis=0)
+
+    def forward(g):
+        blks = [zblk[k] for k in groups[g]]
+        part = dot(
+            together([wgu[b] for b in blks]),
+            together([n_all[b].reshape(PW, T) for b in blks]),
+            0,
+            0,
+        )
+        gu[...] = part if g == 0 else gu[...] + part
+
+    def dhidden(g):
+        blks = [zblk[k] for k in groups[g]]
+        dys = [act(dy_all, b) for b in blks]
+        dy = together(dys)
+        parts = (
+            (0, dot(together([wd[b, 0:PW] for b in blks]), dy, 0, 0)),
+            (DH, dot(together([wgu[b, :, UW - 128 : UW] for b in blks]), dy, 0, 0)),
+        )
+        for r, part in parts:
+            at = pl.ds(r, part.shape[0])
+            dh[at, :] = part if g == 0 else dh[at, :] + part
+        part = dot(wd[blks[0], PW:DR, 0:PW], dys[0], 1, 0)
+        for b, d in zip(blks[1:], dys[1:]):
+            part = part + dot(wd[b, PW:DR, 0:PW], d, 1, 0)
+        at = pl.ds(DH + 128, 16)
+        dh[at, :] = part if g == 0 else dh[at, :] + part
+
+    def hidden():
+        def body(r):
+            gate = gu[pl.ds(r, 16), :]
+            up = gu[pl.ds(pl.multiple_of(FL + r, 16), 16), :]
+            hid[pl.ds(r, 16), :] = (gate * jax.nn.sigmoid(gate) * up).astype(BF16)
+
+        rows(FL, 16, body)
+        hid_mid[0:96, :] = jnp.zeros((96, T), BF16)
+        hid_mid[96:128, :] = hid[DH : DH + 32, :]
+        dgu[GU:UW, :] = jnp.zeros((UW - GU, T), BF16)
 
     def normalize():
         row_scale = lax.rsqrt(collect(ssq_in, "ssq") / D + EPS)
         scale[...] = row_scale
         u = unit[...] * row_scale
         unit[...] = u
-        n_all[z, xl] = (u * gain_ref[:, 0:1]).astype(BF16)
+        n_all[z, xl] = (u * gain[:, 0:1]).astype(BF16)
 
     @pl.when(s == 1)
     def _():
@@ -309,55 +411,65 @@
             w_own("u", ("y+", "y-"))
         with scope("a_norm"):
             normalize()
+        with scope("a_nO"):
             ag_own(n_all, "n")
             w_own("u", ("xh",))
-        with scope("a_dyp"):
+        with scope("a_dyP"):
             ag_partner(dy_all, "dy")
-        with scope("a_np"):
-            ag_partner(n_all, "n")
+        with scope("a_dy10"):
+            ag_fwd(dy_all, "dy", 1, 0)
         with scope("a_wfd"):
             w_fwd("d")
-        for k in (1, 2):
-            with scope(f"a_n{k}"):
-                ag_fwd(n_all, "n", k, 0)
-                ag_fwd(n_all, "n", k, 1)
-            if k == 1:
-                with scope("a_wfu"):
-                    w_fwd("u")
-        with scope("a_wpd"):
+        with scope("a_nP"):
+            ag_partner(n_all, "n")
+        with scope("a_n10"):
+            ag_fwd(n_all, "n", 1, 0)
+        with scope("a_dy11"):
+            ag_fwd(dy_all, "dy", 1, 1)
+        with scope("a_wfu"):
+            w_fwd("u")
             w_pass("d")
+        with scope("a_n11"):
+            ag_fwd(n_all, "n", 1, 1)
+        with scope("a_wxd"):
+            w_far("d")
+        with scope("a_dy20"):
+            ag_fwd(dy_all, "dy", 2, 0)
+        with scope("a_wpu"):
+            w_pass("u")
+        with scope("a_n20"):
+            ag_fwd(n_all, "n", 2, 0)
+        with scope("a_wxu"):
+            w_far("u")
+        with scope("a_n21"):
+            ag_fwd(n_all, "n", 2, 1)
+        with scope("a_dy21"):
+            ag_fwd(dy_all, "dy", 2, 1)
         with scope("a_n3"):
             ag_fwd3(n_all, "n")
-        with scope("a_dy1"):
-            ag_fwd(dy_all, "dy", 1, 0)
-            ag_fwd(dy_all, "dy", 1, 1)
-        with scope("a_wpu"):
-            w_pass("u")
-        with scope("a_wxd"):
-            w_far("d")
-        with scope("a_dy2"):
-            ag_fwd(dy_all, "dy", 2, 0)
-            ag_fwd(dy_all, "dy", 2, 1)
+            pl.semaphore_signal(go, inc=1, device_id=dev["core"], device_id_type=MESH)
+        with scope("a_wl"):
+            w_last("d")
+            w_last("u")
+        with scope("a_h0"):
+            dhidden(0)
+        with scope("a_dy3"):
+            ag_fwd3(dy_all, "dy")
+        with scope("a_f0"):
+            forward(0)
+        with scope("a_f1"):
+            forward(1)
+        with scope("a_h1"):
+            dhidden(1)
         with scope("a_nl"):
             ag_last(n_all, "n")
-        with scope("a_wxu"):
-            w_far("u")
-        with scope("a_f5"):
-            forward(0, 5)
-        with scope("a_dy3"):
-            ag_fwd3(dy_all, "dy")
-        pl.semaphore_signal(go, inc=1, device_id=dev["core"], device_id_type=MESH)
-        with scope("a_wld"):
-            w_last("d")
-        with scope("a_h7"):
-            dhidden(0, 7)
+        with scope("a_f2"):
+            forward(2)
+            hidden()
         with scope("a_dyl"):
             ag_last(dy_all, "dy")
-            dhidden(7, 8)
-        with scope("a_wlu"):
-            w_last("u")
-        with scope("a_f8"):
-            forward(5, 8)
+        with scope("a_h2"):
+            dhidden(2)
         ctx[0] = None
 
     @pl.when(s == 0)
@@ -368,39 +480,41 @@
         with scope("b_go"):
             pl.semaphore_wait(go, 1)
         with scope("b_own"):
-            ag_own(n_all, "n")
+            agz_own(n_all, "n")
             w_own("d", ("y+", "y-", "xh"))
             w_own("u", ("y+", "y-", "xh"))
-        with scope("b_np"):
-            ag_partner(n_all, "n")
         with scope("b_n1"):
-            ag_fwd(n_all, "n", 1, 0)
-            ag_fwd(n_all, "n", 1, 1)
+            agz_fwd(n_all, "n", 1)
         with scope("b_wfd"):
             w_fwd("d")
         with scope("b_n2"):
-            ag_fwd(n_all, "n", 2, 0)
-            ag_fwd(n_all, "n", 2, 1)
+            agz_fwd(n_all, "n", 2)
         with scope("b_wfu"):
             w_fwd("u")
-        with scope("b_n3"):
-            ag_fwd3(n_all, "n")
-        with scope("b_wpd"):
             w_pass("d")
-            w_pass("u")
-        with scope("b_nl"):
-            ag_last(n_all, "n")
         with scope("b_wxd"):
             w_far("d")
+        with scope("b_wpu"):
+            w_pass("u")
+        with scope("b_n3"):
+            agz_fwd(n_all, "n", 3)
         with scope("b_wxu"):
             w_far("u")
-        with scope("b_f5"):
-            forward(0, 5)
+        with scope("b_n4"):
+            agz_far(n_all, "n")
+        with scope("b_nl"):
+            agz_last(n_all, "n")
         with scope("b_wl"):
             w_last("d")
             w_last("u")
-        with scope("b_f8"):
-            forward(5, 8)
+        with scope("b_f0"):
+            forward(0)
+        with scope("b_f1"):
+            forward(1)
+        with scope("b_f2"):
+            forward(2)
+        with scope("b_hid"):
+            hidden()
         with scope("b_core"):
             for h in range(H):
                 arrived(dy_all, (z, xl, h), ("core", h))
@@ -408,20 +522,26 @@
         with scope("b_dyp"):
             for h in range(H):
                 ag_partner(dy_all, "e", (h,))
-        for k in (1, 2):
-            with scope(f"b_dy{k}"):
-                for h in range(H):
-                    for j in range(2):
-                        ag_fwd(dy_all, "e", k, j, (h,))
+        with scope("b_dy1"):
+            for h in range(H):
+                for j in range(2):
+                    ag_fwd(dy_all, "e", 1, j, (h,))
+        with scope("b_dy2"):
+            for h in range(H):
+                for j in range(2):
+                    ag_fwd(dy_all, "e", 2, j, (h,))
+        with scope("b_h0"):
+            dhidden(0)
         with scope("b_dy3"):
             for h in range(H):
                 ag_fwd3(dy_all, "e", (h,))
-        with scope("b_h7"):
-            dhidden(0, 7)
+        with scope("b_h1"):
+            dhidden(1)
         with scope("b_dyl"):
             for h in range(H):
                 ag_last(dy_all, "e", (h,))
-            dhidden(7, 8)
+        with scope("b_h2"):
+            dhidden(2)
         ctx[0] = None
 
     with scope("elem"):
@@ -430,10 +550,9 @@
         def elementwise(r):
             gate = gu[pl.ds(r, 16), :]
             up = gu[pl.ds(pl.multiple_of(FL + r, 16), 16), :]
-            dd = dh[pl.ds(r, 16), :]
+            dd = dh[pl.ds(pl.multiple_of(jnp.where(r < DH, r, r + 96), 16), 16), :]
             sig = jax.nn.sigmoid(gate)
             silu = gate * sig
-            hid[pl.ds(r, 16), :] = (silu * up).astype(BF16)
             d_gate = (dd * up * sig * (1.0 + gate * (1.0 - sig))).astype(BF16)
             d_up = (dd * silu).astype(BF16)
             dgu[pl.ds(r, 16), :] = d_gate
@@ -445,14 +564,11 @@
         stat_in[t] = jnp.sum(stat[...], axis=0, keepdims=True)
         spread(stat_in, "stat")
 
-    def partial(blk, h):
-        return dot(wgu[blk], dgu[:, h * TH : (h + 1) * TH], 1, 0).reshape(NXL, W, TH)
-
     ways = (("z+", 0), ("z-", 1))
 
     def rs_first():
         def body(h, c):
-            part = dot(wgu[zblk[4]], dgu[...], 1, 0).reshape(NXL, W, T)
+            part = dot(wgu[zblk[4], :, 0:GU], dgu[0:GU, :], 1, 0).reshape(NXL, W, T)
             for hh in range(H):
                 pdn[0, hh] = part[:, :, hh * TH : (hh + 1) * TH].astype(BF16)
             return c
@@ -465,7 +581,7 @@
     def rs_compute(k):
         def body(w, c):
             blk = jnp.where(w == 0, zblk[5 - k], zblk[3 + k])
-            part = dot(wgu[blk], dgu[...], 1, 0).reshape(NXL, W, T)
+            part = dot(wgu[blk, :, 0:GU], dgu[0:GU, :], 1, 0).reshape(NXL, W, T)
             for hh in range(H):
                 pf[w, hh] = part[:, :, hh * TH : (hh + 1) * TH]
             return c
@@ -495,7 +611,7 @@
 
     def rs_own():
         def body(h, c):
-            part = dot(wgu[z], dgu[...], 1, 0).reshape(NXL, W, T)
+            part = dot(wgu[z, :, 0:GU], dgu[0:GU, :], 1, 0).reshape(NXL, W, T)
             for hh in range(H):
                 pown[hh] = part[:, :, hh * TH : (hh + 1) * TH]
             return c
@@ -524,10 +640,17 @@
         )
         u = unit[:, cols]
         dx = dy_all[z, xl, h].astype(F32) + scale[:, cols] * (
-            d_normed * gain_ref[:, 0:1] - u * norm_stat[:, cols]
+            d_normed * gain[:, 0:1] - u * norm_stat[:, cols]
         )
         dxs[h] = dx.astype(BF16)
         return d_normed * u
+
+    stores = []
+
+    def store(src, dst):
+        c = pltpu.make_async_copy(src, dst, lsem.at[6 + len(stores)])
+        c.start()
+        stores.append(c)
 
     def gain_dx(parts):
         total = dot(
@@ -538,21 +661,29 @@
             send(gain_in, (f,), gain_in, (f,), ("gain", k), to)
         for h in range(H):
             dx_ref[h * TH : (h + 1) * TH, :] = dot(dxs[h], eye, 0, 0).astype(BF16)
+        store(dx_ref, dx_hbm)
 
     sg, rg, fg = {"u": sgu, "d": sgd}, {"u": rgu, "d": rgd}, {"u": fgu, "d": fgd}
-    size_of = {"u": (PW, 32), "d": (FL, 48)}
-
-    def wgrad(a, blk):
+    size_of = {"u": (PW, 32), "d": (DR, 48)}
+
+    def wgrad(a, blk, dst, i):
+        dy = act(dy_all, blk)
         if a == "u":
-            return dot(n_all[blk].reshape(PW, T), dgu[...], 1, 1)
-        return dot(hid[...], act(dy_all, blk), 1, 1)
+            cut = UW - 128
+            n = n_all[blk].reshape(PW, T)
+            dst[i, :, 0:cut] = dot(n, dgu[0:cut, :], 1, 1).astype(dst.dtype)
+            edge = dot(n, dgu[cut:UW, :], 1, 1) + dot(dy, hid_mid[...], 1, 1)
+            dst[i, :, cut:UW] = edge.astype(dst.dtype)
+        else:
+            dst[i, 0:PW, :] = dot(dy, hid[0:DH, :], 1, 1).astype(dst.dtype)
+            dst[i, PW:DR, 0:PW] = dot(hid[FL - 16 : FL, :], dy, 1, 1).astype(dst.dtype)
 
     direct = [far["o"], right["o"], left["o"]]
     kept = [far["c"], right["c"], left["c"], own["o"], own["c"]]
 
     def g_first(a):
         def body(i, c):
-            sg[a][i] = wgrad(a, pick(i, direct)).astype(BF16)
+            wgrad(a, pick(i, direct), sg[a], i)
             return c
 
         lax.fori_loop(0, 3, body, 0)
@@ -561,7 +692,7 @@
 
     def g_kept(a):
         def body(i, c):
-            fg[a][i] = wgrad(a, pick(i, kept))
+            wgrad(a, pick(i, kept), fg[a], i)
             return c
 
         lax.fori_loop(0, 5, body, 0)
@@ -604,20 +735,52 @@
     def g_last(a):
         for k in (4, 5, 6):
             arrived(rg[a], (k,), ("g", a, k))
-        n, st = size_of[a]
-
-        def body(r):
-            at = pl.ds(r, st)
+
+        def total(at):
             v = fg[a][4, at, :]
             for k in (4, 5, 6):
                 v = v + rg[a][k, at, :].astype(F32)
+            return v
+
+        def body(r):
+            at = pl.ds(r, 32)
+            v = total(at)
             if a == "u":
                 gg_ref[at, :] = v[:, 0:FL]
                 ug_ref[at, :] = v[:, FL:GU]
+                dg_ref[at, DH : DH + 32] = v[:, GU:UW]
             else:
-                dg_ref[at, :] = v
-
-        rows(n, st, body)
+                dg_ref[at, 0:DH] = v
+
+        if a == "d":
+            rows(PW, 32, body)
+            v = total(pl.ds(PW, 16))[:, 0:PW]
+            unit16 = (
+                lax.broadcasted_iota(jnp.int32, (16, 16), 0)
+                == lax.broadcasted_iota(jnp.int32, (16, 16), 1)
+            ).astype(F32)
+            dg_ref[:, DH + 32 : FL] = dot(v, unit16, 0, 0, lax.Precision.HIGHEST)
+            return
+        for c in range(2):
+            def part(r, c=c):
+                body(pl.multiple_of(r + c * 160, 16))
+
+            rows(160, 32, part)
+            at = pl.ds(c * 160, 160)
+            for v_ref, hbm in ((gg_ref, gg_hbm), (ug_ref, ug_hbm), (dg_ref, dg_hbm)):
+                store(v_ref.at[at], hbm.at[at])
+
+    def finish():
+        for k in range(1, NF):
+            arrived(gain_in, (lax.rem(f + NF - k, NF),), ("gain", k - 1))
+        gsum = gain_in[0]
+        for k in range(1, NF):
+            gsum = gsum + gain_in[k]
+        gn_ref[...] = gsum[0:1]
+        store(gn_ref, gn_hbm)
+        for c in stores:
+            c.wait()
+        del stores[:]
 
     @pl.when(s == 1)
     def _():
@@ -625,13 +788,15 @@
         with scope("c_r1"):
             rs_first()
             rs_compute(2)
-        for k in (2, 3, 4):
-            with scope(f"c_r{k}"):
-                rs_step(k)
-                if k < 4:
-                    rs_compute(k + 1)
-                else:
-                    rs_own()
+        with scope("c_r2"):
+            rs_step(2)
+            rs_compute(3)
+        with scope("c_r3"):
+            rs_step(3)
+            rs_compute(4)
+        with scope("c_r4"):
+            rs_step(4)
+            rs_own()
         with scope("c_rl"):
             rs_last()
         with scope("c_stat"):
@@ -641,11 +806,11 @@
             for h in range(H):
                 parts.append(dx_part(h, norm_stat))
                 send(dxs, (h,), dy_all, (z, xl, h), ("core", h), dev["core"])
-        with scope("c_gain"):
-            gain_dx(parts)
         with scope("c_g1"):
             g_first("d")
             g_first("u")
+        with scope("c_gain"):
+            gain_dx(parts)
         with scope("c_gk"):
             g_kept("d")
             g_kept("u")
@@ -665,7 +830,9 @@
             g_last("d")
         with scope("c_glu"):
             g_last("u")
-        wait_sent(1)
+        with scope("c_end"):
+            finish()
+            wait_sent(1)
         ctx[0] = None
 
     @pl.when(s == 0)
@@ -697,14 +864,14 @@
             g_partner("d")
         with scope("d_gnd"):
             g_near("d")
+        with scope("d_rl"):
+            rs_own()
+            rs_last()
+            norm_stat = collect(stat_in, "stat") / D
         with scope("d_gpu"):
             g_partner("u")
         with scope("d_gnu"):
             g_near("u")
-        with scope("d_rl"):
-            rs_own()
-            rs_last()
-            norm_stat = collect(stat_in, "stat") / D
         with scope("d_dx"):
             parts = [dx_part(h, norm_stat) for h in range(H)]
             gain_dx(parts)
@@ -712,15 +879,11 @@
             g_last("d")
         with scope("d_glu"):
             g_last("u")
-        wait_sent(0)
+        with scope("d_end"):
+            finish()
+            wait_sent(0)
         ctx[0] = None
 
-    for k in range(1, NF):
-        arrived(gain_in, (lax.rem(f + NF - k, NF),), ("gain", k - 1))
-    gsum = gain_in[0]
-    for k in range(1, NF):
-        gsum = gsum + gain_in[k]
-    gn_ref[...] = gsum
     wait_sent(None)
     assert size[0] <= NSEM, size[0]
 
@@ -728,30 +891,38 @@
 def body(saved_inputs, top_grad, norm_gain, gate_weight, up_weight, down_weight):
     x = saved_inputs.reshape(T, W)
     tg = top_grad.reshape(T, W)
-    gain = lax.dynamic_slice_in_dim(norm_gain[0], lax.axis_index("tp") * W, W)
-    gain = jnp.broadcast_to(gain[:, None], (W, 128))
-    vm = pl.BlockSpec(memory_space=pltpu.VMEM)
+    hbm = pl.BlockSpec(memory_space=pl.ANY)
+    outs = (
+        jax.ShapeDtypeStruct((T, W), BF16),
+        jax.ShapeDtypeStruct((PW, FL), F32),
+        jax.ShapeDtypeStruct((PW, FL), F32),
+        jax.ShapeDtypeStruct((PW, FL), F32),
+        jax.ShapeDtypeStruct((1, W), F32),
+    )
     out = pl.pallas_call(
         fused_kernel,
         name="fused",
-        out_shape=(
-            jax.ShapeDtypeStruct((T, W), BF16),
-            jax.ShapeDtypeStruct((PW, FL), F32),
-            jax.ShapeDtypeStruct((PW, FL), F32),
-            jax.ShapeDtypeStruct((FL, PW), F32),
-            jax.ShapeDtypeStruct((8, W), F32),
-        ),
-        in_specs=[vm] * 6,
-        out_specs=[vm] * 5,
+        out_shape=outs,
+        in_specs=[hbm] * 6,
+        out_specs=[hbm] * 5,
         scratch_shapes=[
-            pltpu.VMEM((NF, PW, GU), BF16),
-            pltpu.VMEM((NF, FL, PW), BF16),
+            pltpu.VMEM((T, W), BF16),
+            pltpu.VMEM((T, W), BF16),
+            pltpu.VMEM((1, D), F32),
+            pltpu.VMEM((PW, FL), BF16),
+            pltpu.VMEM((PW, FL), BF16),
+            pltpu.VMEM((PW, FL), BF16),
+            *[pltpu.VMEM(o.shape, o.dtype) for o in outs],
+            pltpu.VMEM((W, 128), F32),
+            pltpu.VMEM((NF, PW, UW), BF16),
+            pltpu.VMEM((NF, DR, DH), BF16),
             pltpu.VMEM((NZ, NXL, W, T), BF16),
             pltpu.VMEM((NZ, NXL, H, W, TH), BF16),
-            pltpu.VMEM((GU, T), F32),
-            pltpu.VMEM((FL, T), F32),
-            pltpu.VMEM((GU, T), BF16),
+            pltpu.VMEM((UW, T), F32),
+            pltpu.VMEM((DH + 128 + 16, T), F32),
+            pltpu.VMEM((UW, T), BF16),
             pltpu.VMEM((FL, T), BF16),
+            pltpu.VMEM((128, T), BF16),
             pltpu.VMEM((W, T), F32),
             pltpu.VMEM((1, T), F32),
             pltpu.VMEM((8, T), F32),
@@ -765,28 +936,23 @@
             pltpu.VMEM((H, W, TH), BF16),
             pltpu.VMEM((H, W, TH), BF16),
             pltpu.VMEM((H, W, TH), BF16),
-            pltpu.VMEM((7, PW, GU), BF16),
-            pltpu.VMEM((7, PW, GU), BF16),
-            pltpu.VMEM((5, PW, GU), F32),
-            pltpu.VMEM((7, FL, PW), BF16),
-            pltpu.VMEM((7, FL, PW), BF16),
-            pltpu.VMEM((5, FL, PW), F32),
+            pltpu.VMEM((7, PW, UW), BF16),
+            pltpu.VMEM((7, PW, UW), BF16),
+            pltpu.VMEM((5, PW, UW), F32),
+            pltpu.VMEM((7, DR, DH), BF16),
+            pltpu.VMEM((7, DR, DH), BF16),
+            pltpu.VMEM((5, DR, DH), F32),
             pltpu.SemaphoreType.DMA((NSEM,)),
             pltpu.SemaphoreType.DMA((NSEM,)),
+            pltpu.SemaphoreType.DMA((16,)),
             pltpu.SemaphoreType.REGULAR,
         ],
         compiler_params=pltpu.CompilerParams(
-            collective_id=0, has_side_effects=True, vmem_limit_bytes=62 * 2**20
+            collective_id=0, has_side_effects=True, vmem_limit_bytes=58 * 2**20
         ),
-    )(x, tg, gain, gate_weight[0], up_weight[0], down_weight[0])
+    )(x, tg, norm_gain, gate_weight[0], up_weight[0], down_weight[0].T)
     dx, gg, ug, dg, gn = out
-    return (
-        dx.reshape(1, MICRO, ROWS, W),
-        gg[None],
-        ug[None],
-        dg[None],
-        gn[0:1],
-    )
+    return (dx.reshape(1, MICRO, ROWS, W), gg[None], ug[None], dg.T[None], gn)
 
 
 def solution(mesh):

time: 168 us -> 144 us (0.86)
  Pallas kernels: 156 us -> 137 us
  local copies, waits for them, and re-layouts: 9.76 us -> 6.43 us
    pallas_call x1, Pallas kernels: 156 us -> 137 us  [body(): pl.pallas_call(fused_kernel, name='fused', out_shape=outs, in_specs=[hbm]...]
    unnamed x13 -> x11, local copies, waits for them, and re-layouts: 7.7 us -> 6.43 us
where the time goes in v3:
time: 144 us
  Pallas kernels  137 us (95%)
  local copies, waits for them, and re-layouts  6.43 us (4%)
    pallas_call x1, Pallas kernels, body(): pl.pallas_call(fused_kernel, name='fused', out_shape=outs, in_specs=[hbm]...  137 us
    unnamed x11, local copies, waits for them, and re-layouts  6.43 us

profile of v3, /device:TPU:2, one launch (start us, length us, event | category | flops | bytes accessed | tf_op | source)
XLA Modules:
  0.0 143.7 jit_solution(9306878469594232228)
XLA Ops:
  0.6 136.6 %fused.1 = (bf16[512,160]{1,0:T(8,128)(2,1)}, f32[320,432]{1,0:T(8,128)}, f32[320,432]{1,0:T(8,128)}, f32[320,432]{1,0:T(8,128)}, f32[1,160]{1,0:T(1,128)}) custom-call(bf16[512,160]{1,0:T(8,128)(2,1)} %bitcast.20, bf16[512,160]{1,0:T(8,128)(2,1)} %bitcast.21, f32[1,2560]{1,0:T(1,128)} %gain_hbm.1, bf16[320,432]{1,0:T(8,128)(2,1)} %bitcast.16, ...), custom_call_target="tpu_custom_call" | custom-call | tf_op jit(solution)/shard_map/fused/pallas_call | solution.py:902
  137.3 1.7 %copy.16 = bf16[1,8,64,160]{3,2,1,0:T(8,128)(2,1)} copy(bf16[1,8,64,160]{3,2,1,0:T(8,128)(2,1)} %bitcast.19) | data formatting | bytes 327680
  138.9 0.0 copy-start.1
  138.9 2.0 %copy.17 = f32[1,320,432]{2,1,0:T(8,128)} copy(f32[1,320,432]{2,1,0:T(8,128)} %bitcast.15) | data formatting | bytes 1105920
  141.0 0.0 copy-done.1
  141.0 0.0 copy-start
  141.0 0.8 copy.18
  141.8 0.5 copy-done
  142.3 0.0 copy-start.2
  142.3 0.8 copy.19
  143.1 0.0 copy-done.2
  143.1 0.6 copy.20
Async XLA Ops:
  138.9 2.0 %copy-start.1 = (f32[320,432]{1,0:T(8,128)S(1)}, f32[320,432]{1,0:T(8,128)}, u32[]{:S(2)}) copy-start(f32[320,432]{1,0:T(8,128)} %get-tuple-element.12) | copy-start | bytes 1658884
  141.0 1.3 copy-start
  142.3 0.8 copy-start.2

commit v4 on v3

--- a/solution.py
+++ b/solution.py
@@ -25,7 +25,10 @@
 UW = 896
 DH = 384
 DR = PW + 16
-NSEM = 180
+NCOMMON = 73
+NEACH = 48
+NBIG = 18
+NSMALL = 27
 
 
 def scope(name):
@@ -45,22 +48,17 @@
     wg_hbm,
     wu_hbm,
     wd_hbm,
-    dx_hbm,
-    gg_hbm,
-    ug_hbm,
-    dg_hbm,
-    gn_hbm,
+    dx_ref,
+    gg_ref,
+    ug_ref,
+    dg_ref,
+    gn_ref,
     x_ref,
     tg_ref,
     gain_row,
     wg_ref,
     wu_ref,
     wd_ref,
-    dx_ref,
-    gg_ref,
-    ug_ref,
-    dg_ref,
-    gn_ref,
     gain,
     wgu,
     wd,
@@ -117,6 +115,12 @@
         "xl": (s, f, z * NXL + ol),
         "core": (1 - s, f, t),
     }
+    across = {
+        "core": (1 - s, f, t),
+        "xl": (1 - s, *dev["xl"][1:]),
+        "z+": (1 - s, *dev["z+"][1:]),
+        "z-": (1 - s, *dev["z-"][1:]),
+    }
     tp_peers = [(s, f, lax.rem(t + k, NT)) for k in range(1, NT)]
     fs_peers = [(s, lax.rem(f + k, NF), t) for k in range(1, NF)]
     zblk = [lax.rem(z + k, NZ) for k in range(NZ)]
@@ -125,22 +129,24 @@
     )
 
     ids = {}
-    size = [0]
+    size = {None: 0, 0: 0, 1: 0}
+    private = {"dy": 1, "n": 1, "m": 0, "e": 0}
     ctx = [None]
-    outgoing = {None: {}, 0: {}, 1: {}}
 
     def ident(name, n=1):
         if name not in ids:
-            ids[name] = size[0]
-            size[0] += n
+            sec = private.get(name[0])
+            ids[name] = size[sec] + (0 if sec is None else NCOMMON)
+            size[sec] += n
+            assert size[sec] <= (NCOMMON if sec is None else NEACH), size
         return ids[name]
 
-    def copy(src, dst, m, to):
+    def copy(src, dst, sm, rm, to):
         return pltpu.make_async_remote_copy(
             src_ref=src,
             dst_ref=dst,
-            send_sem=ssem.at[m],
-            recv_sem=rsem.at[m],
+            send_sem=ssem.at[sm],
+            recv_sem=rsem.at[rm],
             device_id=to,
             device_id_type=MESH,
         )
@@ -148,22 +154,38 @@
     def static(idx):
         return tuple(i if isinstance(i, (int, pl.Slice)) else 0 for i in idx)
 
-    def send(src, si, dst, di, name, to, q=None):
-        m = ident(name, 1 if q is None else 2)
-        copy(src.at[si], dst.at[di], m if q is None else m + q, to).start()
-        parts = outgoing[ctx[0]].setdefault(name, [])
-        parts.append((q if isinstance(q, int) else len(parts), src, static(si)))
+    turn = {sec: {"big": 0, "small": 0} for sec in (0, 1)}
+    flying = {0: {}, 1: {}}
+
+    def left_all(kind=None):
+        mine = flying[ctx[0]]
+        for m in sorted(mine):
+            if kind is None or (m < NBIG) == (kind == "big"):
+                src, si = mine.pop(m)
+                r = src.at[si]
+                copy(r, r, m, 0, dev["core"]).wait_send()
+
+    def take(src, si, kind):
+        mine, sec = flying[ctx[0]], ctx[0]
+        base, n = (0, NBIG) if kind == "big" else (NBIG, NSMALL)
+        m = base + turn[sec][kind] % n
+        turn[sec][kind] += 1
+        if m in mine:
+            was, wi = mine.pop(m)
+            r = was.at[wi]
+            copy(r, r, m, 0, dev["core"]).wait_send()
+        mine[m] = (src, static(si))
+        return m
+
+    def send(src, si, dst, di, name, to, q=None, kind="small"):
+        rm = ident(name, 1 if q is None else 2)
+        sm = take(src, si, kind)
+        copy(src.at[si], dst.at[di], sm, rm if q is None else rm + q, to).start()
 
     def arrived(dst, di, name, q=None):
         m = ident(name, 1 if q is None else 2)
         r = dst.at[di]
-        copy(r, r, m if q is None else m + q, dev["core"]).wait_recv()
-
-    def wait_sent(which):
-        for name, parts in outgoing[which].items():
-            for k, src, si in parts:
-                r = src.at[si]
-                copy(r, r, ids[name] + k, dev["core"]).wait_send()
+        copy(r, r, 0, m if q is None else m + q, dev["core"]).wait_recv()
 
     def rows(n, step, fn):
         def body(i, c):
@@ -173,7 +195,8 @@
         lax.fori_loop(0, n // step, body, 0)
 
     barrier = pltpu.get_barrier_semaphore()
-    for to in tp_peers + fs_peers + [dev["core"]]:
+    everyone = tp_peers + fs_peers + list(across.values())
+    for to in everyone:
         pl.semaphore_signal(barrier, inc=1, device_id=to, device_id_type=MESH)
 
     loads = [
@@ -207,18 +230,21 @@
             for h in range(H):
                 dy_all[z, xl, h] = top[:, h * TH : (h + 1) * TH]
 
+    def pack_d():
         loads[3].wait()
 
-        def pack_down(r):
+        def pack(r):
             wd[f, pl.ds(r, 32), :] = wd_ref[pl.ds(r, 32), 0:DH]
             wgu[f, pl.ds(r, 32), GU:UW] = wd_ref[pl.ds(r, 32), DH : DH + 32]
 
-        rows(PW, 32, pack_down)
+        rows(PW, 32, pack)
         last = (
             lax.broadcasted_iota(jnp.int32, (16, FL), 0) + (FL - 16)
             == lax.broadcasted_iota(jnp.int32, (16, FL), 1)
         ).astype(BF16)
         wd[f, PW:DR, 0:PW] = dot(last, wd_ref[...], 1, 1).astype(BF16)
+
+    def pack_u():
         loads[4].wait()
         loads[5].wait()
 
@@ -227,6 +253,8 @@
             wgu[f, pl.ds(r, 32), FL:GU] = wu_ref[pl.ds(r, 32), :]
 
         rows(PW, 32, pack)
+
+    def take_gain():
         loads[2].wait()
 
         def gains(r):
@@ -240,48 +268,70 @@
 
         rows(W, 32, gains)
 
-    with scope("barrier"):
-        pl.semaphore_wait(barrier, NT - 1 + NF - 1 + 1)
-
-    def spread(buf, name):
-        for k, to in enumerate(tp_peers):
-            send(buf, (t,), buf, (t,), (name, k), to)
-
-    def collect(buf, name):
-        for k in range(1, NT):
-            arrived(buf, (lax.rem(t + NT - k, NT),), (name, k - 1))
+    def spread(buf, me, peers, name):
+        m = ident((name,))
+        for to in peers:
+            copy(buf.at[me], buf.at[me], NBIG + NSMALL + ("ssq", "stat", "gain").index(name), m, to).start()
+
+    def collect(buf, peers, name):
+        n = len(peers)
+        r = buf.at[pl.ds(0, n)]
+        copy(r, r, 0, ident((name,)), dev["core"]).wait_recv()
         total = buf[0]
-        for k in range(1, NT):
+        for k in range(1, n + 1):
             total = total + buf[k]
         return total
 
-    spread(ssq_in, "ssq")
+    def spread_left(buf, peers, name):
+        r = buf.at[pl.ds(0, len(peers))]
+        copy(r, r, NBIG + NSMALL + ("ssq", "stat", "gain").index(name), 0, dev["core"]).wait_send()
+
+    with scope("pack"):
+        pack_d()
+        pack_u()
+
+    with scope("barrier"):
+        pl.semaphore_wait(barrier, len(everyone))
+    spread(ssq_in, t, tp_peers, "ssq")
 
     halves = {"u": ((0, 160), (160, 160)), "d": ((0, 160), (160, 176))}
     full = {"u": wgu, "d": wd}
 
     def w_own(a, dirs):
         for d in dirs:
-            send(full[a], (f,), full[a], (f,), ("w", a, "own", d), dev[d])
+            send(full[a], (f,), full[a], (f,), ("w", a, "own", d), dev[d], kind="big")
 
     def w_fwd(a):
         arr = full[a]
         for d, blk, k in (("y+", left["c"], 0), ("y-", right["c"], 1)):
             arrived(arr, (blk,), ("w", a, "own", d))
             part = pl.ds(*halves[a][k])
-            send(arr, (blk, part), arr, (blk, part), ("w", a, "fwd", d), dev[d])
+            send(arr, (blk, part), arr, (blk, part), ("w", a, "fwd", d), dev[d], kind="big")
 
     def w_pass(a):
         arr, blk = full[a], own["o"]
         arrived(arr, (blk,), ("w", a, "own", "xh"))
         for d in ("y+", "y-"):
-            send(arr, (blk,), arr, (blk,), ("w", a, "pass", d), dev[d])
+            send(arr, (blk,), arr, (blk,), ("w", a, "pass", d), dev[d], kind="big")
 
     def w_far(a):
         arr, blk = full[a], far["c"]
         for d, k in (("y+", 0), ("y-", 1)):
             arrived(arr, (blk, pl.ds(*halves[a][k])), ("w", a, "fwd", d))
-        send(arr, (blk,), arr, (blk,), ("w", a, "far"), dev["xh"])
+        send(arr, (blk,), arr, (blk,), ("w", a, "far"), dev["xh"], kind="big")
+
+    def w_fwd_o(a):
+        arr = full[a]
+        for d, blk, k in (("y+", left["o"], 0), ("y-", right["o"], 1)):
+            arrived(arr, (blk,), ("w", a, "pass", d))
+            part = pl.ds(*halves[a][k])
+            send(arr, (blk, part), arr, (blk, part), ("w", a, "fwdo", d), dev[d], kind="big")
+
+    def w_last_y(a):
+        arr = full[a]
+        for blk, nm in ((far["c"], "fwd"), (far["o"], "fwdo")):
+            for d, k in (("y+", 0), ("y-", 1)):
+                arrived(arr, (blk, pl.ds(*halves[a][k])), ("w", a, nm, d))
 
     def w_last(a):
         arr = full[a]
@@ -324,7 +374,6 @@
     def agz_own(buf, nm):
         for d in ("z+", "z-"):
             send(buf, (z, xl), buf, (z, xl), (nm, d, 1), dev[d])
-        agz_pair(buf, nm, 0, z)
 
     def agz_fwd(buf, nm, k):
         for d, blk in (("z+", zblk[NZ - k]), ("z-", zblk[k])):
@@ -357,8 +406,14 @@
     def together(parts):
         return jnp.concatenate(parts, axis=0)
 
-    def forward(g):
-        blks = [zblk[k] for k in groups[g]]
+    z_groups = [[zblk[k] for k in g] for g in groups]
+    w_groups = [
+        [own["c"], left["c"], right["c"], own["o"], left["o"], right["o"]],
+        [far["c"], far["o"]],
+    ]
+
+    def forward(g, blocks=z_groups):
+        blks = blocks[g]
         part = dot(
             together([wgu[b] for b in blks]),
             together([n_all[b].reshape(PW, T) for b in blks]),
@@ -396,7 +451,7 @@
         dgu[GU:UW, :] = jnp.zeros((UW - GU, T), BF16)
 
     def normalize():
-        row_scale = lax.rsqrt(collect(ssq_in, "ssq") / D + EPS)
+        row_scale = lax.rsqrt(collect(ssq_in, tp_peers, "ssq") / D + EPS)
         scale[...] = row_scale
         u = unit[...] * row_scale
         unit[...] = u
@@ -409,6 +464,7 @@
             ag_own(dy_all, "dy")
             w_own("d", ("y+", "y-", "xh"))
             w_own("u", ("y+", "y-"))
+            take_gain()
         with scope("a_norm"):
             normalize()
         with scope("a_nO"):
@@ -448,13 +504,14 @@
         with scope("a_n3"):
             ag_fwd3(n_all, "n")
             pl.semaphore_signal(go, inc=1, device_id=dev["core"], device_id_type=MESH)
+        with scope("a_dy3"):
+            ag_fwd3(dy_all, "dy")
+            pl.semaphore_signal(go, inc=1, device_id=dev["core"], device_id_type=MESH)
         with scope("a_wl"):
             w_last("d")
             w_last("u")
         with scope("a_h0"):
             dhidden(0)
-        with scope("a_dy3"):
-            ag_fwd3(dy_all, "dy")
         with scope("a_f0"):
             forward(0)
         with scope("a_f1"):
@@ -475,50 +532,49 @@
     @pl.when(s == 0)
     def _():
         ctx[0] = 0
+        with scope("b_gain"):
+            take_gain()
         with scope("b_norm"):
             normalize()
         with scope("b_go"):
             pl.semaphore_wait(go, 1)
         with scope("b_own"):
-            agz_own(n_all, "n")
+            agz_pair(n_all, "m", 0, z)
             w_own("d", ("y+", "y-", "xh"))
             w_own("u", ("y+", "y-", "xh"))
-        with scope("b_n1"):
-            agz_fwd(n_all, "n", 1)
+        with scope("b_go2"):
+            pl.semaphore_wait(go, 1)
+            agz_own(n_all, "m")
         with scope("b_wfd"):
             w_fwd("d")
-        with scope("b_n2"):
-            agz_fwd(n_all, "n", 2)
+            w_pass("d")
+        with scope("b_n1"):
+            agz_fwd(n_all, "m", 1)
         with scope("b_wfu"):
             w_fwd("u")
-            w_pass("d")
-        with scope("b_wxd"):
-            w_far("d")
+        with scope("b_n2"):
+            agz_fwd(n_all, "m", 2)
         with scope("b_wpu"):
             w_pass("u")
         with scope("b_n3"):
-            agz_fwd(n_all, "n", 3)
-        with scope("b_wxu"):
-            w_far("u")
+            agz_fwd(n_all, "m", 3)
+        with scope("b_wod"):
+            w_fwd_o("d")
         with scope("b_n4"):
-            agz_far(n_all, "n")
+            agz_far(n_all, "m")
+        with scope("b_wou"):
+            w_fwd_o("u")
         with scope("b_nl"):
-            agz_last(n_all, "n")
+            agz_last(n_all, "m")
+        with scope("b_f0"):
+            forward(0, w_groups)
         with scope("b_wl"):
-            w_last("d")
-            w_last("u")
-        with scope("b_f0"):
-            forward(0)
+            w_last_y("d")
+            w_last_y("u")
         with scope("b_f1"):
-            forward(1)
-        with scope("b_f2"):
-            forward(2)
+            forward(1, w_groups)
         with scope("b_hid"):
             hidden()
-        with scope("b_core"):
-            for h in range(H):
-                arrived(dy_all, (z, xl, h), ("core", h))
-                ag_own(dy_all, "e", (h,))
         with scope("b_dyp"):
             for h in range(H):
                 ag_partner(dy_all, "e", (h,))
@@ -531,6 +587,8 @@
                 for j in range(2):
                     ag_fwd(dy_all, "e", 2, j, (h,))
         with scope("b_h0"):
+            for h in range(H):
+                arrived(dy_all, (z, xl, h), ("e", "core", h))
             dhidden(0)
         with scope("b_dy3"):
             for h in range(H):
@@ -562,7 +620,7 @@
 
         rows(FL, 16, elementwise)
         stat_in[t] = jnp.sum(stat[...], axis=0, keepdims=True)
-        spread(stat_in, "stat")
+        spread(stat_in, t, tp_peers, "stat")
 
     ways = (("z+", 0), ("z-", 1))
 
@@ -645,23 +703,14 @@
         dxs[h] = dx.astype(BF16)
         return d_normed * u
 
-    stores = []
-
-    def store(src, dst):
-        c = pltpu.make_async_copy(src, dst, lsem.at[6 + len(stores)])
-        c.start()
-        stores.append(c)
-
     def gain_dx(parts):
         total = dot(
             jnp.ones((8, T), F32), jnp.concatenate(parts, axis=1), 1, 1, lax.Precision.HIGHEST
         )
         gain_in[f] = total
-        for k, to in enumerate(fs_peers):
-            send(gain_in, (f,), gain_in, (f,), ("gain", k), to)
+        spread(gain_in, f, fs_peers, "gain")
         for h in range(H):
             dx_ref[h * TH : (h + 1) * TH, :] = dot(dxs[h], eye, 0, 0).astype(BF16)
-        store(dx_ref, dx_hbm)
 
     sg, rg, fg = {"u": sgu, "d": sgd}, {"u": rgu, "d": rgd}, {"u": fgu, "d": fgd}
     size_of = {"u": (PW, 32), "d": (DR, 48)}
@@ -679,23 +728,26 @@
             dst[i, PW:DR, 0:PW] = dot(hid[FL - 16 : FL, :], dy, 1, 1).astype(dst.dtype)
 
     direct = [far["o"], right["o"], left["o"]]
-    kept = [far["c"], right["c"], left["c"], own["o"], own["c"]]
+    kept = [far["c"], own["o"], right["c"], left["c"], own["c"]]
 
     def g_first(a):
+        rm = ident(("g", a, 0), 3)
+        sm = [take(sg[a], (0,), "big") for _ in range(3)]
+
         def body(i, c):
             wgrad(a, pick(i, direct), sg[a], i)
+            to = pick(i, [dev[d][1] for d in ("xh", "y+", "y-")])
+            copy(sg[a].at[i], rg[a].at[i], pick(i, sm), rm + i, (s, to, t)).start()
             return c
 
         lax.fori_loop(0, 3, body, 0)
-        for i, d in enumerate(("xh", "y+", "y-")):
-            send(sg[a], (i,), rg[a], (i,), ("g", a, i), dev[d])
-
-    def g_kept(a):
+
+    def g_kept(a, lo, hi):
         def body(i, c):
             wgrad(a, pick(i, kept), fg[a], i)
             return c
 
-        lax.fori_loop(0, 5, body, 0)
+        lax.fori_loop(lo, hi, body, 0)
 
     def g_sum(a, slot, own_i, recv, span=None):
         n, st = size_of[a]
@@ -712,25 +764,25 @@
         rows(n, st, body)
 
     def g_far(a):
-        arrived(rg[a], (0,), ("g", a, 0))
+        arrived(rg[a], (0,), ("g", a, 0), q=0)
         g_sum(a, 3, 0, (0,))
         for d, k in (("y+", 0), ("y-", 1)):
             part = pl.ds(*halves[a][k])
-            send(sg[a], (3, part), rg[a], (3, part), ("g", a, 3, d), dev[d])
+            send(sg[a], (3, part), rg[a], (3, part), ("g", a, 3, d), dev[d], kind="big")
 
     def g_near(a):
         for d, k, slot in (("y+", 0, 4), ("y-", 1, 5)):
             part = pl.ds(*halves[a][k])
             arrived(rg[a], (3, part), ("g", a, 3, d))
-            g_sum(a, slot, 1 + k, (3,), halves[a][k])
-            g_sum(a, slot, 1 + k, (), halves[a][1 - k])
-            send(sg[a], (slot,), rg[a], (slot,), ("g", a, slot), dev[d])
+            g_sum(a, slot, 2 + k, (3,), halves[a][k])
+            g_sum(a, slot, 2 + k, (), halves[a][1 - k])
+            send(sg[a], (slot,), rg[a], (slot,), ("g", a, slot), dev[d], kind="big")
 
     def g_partner(a):
-        arrived(rg[a], (1,), ("g", a, 1))
-        arrived(rg[a], (2,), ("g", a, 2))
-        g_sum(a, 6, 3, (1, 2))
-        send(sg[a], (6,), rg[a], (6,), ("g", a, 6), dev["xh"])
+        arrived(rg[a], (1,), ("g", a, 0), q=1)
+        arrived(rg[a], (2,), ("g", a, 0), q=2)
+        g_sum(a, 6, 1, (1, 2))
+        send(sg[a], (6,), rg[a], (6,), ("g", a, 6), dev["xh"], kind="big")
 
     def g_last(a):
         for k in (4, 5, 6):
@@ -767,20 +819,10 @@
 
             rows(160, 32, part)
             at = pl.ds(c * 160, 160)
-            for v_ref, hbm in ((gg_ref, gg_hbm), (ug_ref, ug_hbm), (dg_ref, dg_hbm)):
-                store(v_ref.at[at], hbm.at[at])
 
     def finish():
-        for k in range(1, NF):
-            arrived(gain_in, (lax.rem(f + NF - k, NF),), ("gain", k - 1))
-        gsum = gain_in[0]
-        for k in range(1, NF):
-            gsum = gsum + gain_in[k]
-        gn_ref[...] = gsum[0:1]
-        store(gn_ref, gn_hbm)
-        for c in stores:
-            c.wait()
-        del stores[:]
+        gn_ref[...] = collect(gain_in, fs_peers, "gain")[0:1]
+        left_all()
 
     @pl.when(s == 1)
     def _():
@@ -800,39 +842,44 @@
         with scope("c_rl"):
             rs_last()
         with scope("c_stat"):
-            norm_stat = collect(stat_in, "stat") / D
+            norm_stat = collect(stat_in, tp_peers, "stat") / D
         with scope("c_dx"):
             parts = []
             for h in range(H):
                 parts.append(dx_part(h, norm_stat))
-                send(dxs, (h,), dy_all, (z, xl, h), ("core", h), dev["core"])
+                for d, name in (("xl", ("xl", h)), ("z+", ("z+", 1, 0, h)), ("z-", ("z-", 1, 0, h)), ("core", ("core", h))):
+                    send(dxs, (h,), dy_all, (z, xl, h), ("e", *name), across[d])
         with scope("c_g1"):
+            left_all("big")
+            g_first("u")
             g_first("d")
-            g_first("u")
         with scope("c_gain"):
             gain_dx(parts)
-        with scope("c_gk"):
-            g_kept("d")
-            g_kept("u")
+        with scope("c_gk1"):
+            g_kept("u", 0, 1)
+            g_kept("d", 0, 1)
+        with scope("c_gk2"):
+            g_kept("u", 1, 5)
+        with scope("c_gfu"):
+            g_far("u")
+        with scope("c_gpu"):
+            g_partner("u")
+        with scope("c_gk3"):
+            g_kept("d", 1, 5)
         with scope("c_gfd"):
             g_far("d")
         with scope("c_gpd"):
             g_partner("d")
-        with scope("c_gfu"):
-            g_far("u")
+        with scope("c_gnu"):
+            g_near("u")
         with scope("c_gnd"):
             g_near("d")
-        with scope("c_gpu"):
-            g_partner("u")
-        with scope("c_gnu"):
-            g_near("u")
+        with scope("c_glu"):
+            g_last("u")
         with scope("c_gld"):
             g_last("d")
-        with scope("c_glu"):
-            g_last("u")
         with scope("c_end"):
             finish()
-            wait_sent(1)
         ctx[0] = None
 
     @pl.when(s == 0)
@@ -841,51 +888,69 @@
         with scope("d_r1"):
             rs_first()
         with scope("d_g1"):
+            left_all("big")
+            g_first("u")
             g_first("d")
-            g_first("u")
+        with scope("d_rc2"):
+            rs_compute(2)
         with scope("d_r2"):
-            rs_compute(2)
             rs_step(2)
-        with scope("d_gkd"):
-            g_kept("d")
+        with scope("d_gk1"):
+            g_kept("u", 0, 2)
+            g_kept("d", 0, 2)
+        with scope("d_rc3"):
+            rs_compute(3)
+        with scope("d_gfu"):
+            g_far("u")
+        with scope("d_gpu"):
+            g_partner("u")
         with scope("d_r3"):
-            rs_compute(3)
             rs_step(3)
-        with scope("d_gku"):
-            g_kept("u")
         with scope("d_gfd"):
             g_far("d")
-        with scope("d_r4"):
-            rs_compute(4)
-            rs_step(4)
-        with scope("d_gfu"):
-            g_far("u")
         with scope("d_gpd"):
             g_partner("d")
+        with scope("d_gk2"):
+            g_kept("u", 2, 4)
+        with scope("d_rc4"):
+            rs_compute(4)
+        with scope("d_gnu"):
+            g_near("u")
+        with scope("d_r4"):
+            rs_step(4)
+        with scope("d_gk3"):
+            g_kept("d", 2, 4)
         with scope("d_gnd"):
             g_near("d")
+        with scope("d_gk4"):
+            g_kept("u", 4, 5)
+            g_kept("d", 4, 5)
+            rs_own()
         with scope("d_rl"):
-            rs_own()
             rs_last()
-            norm_stat = collect(stat_in, "stat") / D
-        with scope("d_gpu"):
-            g_partner("u")
-        with scope("d_gnu"):
-            g_near("u")
+            norm_stat = collect(stat_in, tp_peers, "stat") / D
         with scope("d_dx"):
             parts = [dx_part(h, norm_stat) for h in range(H)]
             gain_dx(parts)
+        with scope("d_glu"):
+            g_last("u")
         with scope("d_gld"):
             g_last("d")
-        with scope("d_glu"):
-            g_last("u")
         with scope("d_end"):
             finish()
-            wait_sent(0)
         ctx[0] = None
 
-    wait_sent(None)
-    assert size[0] <= NSEM, size[0]
+    spread_left(ssq_in, tp_peers, "ssq")
+    spread_left(stat_in, tp_peers, "stat")
+    spread_left(gain_in, fs_peers, "gain")
+
+
+def put_kernel(*refs):
+    copies = [pltpu.make_async_copy(refs[k], refs[5 + k], refs[10].at[k]) for k in range(5)]
+    for c in copies:
+        c.start()
+    for c in copies:
+        c.wait()
 
 
 def body(saved_inputs, top_grad, norm_gain, gate_weight, up_weight, down_weight):
@@ -902,9 +967,9 @@
     out = pl.pallas_call(
         fused_kernel,
         name="fused",
-        out_shape=outs,
+        out_shape=[pltpu.VMEM(o.shape, o.dtype) for o in outs],
         in_specs=[hbm] * 6,
-        out_specs=[hbm] * 5,
+        out_specs=[pl.BlockSpec(memory_space=pltpu.VMEM)] * 5,
         scratch_shapes=[
             pltpu.VMEM((T, W), BF16),
             pltpu.VMEM((T, W), BF16),
@@ -912,7 +977,6 @@
             pltpu.VMEM((PW, FL), BF16),
             pltpu.VMEM((PW, FL), BF16),
             pltpu.VMEM((PW, FL), BF16),
-            *[pltpu.VMEM(o.shape, o.dtype) for o in outs],
             pltpu.VMEM((W, 128), F32),
             pltpu.VMEM((NF, PW, UW), BF16),
             pltpu.VMEM((NF, DR, DH), BF16),
@@ -942,16 +1006,23 @@
             pltpu.VMEM((7, DR, DH), BF16),
             pltpu.VMEM((7, DR, DH), BF16),
             pltpu.VMEM((5, DR, DH), F32),
-            pltpu.SemaphoreType.DMA((NSEM,)),
-            pltpu.SemaphoreType.DMA((NSEM,)),
-            pltpu.SemaphoreType.DMA((16,)),
+            pltpu.SemaphoreType.DMA((NBIG + NSMALL + 3,)),
+            pltpu.SemaphoreType.DMA((NCOMMON + NEACH,)),
+            pltpu.SemaphoreType.DMA((6,)),
             pltpu.SemaphoreType.REGULAR,
         ],
         compiler_params=pltpu.CompilerParams(
             collective_id=0, has_side_effects=True, vmem_limit_bytes=58 * 2**20
         ),
     )(x, tg, norm_gain, gate_weight[0], up_weight[0], down_weight[0].T)
-    dx, gg, ug, dg, gn = out
+    dx, gg, ug, dg, gn = pl.pallas_call(
+        put_kernel,
+        name="put",
+        out_shape=outs,
+        in_specs=[pl.BlockSpec(memory_space=pltpu.VMEM)] * 5,
+        out_specs=[hbm] * 5,
+        scratch_shapes=[pltpu.SemaphoreType.DMA((5,))],
+    )(*[pltpu.with_memory_space_constraint(o, pltpu.VMEM) for o in out])
     return (dx.reshape(1, MICRO, ROWS, W), gg[None], ug[None], dg.T[None], gn)
 
 

time: 144 us -> 123 us (0.85)
  Pallas kernels: 137 us -> 122 us
  local copies, waits for them, and re-layouts: 6.43 us -> 0 us
    pallas_call x1 -> x2, Pallas kernels: 137 us -> 122 us  [the longest x1 121 us: body(): pl.pallas_call(fused_kernel, name='fused', out_shape=[pltpu.VMEM(o.shape,...]
    unnamed x11 -> x0, local copies, waits for them, and re-layouts: 6.43 us -> none
where the time goes in v4:
time: 123 us
  Pallas kernels  122 us (99%)
    pallas_call x1, Pallas kernels, body(): pl.pallas_call(fused_kernel, name='fused', out_shape=[pltpu.VMEM(o.shape,...  121 us

profile of v4, /device:TPU:2, one launch (start us, length us, event | category | flops | bytes accessed | tf_op | source)
XLA Modules:
  0.0 123.0 jit_solution(12613676703985756799)
XLA Ops:
  0.6 120.8 %fused.1 = (bf16[512,160]{1,0:T(8,128)(2,1)S(1)}, f32[320,432]{1,0:T(8,128)S(1)}, f32[320,432]{1,0:T(8,128)S(1)}, f32[320,432]{1,0:T(8,128)S(1)}, f32[1,160]{1,0:T(1,128)S(1)}) custom-call(bf16[512,160]{1,0:T(8,128)(2,1)} %bitcast.16, bf16[512,160]{1,0:T(8,128)(2,1)} %bitcast.17, f32[1,2560]{1,0:T(1,128)} %gain_hbm.1, bf16[320,432]{1,0:T(8,128)(2,1)} %bitcast.13, ...), custom_call_target="tpu_custom_call" | custom-call | tf_op jit(solution)/shard_map/fused/pallas_call | solution.py:967
  121.4 1.4 %put.1 = (bf16[512,160]{1,0:T(8,128)(2,1)}, f32[320,432]{1,0:T(8,128)}, f32[320,432]{1,0:T(8,128)}, f32[320,432]{1,0:T(8,128)}, f32[1,160]{1,0:T(1,128)}) custom-call(bf16[512,160]{1,0:T(8,128)(2,1)S(1)} %get-tuple-element.15.refs_0_, f32[320,432]{1,0:T(8,128)S(1)} %get-tuple-element.16.refs_1_, f32[320,432]{1,0:T(8,128)S(1)} %get-tuple-element.17.refs_2_, ...), custom_call_target="tpu_custom_call" | custom-call | tf_op jit(solution)/shard_map/put/pallas_call | solution.py:1018

commit v5 on v4

--- a/solution.py
+++ b/solution.py
@@ -25,14 +25,10 @@
 UW = 896
 DH = 384
 DR = PW + 16
-NCOMMON = 73
+NCOMMON = 77
 NEACH = 48
-NBIG = 18
+NBIG = 20
 NSMALL = 27
-
-
-def scope(name):
-    return jax.named_scope(name)
 
 
 def dot(a, b, ca, cb, precision=None):
@@ -214,21 +210,20 @@
     ]
     for c in loads:
         c.start()
-    with scope("prep"):
-        eye = (
-            lax.broadcasted_iota(jnp.int32, (W, W), 0) == lax.broadcasted_iota(jnp.int32, (W, W), 1)
-        ).astype(BF16)
-        loads[0].wait()
-        xt = dot(eye, x_ref[...], 1, 1)
-        ssq_in[t] = jnp.sum(xt * xt, axis=0, keepdims=True)
-        unit[...] = xt
-        loads[1].wait()
-
-        @pl.when(s == 1)
-        def _():
-            top = dot(eye, tg_ref[...], 1, 1).astype(BF16)
-            for h in range(H):
-                dy_all[z, xl, h] = top[:, h * TH : (h + 1) * TH]
+    eye = (
+        lax.broadcasted_iota(jnp.int32, (W, W), 0) == lax.broadcasted_iota(jnp.int32, (W, W), 1)
+    ).astype(BF16)
+    loads[0].wait()
+    xt = dot(eye, x_ref[...], 1, 1)
+    ssq_in[t] = jnp.sum(xt * xt, axis=0, keepdims=True)
+    unit[...] = xt
+    loads[1].wait()
+
+    @pl.when(s == 1)
+    def _():
+        top = dot(eye, tg_ref[...], 1, 1).astype(BF16)
+        for h in range(H):
+            dy_all[z, xl, h] = top[:, h * TH : (h + 1) * TH]
 
     def pack_d():
         loads[3].wait()
@@ -286,12 +281,10 @@
         r = buf.at[pl.ds(0, len(peers))]
         copy(r, r, NBIG + NSMALL + ("ssq", "stat", "gain").index(name), 0, dev["core"]).wait_send()
 
-    with scope("pack"):
-        pack_d()
-        pack_u()
-
-    with scope("barrier"):
-        pl.semaphore_wait(barrier, len(everyone))
+    pack_d()
+    pack_u()
+
+    pl.semaphore_wait(barrier, len(everyone))
     spread(ssq_in, t, tp_peers, "ssq")
 
     halves = {"u": ((0, 160), (160, 160)), "d": ((0, 160), (160, 176))}
@@ -339,11 +332,16 @@
         arrived(arr, (right["o"],), ("w", a, "pass", "y-"))
         arrived(arr, (far["o"],), ("w", a, "far"))
 
-    def ag_own(buf, nm, hh=()):
-        own_at = (z, xl, *hh)
-        send(buf, own_at, buf, own_at, (nm, "xl", *hh), dev["xl"])
-        send(buf, own_at, buf, own_at, (nm, "z+", 1, 0, *hh), dev["z+"])
-        send(buf, own_at, buf, own_at, (nm, "z-", 1, 0, *hh), dev["z-"])
+    def ag_xl(buf, nm):
+        send(buf, (z, xl), buf, (z, xl), (nm, "xl"), dev["xl"])
+
+    def ag_z(buf, nm):
+        for d in ("z+", "z-"):
+            send(buf, (z, xl), buf, (z, xl), (nm, d, 1, 0), dev[d])
+
+    def ag_own(buf, nm):
+        ag_xl(buf, nm)
+        ag_z(buf, nm)
 
     def ag_partner(buf, nm, hh=()):
         at = (z, ol, *hh)
@@ -368,30 +366,6 @@
         arrived(buf, (zblk[4], 0, *hh), (nm, "z+", 4, *hh))
         arrived(buf, (zblk[4], 1, *hh), (nm, "z-", 4, *hh))
 
-    def agz_pair(buf, nm, k, blk):
-        send(buf, (blk, xl), buf, (blk, xl), (nm, "pair", k), dev["xl"])
-
-    def agz_own(buf, nm):
-        for d in ("z+", "z-"):
-            send(buf, (z, xl), buf, (z, xl), (nm, d, 1), dev[d])
-
-    def agz_fwd(buf, nm, k):
-        for d, blk in (("z+", zblk[NZ - k]), ("z-", zblk[k])):
-            arrived(buf, (blk, xl), (nm, d, k))
-            part = () if k < 3 else (pl.ds(0, 80),) if d == "z+" else (pl.ds(80, 80),)
-            send(buf, (blk, xl, *part), buf, (blk, xl, *part), (nm, d, k + 1), dev[d])
-        agz_pair(buf, nm, NZ - k, zblk[NZ - k])
-        agz_pair(buf, nm, k, zblk[k])
-
-    def agz_far(buf, nm):
-        for d, lo in (("z+", 0), ("z-", 80)):
-            arrived(buf, (zblk[4], xl, pl.ds(lo, 80)), (nm, d, 4))
-        agz_pair(buf, nm, 4, zblk[4])
-
-    def agz_last(buf, nm):
-        for k in range(NZ):
-            arrived(buf, (zblk[k], ol), (nm, "pair", k))
-
     def act(buf, i):
         return jnp.concatenate([buf[i, :, h].reshape(PW, TH) for h in range(H)], axis=1)
 
@@ -401,29 +375,21 @@
             v = jnp.where(i == k, table[k], v)
         return v
 
-    groups = ((0, 1, 7), (2, 6), (3, 5, 4))
-
     def together(parts):
         return jnp.concatenate(parts, axis=0)
 
-    z_groups = [[zblk[k] for k in g] for g in groups]
-    w_groups = [
-        [own["c"], left["c"], right["c"], own["o"], left["o"], right["o"]],
-        [far["c"], far["o"]],
-    ]
-
-    def forward(g, blocks=z_groups):
-        blks = blocks[g]
+    def forward(*ks):
+        blks = [zblk[k] for k in ks]
         part = dot(
             together([wgu[b] for b in blks]),
             together([n_all[b].reshape(PW, T) for b in blks]),
             0,
             0,
         )
-        gu[...] = part if g == 0 else gu[...] + part
-
-    def dhidden(g):
-        blks = [zblk[k] for k in groups[g]]
+        gu[...] = part if 0 in ks else gu[...] + part
+
+    def dhidden(*ks):
+        blks = [zblk[k] for k in ks]
         dys = [act(dy_all, b) for b in blks]
         dy = together(dys)
         parts = (
@@ -432,12 +398,12 @@
         )
         for r, part in parts:
             at = pl.ds(r, part.shape[0])
-            dh[at, :] = part if g == 0 else dh[at, :] + part
+            dh[at, :] = part if 0 in ks else dh[at, :] + part
         part = dot(wd[blks[0], PW:DR, 0:PW], dys[0], 1, 0)
         for b, d in zip(blks[1:], dys[1:]):
             part = part + dot(wd[b, PW:DR, 0:PW], d, 1, 0)
         at = pl.ds(DH + 128, 16)
-        dh[at, :] = part if g == 0 else dh[at, :] + part
+        dh[at, :] = part if 0 in ks else dh[at, :] + part
 
     def hidden():
         def body(r):
@@ -448,7 +414,6 @@
         rows(FL, 16, body)
         hid_mid[0:96, :] = jnp.zeros((96, T), BF16)
         hid_mid[96:128, :] = hid[DH : DH + 32, :]
-        dgu[GU:UW, :] = jnp.zeros((UW - GU, T), BF16)
 
     def normalize():
         row_scale = lax.rsqrt(collect(ssq_in, tp_peers, "ssq") / D + EPS)
@@ -457,153 +422,9 @@
         unit[...] = u
         n_all[z, xl] = (u * gain[:, 0:1]).astype(BF16)
 
-    @pl.when(s == 1)
-    def _():
-        ctx[0] = 1
-        with scope("a_own"):
-            ag_own(dy_all, "dy")
-            w_own("d", ("y+", "y-", "xh"))
-            w_own("u", ("y+", "y-"))
-            take_gain()
-        with scope("a_norm"):
-            normalize()
-        with scope("a_nO"):
-            ag_own(n_all, "n")
-            w_own("u", ("xh",))
-        with scope("a_dyP"):
-            ag_partner(dy_all, "dy")
-        with scope("a_dy10"):
-            ag_fwd(dy_all, "dy", 1, 0)
-        with scope("a_wfd"):
-            w_fwd("d")
-        with scope("a_nP"):
-            ag_partner(n_all, "n")
-        with scope("a_n10"):
-            ag_fwd(n_all, "n", 1, 0)
-        with scope("a_dy11"):
-            ag_fwd(dy_all, "dy", 1, 1)
-        with scope("a_wfu"):
-            w_fwd("u")
-            w_pass("d")
-        with scope("a_n11"):
-            ag_fwd(n_all, "n", 1, 1)
-        with scope("a_wxd"):
-            w_far("d")
-        with scope("a_dy20"):
-            ag_fwd(dy_all, "dy", 2, 0)
-        with scope("a_wpu"):
-            w_pass("u")
-        with scope("a_n20"):
-            ag_fwd(n_all, "n", 2, 0)
-        with scope("a_wxu"):
-            w_far("u")
-        with scope("a_n21"):
-            ag_fwd(n_all, "n", 2, 1)
-        with scope("a_dy21"):
-            ag_fwd(dy_all, "dy", 2, 1)
-        with scope("a_n3"):
-            ag_fwd3(n_all, "n")
-            pl.semaphore_signal(go, inc=1, device_id=dev["core"], device_id_type=MESH)
-        with scope("a_dy3"):
-            ag_fwd3(dy_all, "dy")
-            pl.semaphore_signal(go, inc=1, device_id=dev["core"], device_id_type=MESH)
-        with scope("a_wl"):
-            w_last("d")
-            w_last("u")
-        with scope("a_h0"):
-            dhidden(0)
-        with scope("a_f0"):
-            forward(0)
-        with scope("a_f1"):
-            forward(1)
-        with scope("a_h1"):
-            dhidden(1)
-        with scope("a_nl"):
-            ag_last(n_all, "n")
-        with scope("a_f2"):
-            forward(2)
-            hidden()
-        with scope("a_dyl"):
-            ag_last(dy_all, "dy")
-        with scope("a_h2"):
-            dhidden(2)
-        ctx[0] = None
-
-    @pl.when(s == 0)
-    def _():
-        ctx[0] = 0
-        with scope("b_gain"):
-            take_gain()
-        with scope("b_norm"):
-            normalize()
-        with scope("b_go"):
-            pl.semaphore_wait(go, 1)
-        with scope("b_own"):
-            agz_pair(n_all, "m", 0, z)
-            w_own("d", ("y+", "y-", "xh"))
-            w_own("u", ("y+", "y-", "xh"))
-        with scope("b_go2"):
-            pl.semaphore_wait(go, 1)
-            agz_own(n_all, "m")
-        with scope("b_wfd"):
-            w_fwd("d")
-            w_pass("d")
-        with scope("b_n1"):
-            agz_fwd(n_all, "m", 1)
-        with scope("b_wfu"):
-            w_fwd("u")
-        with scope("b_n2"):
-            agz_fwd(n_all, "m", 2)
-        with scope("b_wpu"):
-            w_pass("u")
-        with scope("b_n3"):
-            agz_fwd(n_all, "m", 3)
-        with scope("b_wod"):
-            w_fwd_o("d")
-        with scope("b_n4"):
-            agz_far(n_all, "m")
-        with scope("b_wou"):
-            w_fwd_o("u")
-        with scope("b_nl"):
-            agz_last(n_all, "m")
-        with scope("b_f0"):
-            forward(0, w_groups)
-        with scope("b_wl"):
-            w_last_y("d")
-            w_last_y("u")
-        with scope("b_f1"):
-            forward(1, w_groups)
-        with scope("b_hid"):
-            hidden()
-        with scope("b_dyp"):
-            for h in range(H):
-                ag_partner(dy_all, "e", (h,))
-        with scope("b_dy1"):
-            for h in range(H):
-                for j in range(2):
-                    ag_fwd(dy_all, "e", 1, j, (h,))
-        with scope("b_dy2"):
-            for h in range(H):
-                for j in range(2):
-                    ag_fwd(dy_all, "e", 2, j, (h,))
-        with scope("b_h0"):
-            for h in range(H):
-                arrived(dy_all, (z, xl, h), ("e", "core", h))
-            dhidden(0)
-        with scope("b_dy3"):
-            for h in range(H):
-                ag_fwd3(dy_all, "e", (h,))
-        with scope("b_h1"):
-            dhidden(1)
-        with scope("b_dyl"):
-            for h in range(H):
-                ag_last(dy_all, "e", (h,))
-        with scope("b_h2"):
-            dhidden(2)
-        ctx[0] = None
-
-    with scope("elem"):
+    def cotangents():
         stat[...] = jnp.zeros_like(stat)
+        dgu[GU:UW, :] = jnp.zeros((UW - GU, T), BF16)
 
         def elementwise(r):
             gate = gu[pl.ds(r, 16), :]
@@ -646,23 +467,18 @@
 
         lax.fori_loop(0, 2, body, 0)
 
-    def rs_step(k):
+    def rs_step(k, hs=range(H)):
         slot = 2 * k - 3
         if k == 2:
-            for h in range(H):
+            for h in hs:
                 for d, w in ways:
                     q = 1 - w
                     pdn[slot + w, h, q] = pf[w, h, q].astype(BF16)
                     send(pdn, (slot + w, h, q), rdn, (w, k - 1, h, q), ("rs", d, k, h), dev[d], q=q)
-        for h in range(H):
-            for j in range(2):
+        for h in hs:
+            for j in range(2 if k > 2 else 1):
                 for d, w in ways:
-                    if k == 2:
-                        q = w
-                        if j:
-                            continue
-                    else:
-                        q = (ol, xl)[j]
+                    q = w if k == 2 else (ol, xl)[j]
                     arrived(rdn, (w, k - 2, h, q), ("rs", d, k - 1, h), q=q)
                     pdn[slot + w, h, q] = (pf[w, h, q] + rdn[w, k - 2, h, q].astype(F32)).astype(BF16)
                     send(pdn, (slot + w, h, q), rdn, (w, k - 1, h, q), ("rs", d, k, h), dev[d], q=q)
@@ -730,9 +546,9 @@
     direct = [far["o"], right["o"], left["o"]]
     kept = [far["c"], own["o"], right["c"], left["c"], own["c"]]
 
-    def g_first(a):
+    def g_first(a, lo=0, hi=3):
         rm = ident(("g", a, 0), 3)
-        sm = [take(sg[a], (0,), "big") for _ in range(3)]
+        sm = [take(sg[a], (0,), "big") if lo <= i < hi else 0 for i in range(3)]
 
         def body(i, c):
             wgrad(a, pick(i, direct), sg[a], i)
@@ -740,7 +556,7 @@
             copy(sg[a].at[i], rg[a].at[i], pick(i, sm), rm + i, (s, to, t)).start()
             return c
 
-        lax.fori_loop(0, 3, body, 0)
+        lax.fori_loop(lo, hi, body, 0)
 
     def g_kept(a, lo, hi):
         def body(i, c):
@@ -770,13 +586,14 @@
             part = pl.ds(*halves[a][k])
             send(sg[a], (3, part), rg[a], (3, part), ("g", a, 3, d), dev[d], kind="big")
 
-    def g_near(a):
+    def g_near(a, waits):
         for d, k, slot in (("y+", 0, 4), ("y-", 1, 5)):
-            part = pl.ds(*halves[a][k])
-            arrived(rg[a], (3, part), ("g", a, 3, d))
-            g_sum(a, slot, 2 + k, (3,), halves[a][k])
-            g_sum(a, slot, 2 + k, (), halves[a][1 - k])
-            send(sg[a], (slot,), rg[a], (slot,), ("g", a, slot), dev[d], kind="big")
+            half = halves[a][k if waits else 1 - k]
+            part = pl.ds(*half)
+            if waits:
+                arrived(rg[a], (3, part), ("g", a, 3, d))
+            g_sum(a, slot, 2 + k, (3,) if waits else (), half)
+            send(sg[a], (slot, part), rg[a], (slot, part), ("g", a, slot, waits), dev[d], kind="big")
 
     def g_partner(a):
         arrived(rg[a], (1,), ("g", a, 0), q=1)
@@ -785,8 +602,11 @@
         send(sg[a], (6,), rg[a], (6,), ("g", a, 6), dev["xh"], kind="big")
 
     def g_last(a):
-        for k in (4, 5, 6):
-            arrived(rg[a], (k,), ("g", a, k))
+        for k in (0, 1):
+            for waits in (False, True):
+                part = pl.ds(*halves[a][k if waits else 1 - k])
+                arrived(rg[a], (4 + k, part), ("g", a, 4 + k, waits))
+        arrived(rg[a], (6,), ("g", a, 6))
 
         def total(at):
             v = fg[a][4, at, :]
@@ -827,117 +647,163 @@
     @pl.when(s == 1)
     def _():
         ctx[0] = 1
-        with scope("c_r1"):
-            rs_first()
-            rs_compute(2)
-        with scope("c_r2"):
-            rs_step(2)
-            rs_compute(3)
-        with scope("c_r3"):
-            rs_step(3)
-            rs_compute(4)
-        with scope("c_r4"):
-            rs_step(4)
-            rs_own()
-        with scope("c_rl"):
-            rs_last()
-        with scope("c_stat"):
-            norm_stat = collect(stat_in, tp_peers, "stat") / D
-        with scope("c_dx"):
-            parts = []
-            for h in range(H):
-                parts.append(dx_part(h, norm_stat))
-                for d, name in (("xl", ("xl", h)), ("z+", ("z+", 1, 0, h)), ("z-", ("z-", 1, 0, h)), ("core", ("core", h))):
-                    send(dxs, (h,), dy_all, (z, xl, h), ("e", *name), across[d])
-        with scope("c_g1"):
-            left_all("big")
-            g_first("u")
-            g_first("d")
-        with scope("c_gain"):
-            gain_dx(parts)
-        with scope("c_gk1"):
-            g_kept("u", 0, 1)
-            g_kept("d", 0, 1)
-        with scope("c_gk2"):
-            g_kept("u", 1, 5)
-        with scope("c_gfu"):
-            g_far("u")
-        with scope("c_gpu"):
-            g_partner("u")
-        with scope("c_gk3"):
-            g_kept("d", 1, 5)
-        with scope("c_gfd"):
-            g_far("d")
-        with scope("c_gpd"):
-            g_partner("d")
-        with scope("c_gnu"):
-            g_near("u")
-        with scope("c_gnd"):
-            g_near("d")
-        with scope("c_glu"):
-            g_last("u")
-        with scope("c_gld"):
-            g_last("d")
-        with scope("c_end"):
-            finish()
+        ag_own(dy_all, "dy")
+        w_own("d", ("y+", "y-", "xh"))
+        w_own("u", ("y+", "y-"))
+        take_gain()
+        normalize()
+        ag_own(n_all, "n")
+        w_own("u", ("xh",))
+        ag_partner(dy_all, "dy")
+        ag_fwd(dy_all, "dy", 1, 0)
+        w_fwd("d")
+        ag_partner(n_all, "n")
+        ag_fwd(n_all, "n", 1, 0)
+        ag_fwd(dy_all, "dy", 1, 1)
+        w_fwd("u")
+        w_pass("d")
+        ag_fwd(n_all, "n", 1, 1)
+        w_far("d")
+        ag_fwd(dy_all, "dy", 2, 0)
+        w_pass("u")
+        ag_fwd(n_all, "n", 2, 0)
+        w_far("u")
+        ag_fwd(n_all, "n", 2, 1)
+        ag_fwd(dy_all, "dy", 2, 1)
+        ag_fwd3(n_all, "n")
+        pl.semaphore_signal(go, inc=1, device_id=dev["core"], device_id_type=MESH)
+        ag_fwd3(dy_all, "dy")
+        w_last("d")
+        w_last("u")
+        dhidden(0, 1, 7)
+        forward(0, 1, 7)
+        forward(2, 6, 3, 5)
+        dhidden(2, 6, 3, 5)
+        ag_last(n_all, "n")
+        forward(4)
+        ag_last(dy_all, "dy")
+        dhidden(4)
+        cotangents()
+        rs_first()
+        rs_compute(2)
+        hidden()
+        rs_step(2)
+        rs_compute(3)
+        rs_step(3)
+        rs_compute(4)
+        rs_step(4)
+        pl.semaphore_signal(go, inc=1, device_id=dev["core"], device_id_type=MESH)
+        rs_own()
+        left_all("big")
+        g_first("u", 1, 3)
+        rs_last()
+        norm_stat = collect(stat_in, tp_peers, "stat") / D
+        parts = []
+        for h in range(H):
+            parts.append(dx_part(h, norm_stat))
+            for d, name in (("xl", ("xl", h)), ("z+", ("z+", 1, 0, h)), ("z-", ("z-", 1, 0, h)), ("core", ("core", h))):
+                send(dxs, (h,), dy_all, (z, xl, h), ("e", *name), across[d])
+        g_first("u", 0, 1)
+        g_kept("u", 2, 4)
+        g_near("u", False)
+        g_first("d")
+        gain_dx(parts)
+        g_kept("u", 0, 2)
+        g_partner("u")
+        g_kept("d", 0, 4)
+        g_far("u")
+        g_far("d")
+        g_partner("d")
+        g_near("d", False)
+        g_kept("u", 4, 5)
+        g_kept("d", 4, 5)
+        g_near("u", True)
+        g_near("d", True)
+        g_last("u")
+        g_last("d")
+        finish()
         ctx[0] = None
 
     @pl.when(s == 0)
     def _():
         ctx[0] = 0
-        with scope("d_r1"):
-            rs_first()
-        with scope("d_g1"):
-            left_all("big")
-            g_first("u")
-            g_first("d")
-        with scope("d_rc2"):
-            rs_compute(2)
-        with scope("d_r2"):
-            rs_step(2)
-        with scope("d_gk1"):
-            g_kept("u", 0, 2)
-            g_kept("d", 0, 2)
-        with scope("d_rc3"):
-            rs_compute(3)
-        with scope("d_gfu"):
-            g_far("u")
-        with scope("d_gpu"):
-            g_partner("u")
-        with scope("d_r3"):
-            rs_step(3)
-        with scope("d_gfd"):
-            g_far("d")
-        with scope("d_gpd"):
-            g_partner("d")
-        with scope("d_gk2"):
-            g_kept("u", 2, 4)
-        with scope("d_rc4"):
-            rs_compute(4)
-        with scope("d_gnu"):
-            g_near("u")
-        with scope("d_r4"):
-            rs_step(4)
-        with scope("d_gk3"):
-            g_kept("d", 2, 4)
-        with scope("d_gnd"):
-            g_near("d")
-        with scope("d_gk4"):
-            g_kept("u", 4, 5)
-            g_kept("d", 4, 5)
-            rs_own()
-        with scope("d_rl"):
-            rs_last()
-            norm_stat = collect(stat_in, tp_peers, "stat") / D
-        with scope("d_dx"):
-            parts = [dx_part(h, norm_stat) for h in range(H)]
-            gain_dx(parts)
-        with scope("d_glu"):
-            g_last("u")
-        with scope("d_gld"):
-            g_last("d")
-        with scope("d_end"):
-            finish()
+        take_gain()
+        normalize()
+        pl.semaphore_wait(go, 1)
+        ag_own(n_all, "m")
+        w_own("d", ("y+", "y-", "xh"))
+        w_own("u", ("y+", "y-", "xh"))
+        ag_partner(n_all, "m")
+        ag_fwd(n_all, "m", 1, 0)
+        w_fwd("d")
+        ag_fwd(n_all, "m", 1, 1)
+        w_fwd("u")
+        w_pass("d")
+        w_far("d")
+        w_pass("u")
+        w_far("u")
+        pl.semaphore_wait(go, 1)
+        ag_fwd(n_all, "m", 2, 0)
+        ag_fwd(n_all, "m", 2, 1)
+        w_last("d")
+        w_last("u")
+        forward(0, 1, 7)
+        for h in range(H):
+            ag_partner(dy_all, "e", (h,))
+        ag_fwd3(n_all, "m")
+        forward(2, 6)
+        for h in range(H):
+            for j in range(2):
+                ag_fwd(dy_all, "e", 1, j, (h,))
+        forward(3, 5)
+        for h in range(H):
+            for j in range(2):
+                ag_fwd(dy_all, "e", 2, j, (h,))
+        ag_last(n_all, "m")
+        forward(4)
+        hidden()
+        for h in range(H):
+            arrived(dy_all, (z, xl, h), ("e", "core", h))
+        dhidden(0, 1, 7)
+        for h in range(H):
+            ag_fwd3(dy_all, "e", (h,))
+        dhidden(2, 6, 3, 5)
+        for h in range(H):
+            ag_last(dy_all, "e", (h,))
+        dhidden(4)
+        cotangents()
+        rs_first()
+        left_all("big")
+        g_first("u")
+        rs_compute(2)
+        rs_step(2)
+        g_kept("u", 2, 4)
+        g_near("u", False)
+        g_first("d")
+        rs_compute(3)
+        rs_step(3, (0,))
+        rs_step(3, (1,))
+        g_kept("u", 0, 2)
+        g_far("u")
+        g_partner("u")
+        rs_compute(4)
+        rs_step(4)
+        g_kept("d", 0, 4)
+        g_far("d")
+        g_near("d", False)
+        rs_own()
+        rs_last()
+        norm_stat = collect(stat_in, tp_peers, "stat") / D
+        g_partner("d")
+        g_kept("u", 4, 5)
+        g_kept("d", 4, 5)
+        g_near("u", True)
+        parts = [dx_part(h, norm_stat) for h in range(H)]
+        gain_dx(parts)
+        g_near("d", True)
+        g_last("u")
+        g_last("d")
+        finish()
         ctx[0] = None
 
     spread_left(ssq_in, tp_peers, "ssq")

time: 123 us -> 117 us (0.951)
  Pallas kernels: 122 us -> 116 us
    pallas_call x1, Pallas kernels: 121 us -> 115 us  [body(): pl.pallas_call(fused_kernel, name='fused', out_shape=[pltpu.VMEM(o.shape,...]
where the time goes in v5:
time: 117 us
  Pallas kernels  116 us (99%)
    pallas_call x1, Pallas kernels, body(): pl.pallas_call(fused_kernel, name='fused', out_shape=[pltpu.VMEM(o.shape,...  115 us

profile of v5, /device:TPU:2, one launch (start us, length us, event | category | flops | bytes accessed | tf_op | source)
XLA Modules:
  0.0 117.0 jit_solution(16599668360043451004)
XLA Ops:
  0.6 114.8 %fused.1 = (bf16[512,160]{1,0:T(8,128)(2,1)S(1)}, f32[320,432]{1,0:T(8,128)S(1)}, f32[320,432]{1,0:T(8,128)S(1)}, f32[320,432]{1,0:T(8,128)S(1)}, f32[1,160]{1,0:T(1,128)S(1)}) custom-call(bf16[512,160]{1,0:T(8,128)(2,1)} %bitcast.16, bf16[512,160]{1,0:T(8,128)(2,1)} %bitcast.17, f32[1,2560]{1,0:T(1,128)} %gain_hbm.1, bf16[320,432]{1,0:T(8,128)(2,1)} %bitcast.13, ...), custom_call_target="tpu_custom_call" | custom-call | tf_op jit(solution)/shard_map/fused/pallas_call | solution.py:833
  115.4 1.4 %put.1 = (bf16[512,160]{1,0:T(8,128)(2,1)}, f32[320,432]{1,0:T(8,128)}, f32[320,432]{1,0:T(8,128)}, f32[320,432]{1,0:T(8,128)}, f32[1,160]{1,0:T(1,128)}) custom-call(bf16[512,160]{1,0:T(8,128)(2,1)S(1)} %get-tuple-element.15.refs_0_, f32[320,432]{1,0:T(8,128)S(1)} %get-tuple-element.16.refs_1_, f32[320,432]{1,0:T(8,128)S(1)} %get-tuple-element.17.refs_2_, ...), custom_call_target="tpu_custom_call" | custom-call | tf_op jit(solution)/shard_map/put/pallas_call | solution.py:884

commit v6 on v5

--- a/solution.py
+++ b/solution.py
@@ -25,7 +25,7 @@
 UW = 896
 DH = 384
 DR = PW + 16
-NCOMMON = 77
+NCOMMON = 79
 NEACH = 48
 NBIG = 20
 NSMALL = 27
@@ -56,6 +56,9 @@
     wu_ref,
     wd_ref,
     gain,
+    gain_sq,
+    gain_all,
+    x_all,
     wgu,
     wd,
     n_all,
@@ -75,6 +78,8 @@
     rdn,
     pf,
     pown,
+    gx,
+    nstat,
     xs,
     xr,
     dxs,
@@ -221,6 +226,7 @@
 
     @pl.when(s == 1)
     def _():
+        x_all[z, xl] = xt.astype(BF16)
         top = dot(eye, tg_ref[...], 1, 1).astype(BF16)
         for h in range(H):
             dy_all[z, xl, h] = top[:, h * TH : (h + 1) * TH]
@@ -251,17 +257,13 @@
 
     def take_gain():
         loads[2].wait()
-
-        def gains(r):
-            mine = lax.broadcasted_iota(jnp.int32, (32, D), 1) == (
-                lax.broadcasted_iota(jnp.int32, (32, D), 0) + (t * W + r)
-            )
-            row = jnp.broadcast_to(gain_row[...], (32, D))
-            gain[pl.ds(r, 32), :] = jnp.broadcast_to(
-                jnp.sum(jnp.where(mine, row, 0.0), axis=1, keepdims=True), (32, 128)
-            )
-
-        rows(W, 32, gains)
+        gain_sq[...] = jnp.zeros_like(gain_sq)
+        for c in range(D // 128):
+            gain_sq[c : c + 1, :] = gain_row[:, c * 128 : (c + 1) * 128]
+        cols = gain_sq[...].T
+        for c in range(D // 128):
+            gain_all[c * 128 : (c + 1) * 128, :] = jnp.broadcast_to(cols[:, c : c + 1], (128, 128))
+        gain[...] = gain_all[pl.ds(pl.multiple_of(t * W, 8), W), :]
 
     def spread(buf, me, peers, name):
         m = ident((name,))
@@ -292,14 +294,20 @@
 
     def w_own(a, dirs):
         for d in dirs:
-            send(full[a], (f,), full[a], (f,), ("w", a, "own", d), dev[d], kind="big")
+            if d == "xh":
+                send(full[a], (f,), full[a], (f,), ("w", a, "own", d), dev[d], kind="big")
+        for i in range(2):
+            for d, k in (("y+", i), ("y-", 1 - i)):
+                if d in dirs:
+                    at = (f, pl.ds(*halves[a][k]))
+                    send(full[a], at, full[a], at, ("w", a, "own", d, i), dev[d], kind="big")
 
     def w_fwd(a):
         arr = full[a]
         for d, blk, k in (("y+", left["c"], 0), ("y-", right["c"], 1)):
-            arrived(arr, (blk,), ("w", a, "own", d))
-            part = pl.ds(*halves[a][k])
-            send(arr, (blk, part), arr, (blk, part), ("w", a, "fwd", d), dev[d], kind="big")
+            at = (blk, pl.ds(*halves[a][k]))
+            arrived(arr, at, ("w", a, "own", d, 0))
+            send(arr, at, arr, at, ("w", a, "fwd", d), dev[d], kind="big")
 
     def w_pass(a):
         arr, blk = full[a], own["o"]
@@ -313,24 +321,13 @@
             arrived(arr, (blk, pl.ds(*halves[a][k])), ("w", a, "fwd", d))
         send(arr, (blk,), arr, (blk,), ("w", a, "far"), dev["xh"], kind="big")
 
-    def w_fwd_o(a):
-        arr = full[a]
-        for d, blk, k in (("y+", left["o"], 0), ("y-", right["o"], 1)):
-            arrived(arr, (blk,), ("w", a, "pass", d))
-            part = pl.ds(*halves[a][k])
-            send(arr, (blk, part), arr, (blk, part), ("w", a, "fwdo", d), dev[d], kind="big")
-
-    def w_last_y(a):
-        arr = full[a]
-        for blk, nm in ((far["c"], "fwd"), (far["o"], "fwdo")):
-            for d, k in (("y+", 0), ("y-", 1)):
-                arrived(arr, (blk, pl.ds(*halves[a][k])), ("w", a, nm, d))
-
     def w_last(a):
         arr = full[a]
         arrived(arr, (left["o"],), ("w", a, "pass", "y+"))
         arrived(arr, (right["o"],), ("w", a, "pass", "y-"))
         arrived(arr, (far["o"],), ("w", a, "far"))
+        for d, blk, k in (("y+", left["c"], 1), ("y-", right["c"], 0)):
+            arrived(arr, (blk, pl.ds(*halves[a][k])), ("w", a, "own", d, 1))
 
     def ag_xl(buf, nm):
         send(buf, (z, xl), buf, (z, xl), (nm, "xl"), dev["xl"])
@@ -365,6 +362,24 @@
     def ag_last(buf, nm, hh=()):
         arrived(buf, (zblk[4], 0, *hh), (nm, "z+", 4, *hh))
         arrived(buf, (zblk[4], 1, *hh), (nm, "z-", 4, *hh))
+
+    def pair_send(buf, nm, *ks):
+        for k in ks:
+            at = (zblk[k], xl)
+            send(buf, at, buf, at, (nm, "pair", k), dev["xl"])
+
+    def pair_wait(buf, nm, *ks):
+        for k in ks:
+            arrived(buf, (zblk[k], ol), (nm, "pair", k))
+
+    def own_wait(buf, nm, k):
+        for d, b in (("z+", zblk[NZ - k]), ("z-", zblk[k])):
+            arrived(buf, (b, xl), (nm, d, k, 0))
+
+    def z_send(buf, nm, k, j):
+        for d, b in (("z+", zblk[NZ - k]), ("z-", zblk[k])):
+            at = (b, (xl, ol)[j])
+            send(buf, at, buf, at, (nm, d, k + 1, j), dev[d])
 
     def act(buf, i):
         return jnp.concatenate([buf[i, :, h].reshape(PW, TH) for h in range(H)], axis=1)
@@ -394,7 +409,6 @@
         dy = together(dys)
         parts = (
             (0, dot(together([wd[b, 0:PW] for b in blks]), dy, 0, 0)),
-            (DH, dot(together([wgu[b, :, UW - 128 : UW] for b in blks]), dy, 0, 0)),
         )
         for r, part in parts:
             at = pl.ds(r, part.shape[0])
@@ -405,22 +419,38 @@
         at = pl.ds(DH + 128, 16)
         dh[at, :] = part if 0 in ks else dh[at, :] + part
 
+    def dhidden_mid():
+        lhs = together([wgu[b, :, UW - 128 : UW] for b in range(NF)])
+        dh[DH : DH + 128, :] = dot(lhs, together([act(dy_all, b) for b in range(NF)]), 0, 0)
+
     def hidden():
         def body(r):
             gate = gu[pl.ds(r, 16), :]
             up = gu[pl.ds(pl.multiple_of(FL + r, 16), 16), :]
             hid[pl.ds(r, 16), :] = (gate * jax.nn.sigmoid(gate) * up).astype(BF16)
 
-        rows(FL, 16, body)
+        rows(FL, 48, lambda r: [body(pl.multiple_of(r + k, 16)) for k in (0, 16, 32)])
         hid_mid[0:96, :] = jnp.zeros((96, T), BF16)
         hid_mid[96:128, :] = hid[DH : DH + 32, :]
 
     def normalize():
         row_scale = lax.rsqrt(collect(ssq_in, tp_peers, "ssq") / D + EPS)
         scale[...] = row_scale
-        u = unit[...] * row_scale
-        unit[...] = u
-        n_all[z, xl] = (u * gain[:, 0:1]).astype(BF16)
+        unit[...] = unit[...] * row_scale
+
+    def norm_own():
+        n_all[z, xl] = (unit[...] * gain[:, 0:1]).astype(BF16)
+
+    def norm_blocks(*ks):
+        for k in ks:
+            b = zblk[k]
+            for q in range(NXL):
+                g = gain_all[pl.ds(pl.multiple_of(b * PW + q * W, 8), W), :]
+                for c in range(T // 128):
+                    at = slice(c * 128, (c + 1) * 128)
+                    n_all[b, q, :, at] = (
+                        x_all[b, q, :, at].astype(F32) * scale[:, at] * g
+                    ).astype(BF16)
 
     def cotangents():
         stat[...] = jnp.zeros_like(stat)
@@ -439,7 +469,7 @@
             both = d_gate.astype(F32) * gate + d_up.astype(F32) * up
             stat[...] += both[0:8] + both[8:16]
 
-        rows(FL, 16, elementwise)
+        rows(FL, 48, lambda r: [elementwise(pl.multiple_of(r + k, 16)) for k in (0, 16, 32)])
         stat_in[t] = jnp.sum(stat[...], axis=0, keepdims=True)
         spread(stat_in, t, tp_peers, "stat")
 
@@ -462,25 +492,28 @@
             blk = jnp.where(w == 0, zblk[5 - k], zblk[3 + k])
             part = dot(wgu[blk, :, 0:GU], dgu[0:GU, :], 1, 0).reshape(NXL, W, T)
             for hh in range(H):
-                pf[w, hh] = part[:, :, hh * TH : (hh + 1) * TH]
+                pf[k - 2, w, hh] = part[:, :, hh * TH : (hh + 1) * TH]
             return c
 
         lax.fori_loop(0, 2, body, 0)
 
-    def rs_step(k, hs=range(H)):
+    def rs_free():
+        for h in range(H):
+            for d, w in ways:
+                q = 1 - w
+                pdn[1 + w, h, q] = pf[0, w, h, q].astype(BF16)
+                send(pdn, (1 + w, h, q), rdn, (w, 1, h, q), ("rs", d, 2, h), dev[d], q=q)
+
+    def rs_step(k, ahead=(True, False), hs=range(H)):
         slot = 2 * k - 3
-        if k == 2:
+        for first in ahead:
             for h in hs:
                 for d, w in ways:
-                    q = 1 - w
-                    pdn[slot + w, h, q] = pf[w, h, q].astype(BF16)
-                    send(pdn, (slot + w, h, q), rdn, (w, k - 1, h, q), ("rs", d, k, h), dev[d], q=q)
-        for h in hs:
-            for j in range(2 if k > 2 else 1):
-                for d, w in ways:
-                    q = w if k == 2 else (ol, xl)[j]
+                    q = 1 - w if first else w
                     arrived(rdn, (w, k - 2, h, q), ("rs", d, k - 1, h), q=q)
-                    pdn[slot + w, h, q] = (pf[w, h, q] + rdn[w, k - 2, h, q].astype(F32)).astype(BF16)
+                    pdn[slot + w, h, q] = (
+                        pf[k - 2, w, h, q] + rdn[w, k - 2, h, q].astype(F32)
+                    ).astype(BF16)
                     send(pdn, (slot + w, h, q), rdn, (w, k - 1, h, q), ("rs", d, k, h), dev[d], q=q)
 
     def rs_own():
@@ -492,18 +525,20 @@
 
         lax.fori_loop(0, 1, body, 0)
 
-    def rs_last():
-        for h in range(H):
-            for q in (ol, xl):
-                for d, w in ways:
-                    arrived(rdn, (w, 3, h, q), ("rs", d, 4, h), q=q)
-                if q is ol:
-                    xs[h] = (
-                        pown[h, q] + rdn[0, 3, h, q].astype(F32) + rdn[1, 3, h, q].astype(F32)
-                    ).astype(BF16)
-                    send(xs, (h,), xr, (h,), ("rx", h), dev["xl"])
-
-    def dx_part(h, norm_stat):
+    def rs_last(h):
+        for q in (ol, xl):
+            for d, w in ways:
+                arrived(rdn, (w, 3, h, q), ("rs", d, 4, h), q=q)
+            if q is ol:
+                xs[h] = (
+                    pown[h, q] + rdn[0, 3, h, q].astype(F32) + rdn[1, 3, h, q].astype(F32)
+                ).astype(BF16)
+                send(xs, (h,), xr, (h,), ("rx", h), dev["xl"])
+
+    def take_stat():
+        nstat[...] = collect(stat_in, tp_peers, "stat") / D
+
+    def dx_part(h):
         arrived(xr, (h,), ("rx", h))
         cols = slice(h * TH, (h + 1) * TH)
         d_normed = (
@@ -514,14 +549,28 @@
         )
         u = unit[:, cols]
         dx = dy_all[z, xl, h].astype(F32) + scale[:, cols] * (
-            d_normed * gain[:, 0:1] - u * norm_stat[:, cols]
+            d_normed * gain[:, 0:1] - u * nstat[:, cols]
         )
         dxs[h] = dx.astype(BF16)
-        return d_normed * u
-
-    def gain_dx(parts):
+        gx[h] = d_normed * u
+
+    def dx_send(h):
+        dx_part(h)
+        for d, name in (
+            ("xl", ("xl", h)),
+            ("z+", ("z+", 1, 0, h)),
+            ("z-", ("z-", 1, 0, h)),
+            ("core", ("core", h)),
+        ):
+            send(dxs, (h,), dy_all, (z, xl, h), ("e", *name), across[d])
+
+    def gain_dx():
         total = dot(
-            jnp.ones((8, T), F32), jnp.concatenate(parts, axis=1), 1, 1, lax.Precision.HIGHEST
+            jnp.ones((8, T), F32),
+            jnp.concatenate([gx[h] for h in range(H)], axis=1),
+            1,
+            1,
+            lax.Precision.HIGHEST,
         )
         gain_in[f] = total
         spread(gain_in, f, fs_peers, "gain")
@@ -543,7 +592,7 @@
             dst[i, 0:PW, :] = dot(dy, hid[0:DH, :], 1, 1).astype(dst.dtype)
             dst[i, PW:DR, 0:PW] = dot(hid[FL - 16 : FL, :], dy, 1, 1).astype(dst.dtype)
 
-    direct = [far["o"], right["o"], left["o"]]
+    direct = [right["o"], left["o"], far["o"]]
     kept = [far["c"], own["o"], right["c"], left["c"], own["c"]]
 
     def g_first(a, lo=0, hi=3):
@@ -552,7 +601,7 @@
 
         def body(i, c):
             wgrad(a, pick(i, direct), sg[a], i)
-            to = pick(i, [dev[d][1] for d in ("xh", "y+", "y-")])
+            to = pick(i, [dev[d][1] for d in ("y+", "y-", "xh")])
             copy(sg[a].at[i], rg[a].at[i], pick(i, sm), rm + i, (s, to, t)).start()
             return c
 
@@ -580,8 +629,8 @@
         rows(n, st, body)
 
     def g_far(a):
-        arrived(rg[a], (0,), ("g", a, 0), q=0)
-        g_sum(a, 3, 0, (0,))
+        arrived(rg[a], (2,), ("g", a, 0), q=2)
+        g_sum(a, 3, 0, (2,))
         for d, k in (("y+", 0), ("y-", 1)):
             part = pl.ds(*halves[a][k])
             send(sg[a], (3, part), rg[a], (3, part), ("g", a, 3, d), dev[d], kind="big")
@@ -596,49 +645,51 @@
             send(sg[a], (slot, part), rg[a], (slot, part), ("g", a, slot, waits), dev[d], kind="big")
 
     def g_partner(a):
+        arrived(rg[a], (0,), ("g", a, 0), q=0)
         arrived(rg[a], (1,), ("g", a, 0), q=1)
-        arrived(rg[a], (2,), ("g", a, 0), q=2)
-        g_sum(a, 6, 1, (1, 2))
+        g_sum(a, 6, 1, (0, 1))
         send(sg[a], (6,), rg[a], (6,), ("g", a, 6), dev["xh"], kind="big")
+
+    def g_most(a):
+        for k in (0, 1):
+            part = pl.ds(*halves[a][1 - k])
+            arrived(rg[a], (4 + k, part), ("g", a, 4 + k, False))
+        arrived(rg[a], (6,), ("g", a, 6))
+        for k in (0, 1):
+            lo, n = halves[a][1 - k]
+
+            def body(r, k=k, lo=lo):
+                at = pl.ds(pl.multiple_of(r + lo, 16), 16)
+                fg[a][4, at, :] += rg[a][4 + k, at, :].astype(F32) + rg[a][6, at, :].astype(F32)
+
+            rows(n, 16, body)
 
     def g_last(a):
         for k in (0, 1):
-            for waits in (False, True):
-                part = pl.ds(*halves[a][k if waits else 1 - k])
-                arrived(rg[a], (4 + k, part), ("g", a, 4 + k, waits))
-        arrived(rg[a], (6,), ("g", a, 6))
-
-        def total(at):
-            v = fg[a][4, at, :]
-            for k in (4, 5, 6):
-                v = v + rg[a][k, at, :].astype(F32)
-            return v
-
-        def body(r):
-            at = pl.ds(r, 32)
-            v = total(at)
-            if a == "u":
-                gg_ref[at, :] = v[:, 0:FL]
-                ug_ref[at, :] = v[:, FL:GU]
-                dg_ref[at, DH : DH + 32] = v[:, GU:UW]
-            else:
-                dg_ref[at, 0:DH] = v
-
-        if a == "d":
-            rows(PW, 32, body)
-            v = total(pl.ds(PW, 16))[:, 0:PW]
-            unit16 = (
-                lax.broadcasted_iota(jnp.int32, (16, 16), 0)
-                == lax.broadcasted_iota(jnp.int32, (16, 16), 1)
-            ).astype(F32)
-            dg_ref[:, DH + 32 : FL] = dot(v, unit16, 0, 0, lax.Precision.HIGHEST)
-            return
-        for c in range(2):
-            def part(r, c=c):
-                body(pl.multiple_of(r + c * 160, 16))
-
-            rows(160, 32, part)
-            at = pl.ds(c * 160, 160)
+            lo, n = halves[a][k]
+            arrived(rg[a], (4 + k, pl.ds(lo, n)), ("g", a, 4 + k, True))
+
+            def total(at, k=k):
+                return fg[a][4, at, :] + rg[a][4 + k, at, :].astype(F32)
+
+            def body(r, total=total, lo=lo):
+                at = pl.ds(pl.multiple_of(r + lo, 16), 32)
+                v = total(at)
+                if a == "u":
+                    gg_ref[at, :] = v[:, 0:FL]
+                    ug_ref[at, :] = v[:, FL:GU]
+                    dg_ref[at, DH : DH + 32] = v[:, GU:UW]
+                else:
+                    dg_ref[at, 0:DH] = v
+
+            rows(160, 32, body)
+            if n > 160:
+                v = total(pl.ds(PW, 16))[:, 0:PW]
+                unit16 = (
+                    lax.broadcasted_iota(jnp.int32, (16, 16), 0)
+                    == lax.broadcasted_iota(jnp.int32, (16, 16), 1)
+                ).astype(F32)
+                dg_ref[:, DH + 32 : FL] = dot(v, unit16, 0, 0, lax.Precision.HIGHEST)
 
     def finish():
         gn_ref[...] = collect(gain_in, fs_peers, "gain")[0:1]
@@ -648,78 +699,96 @@
     def _():
         ctx[0] = 1
         ag_own(dy_all, "dy")
+        ag_own(x_all, "n")
         w_own("d", ("y+", "y-", "xh"))
-        w_own("u", ("y+", "y-"))
+        w_own("u", ("y+", "y-", "xh"))
         take_gain()
-        normalize()
-        ag_own(n_all, "n")
-        w_own("u", ("xh",))
         ag_partner(dy_all, "dy")
         ag_fwd(dy_all, "dy", 1, 0)
+        normalize()
+        ag_partner(x_all, "n")
+        ag_fwd(x_all, "n", 1, 0)
         w_fwd("d")
-        ag_partner(n_all, "n")
-        ag_fwd(n_all, "n", 1, 0)
         ag_fwd(dy_all, "dy", 1, 1)
+        ag_fwd(dy_all, "dy", 2, 0)
         w_fwd("u")
         w_pass("d")
-        ag_fwd(n_all, "n", 1, 1)
+        ag_fwd(x_all, "n", 1, 1)
+        ag_fwd(x_all, "n", 2, 0)
         w_far("d")
-        ag_fwd(dy_all, "dy", 2, 0)
+        norm_blocks(0, 1, 7)
+        ag_fwd(dy_all, "dy", 2, 1)
         w_pass("u")
-        ag_fwd(n_all, "n", 2, 0)
         w_far("u")
-        ag_fwd(n_all, "n", 2, 1)
-        ag_fwd(dy_all, "dy", 2, 1)
-        ag_fwd3(n_all, "n")
-        pl.semaphore_signal(go, inc=1, device_id=dev["core"], device_id_type=MESH)
+        ag_fwd(x_all, "n", 2, 1)
+        norm_blocks(2, 6)
         ag_fwd3(dy_all, "dy")
         w_last("d")
+        dhidden(0, 1, 7)
+        ag_fwd3(x_all, "n")
+        pl.semaphore_signal(go, inc=1, device_id=dev["core"], device_id_type=MESH)
+        norm_blocks(3, 5)
+        dhidden(2, 6, 3, 5)
         w_last("u")
-        dhidden(0, 1, 7)
         forward(0, 1, 7)
-        forward(2, 6, 3, 5)
-        dhidden(2, 6, 3, 5)
-        ag_last(n_all, "n")
-        forward(4)
+        pl.semaphore_signal(go, inc=1, device_id=dev["core"], device_id_type=MESH)
         ag_last(dy_all, "dy")
         dhidden(4)
+        dhidden_mid()
+        ag_last(x_all, "n")
+        norm_blocks(4)
+        forward(2, 6, 3, 5, 4)
         cotangents()
         rs_first()
         rs_compute(2)
+        rs_free()
+        rs_step(2, (False,), (0,))
         hidden()
-        rs_step(2)
         rs_compute(3)
-        rs_step(3)
+        rs_step(2, (False,), (1,))
+        left_all("big")
+        g_first("u", 0, 1)
+        rs_step(3, (True,), (0,))
+        rs_step(3, (True,), (1,))
+        rs_step(3, (False,), (0,))
         rs_compute(4)
-        rs_step(4)
+        rs_step(3, (False,), (1,))
+        g_first("u", 1, 2)
+        rs_step(4, (True,), (0,))
+        rs_own()
+        rs_step(4, (False,), (0,))
+        rs_step(4, (False,), (1,))
+        g_kept("d", 0, 1)
+        rs_step(4, (True,), (1,))
+        rs_last(0)
+        g_first("d", 1, 2)
+        g_kept("d", 1, 2)
+        rs_last(1)
         pl.semaphore_signal(go, inc=1, device_id=dev["core"], device_id_type=MESH)
-        rs_own()
-        left_all("big")
-        g_first("u", 1, 3)
-        rs_last()
-        norm_stat = collect(stat_in, tp_peers, "stat") / D
-        parts = []
-        for h in range(H):
-            parts.append(dx_part(h, norm_stat))
-            for d, name in (("xl", ("xl", h)), ("z+", ("z+", 1, 0, h)), ("z-", ("z-", 1, 0, h)), ("core", ("core", h))):
-                send(dxs, (h,), dy_all, (z, xl, h), ("e", *name), across[d])
-        g_first("u", 0, 1)
+        g_first("d", 0, 1)
+        take_stat()
+        dx_send(0)
+        dx_send(1)
+        g_first("u", 2, 3)
+        g_kept("u", 1, 2)
+        g_kept("u", 0, 1)
+        g_first("d", 2, 3)
         g_kept("u", 2, 4)
         g_near("u", False)
-        g_first("d")
-        gain_dx(parts)
-        g_kept("u", 0, 2)
+        gain_dx()
         g_partner("u")
-        g_kept("d", 0, 4)
+        g_kept("d", 4, 5)
+        g_kept("d", 2, 4)
+        g_near("d", False)
         g_far("u")
+        g_partner("d")
+        g_kept("u", 4, 5)
         g_far("d")
-        g_partner("d")
-        g_near("d", False)
-        g_kept("u", 4, 5)
-        g_kept("d", 4, 5)
         g_near("u", True)
         g_near("d", True)
+        g_most("u")
         g_last("u")
+        g_most("d")
         g_last("d")
         finish()
         ctx[0] = None
@@ -729,79 +798,104 @@
         ctx[0] = 0
         take_gain()
         normalize()
+        norm_own()
         pl.semaphore_wait(go, 1)
-        ag_own(n_all, "m")
+        ag_xl(n_all, "m")
         w_own("d", ("y+", "y-", "xh"))
         w_own("u", ("y+", "y-", "xh"))
+        pl.semaphore_wait(go, 1)
+        ag_z(n_all, "m")
         ag_partner(n_all, "m")
-        ag_fwd(n_all, "m", 1, 0)
         w_fwd("d")
-        ag_fwd(n_all, "m", 1, 1)
+        own_wait(n_all, "m", 1)
+        z_send(n_all, "m", 1, 0)
         w_fwd("u")
         w_pass("d")
+        own_wait(n_all, "m", 2)
+        pair_send(n_all, "m", 2, 6)
         w_far("d")
         w_pass("u")
         w_far("u")
         pl.semaphore_wait(go, 1)
-        ag_fwd(n_all, "m", 2, 0)
-        ag_fwd(n_all, "m", 2, 1)
-        w_last("d")
-        w_last("u")
-        forward(0, 1, 7)
+        z_send(n_all, "m", 2, 0)
+        pair_wait(n_all, "m", 2, 6)
+        z_send(n_all, "m", 2, 1)
         for h in range(H):
             ag_partner(dy_all, "e", (h,))
         ag_fwd3(n_all, "m")
-        forward(2, 6)
         for h in range(H):
             for j in range(2):
                 ag_fwd(dy_all, "e", 1, j, (h,))
-        forward(3, 5)
+        w_last("d")
+        w_last("u")
+        arrived(n_all, (zblk[7], ol), ("m", "z+", 1, 1))
+        arrived(n_all, (zblk[1], ol), ("m", "z-", 1, 1))
+        forward(0, 1, 7)
         for h in range(H):
             for j in range(2):
                 ag_fwd(dy_all, "e", 2, j, (h,))
-        ag_last(n_all, "m")
-        forward(4)
-        hidden()
+        forward(2, 6, 3, 5)
         for h in range(H):
             arrived(dy_all, (z, xl, h), ("e", "core", h))
         dhidden(0, 1, 7)
         for h in range(H):
             ag_fwd3(dy_all, "e", (h,))
+        ag_last(n_all, "m")
+        forward(4)
+        hidden()
         dhidden(2, 6, 3, 5)
         for h in range(H):
             ag_last(dy_all, "e", (h,))
         dhidden(4)
+        dhidden_mid()
         cotangents()
+        left_all("big")
+        g_first("u", 0, 2)
         rs_first()
-        left_all("big")
-        g_first("u")
+        g_first("u", 2, 3)
         rs_compute(2)
-        rs_step(2)
+        rs_free()
         g_kept("u", 2, 4)
         g_near("u", False)
-        g_first("d")
+        g_first("d", 1, 2)
+        rs_step(2, (False,), (0,))
+        g_kept("u", 1, 2)
+        rs_step(2, (False,), (1,))
         rs_compute(3)
-        rs_step(3, (0,))
-        rs_step(3, (1,))
-        g_kept("u", 0, 2)
+        rs_step(3, (True,), (0,))
+        g_first("d", 2, 3)
+        g_first("d", 0, 1)
+        rs_step(3, (True,), (1,))
+        rs_compute(4)
+        rs_step(3, (False,), (0,))
+        rs_own()
+        rs_step(3, (False,), (1,))
+        g_partner("u")
+        rs_step(4, (True,), (0,))
+        g_kept("u", 0, 1)
         g_far("u")
-        g_partner("u")
-        rs_compute(4)
-        rs_step(4)
-        g_kept("d", 0, 4)
+        rs_step(4, (True,), (1,))
+        g_kept("d", 0, 1)
+        rs_step(4, (False,), (0,))
+        g_kept("d", 4, 5)
         g_far("d")
+        rs_step(4, (False,), (1,))
+        g_kept("d", 1, 2)
+        g_kept("d", 2, 4)
         g_near("d", False)
-        rs_own()
-        rs_last()
-        norm_stat = collect(stat_in, tp_peers, "stat") / D
+        rs_last(0)
+        rs_last(1)
         g_partner("d")
         g_kept("u", 4, 5)
-        g_kept("d", 4, 5)
         g_near("u", True)
-        parts = [dx_part(h, norm_stat) for h in range(H)]
-        gain_dx(parts)
         g_near("d", True)
+        take_stat()
+        dx_part(0)
+        g_most("u")
+        dx_part(1)
+        gain_dx()
         g_last("u")
+        g_most("d")
         g_last("d")
         finish()
         ctx[0] = None
@@ -844,6 +938,9 @@
             pltpu.VMEM((PW, FL), BF16),
             pltpu.VMEM((PW, FL), BF16),
             pltpu.VMEM((W, 128), F32),
+            pltpu.VMEM((128, 128), F32),
+            pltpu.VMEM((D, 128), F32),
+            pltpu.VMEM((NZ, NXL, W, T), BF16),
             pltpu.VMEM((NF, PW, UW), BF16),
             pltpu.VMEM((NF, DR, DH), BF16),
             pltpu.VMEM((NZ, NXL, W, T), BF16),
@@ -861,8 +958,10 @@
             pltpu.VMEM((NF, 8, W), F32),
             pltpu.VMEM((7, H, NXL, W, TH), BF16),
             pltpu.VMEM((2, 4, H, NXL, W, TH), BF16),
-            pltpu.VMEM((2, H, NXL, W, TH), F32),
+            pltpu.VMEM((3, 2, H, NXL, W, TH), F32),
             pltpu.VMEM((H, NXL, W, TH), F32),
+            pltpu.VMEM((H, W, TH), F32),
+            pltpu.VMEM((1, T), F32),
             pltpu.VMEM((H, W, TH), BF16),
             pltpu.VMEM((H, W, TH), BF16),
             pltpu.VMEM((H, W, TH), BF16),

time: 117 us -> 117 us (level)
  no operation moved by 1% of the time
where the time goes in v6:
time: 117 us; the launch traced here: 116 us
  Pallas kernels  116 us (99%)
    pallas_call x1, Pallas kernels, body(): pl.pallas_call(fused_kernel, name='fused', out_shape=[pltpu.VMEM(o.shape,...  114 us

profile of v6, /device:TPU:2, one launch (start us, length us, event | category | flops | bytes accessed | tf_op | source)
XLA Modules:
  0.0 116.5 jit_solution(3448469813421902810)
XLA Ops:
  0.6 114.3 %fused.1 = (bf16[512,160]{1,0:T(8,128)(2,1)S(1)}, f32[320,432]{1,0:T(8,128)S(1)}, f32[320,432]{1,0:T(8,128)S(1)}, f32[320,432]{1,0:T(8,128)S(1)}, f32[1,160]{1,0:T(1,128)S(1)}) custom-call(bf16[512,160]{1,0:T(8,128)(2,1)} %bitcast.16, bf16[512,160]{1,0:T(8,128)(2,1)} %bitcast.17, f32[1,2560]{1,0:T(1,128)} %gain_hbm.1, bf16[320,432]{1,0:T(8,128)(2,1)} %bitcast.13, ...), custom_call_target="tpu_custom_call" | custom-call | tf_op jit(solution)/shard_map/fused/pallas_call | solution.py:927
  114.9 1.4 %put.1 = (bf16[512,160]{1,0:T(8,128)(2,1)}, f32[320,432]{1,0:T(8,128)}, f32[320,432]{1,0:T(8,128)}, f32[320,432]{1,0:T(8,128)}, f32[1,160]{1,0:T(1,128)}) custom-call(bf16[512,160]{1,0:T(8,128)(2,1)S(1)} %get-tuple-element.15.refs_0_, f32[320,432]{1,0:T(8,128)S(1)} %get-tuple-element.16.refs_1_, f32[320,432]{1,0:T(8,128)S(1)} %get-tuple-element.17.refs_2_, ...), custom_call_target="tpu_custom_call" | custom-call | tf_op jit(solution)/shard_map/put/pallas_call | solution.py:983

commit v7 on v6

--- a/solution.py
+++ b/solution.py
@@ -27,8 +27,8 @@
 DR = PW + 16
 NCOMMON = 79
 NEACH = 48
-NBIG = 20
-NSMALL = 27
+NBIG = 16
+NSMALL = 20
 
 
 def dot(a, b, ca, cb, precision=None):
@@ -196,7 +196,7 @@
         lax.fori_loop(0, n // step, body, 0)
 
     barrier = pltpu.get_barrier_semaphore()
-    everyone = tp_peers + fs_peers + list(across.values())
+    everyone = tp_peers[4:11] + tp_peers[:4] + tp_peers[11:] + fs_peers + list(across.values())
     for to in everyone:
         pl.semaphore_signal(barrier, inc=1, device_id=to, device_id_type=MESH)
 
@@ -292,15 +292,14 @@
     halves = {"u": ((0, 160), (160, 160)), "d": ((0, 160), (160, 176))}
     full = {"u": wgu, "d": wd}
 
-    def w_own(a, dirs):
-        for d in dirs:
-            if d == "xh":
-                send(full[a], (f,), full[a], (f,), ("w", a, "own", d), dev[d], kind="big")
-        for i in range(2):
+    def w_own_x(a):
+        send(full[a], (f,), full[a], (f,), ("w", a, "own", "xh"), dev["xh"], kind="big")
+
+    def w_own_y(a, *parts):
+        for i in parts:
             for d, k in (("y+", i), ("y-", 1 - i)):
-                if d in dirs:
-                    at = (f, pl.ds(*halves[a][k]))
-                    send(full[a], at, full[a], at, ("w", a, "own", d, i), dev[d], kind="big")
+                at = (f, pl.ds(*halves[a][k]))
+                send(full[a], at, full[a], at, ("w", a, "own", d, i), dev[d], kind="big")
 
     def w_fwd(a):
         arr = full[a]
@@ -700,8 +699,10 @@
         ctx[0] = 1
         ag_own(dy_all, "dy")
         ag_own(x_all, "n")
-        w_own("d", ("y+", "y-", "xh"))
-        w_own("u", ("y+", "y-", "xh"))
+        w_own_x("d")
+        w_own_y("d", 0, 1)
+        w_own_y("u", 0, 1)
+        w_own_x("u")
         take_gain()
         ag_partner(dy_all, "dy")
         ag_fwd(dy_all, "dy", 1, 0)
@@ -732,12 +733,13 @@
         w_last("u")
         forward(0, 1, 7)
         pl.semaphore_signal(go, inc=1, device_id=dev["core"], device_id_type=MESH)
+        forward(2, 6, 3, 5)
+        ag_last(x_all, "n")
+        norm_blocks(4)
+        forward(4)
         ag_last(dy_all, "dy")
         dhidden(4)
         dhidden_mid()
-        ag_last(x_all, "n")
-        norm_blocks(4)
-        forward(2, 6, 3, 5, 4)
         cotangents()
         rs_first()
         rs_compute(2)
@@ -799,53 +801,58 @@
         take_gain()
         normalize()
         norm_own()
+        ag_xl(n_all, "m")
         pl.semaphore_wait(go, 1)
-        ag_xl(n_all, "m")
-        w_own("d", ("y+", "y-", "xh"))
-        w_own("u", ("y+", "y-", "xh"))
+        w_own_x("d")
+        w_own_y("d", 0, 1)
+        w_own_y("u", 0)
+        w_own_x("u")
         pl.semaphore_wait(go, 1)
         ag_z(n_all, "m")
         ag_partner(n_all, "m")
         w_fwd("d")
+        w_own_y("u", 1)
+        w_fwd("u")
+        w_pass("d")
         own_wait(n_all, "m", 1)
         z_send(n_all, "m", 1, 0)
-        w_fwd("u")
-        w_pass("d")
+        w_far("d")
         own_wait(n_all, "m", 2)
         pair_send(n_all, "m", 2, 6)
-        w_far("d")
         w_pass("u")
         w_far("u")
         pl.semaphore_wait(go, 1)
         z_send(n_all, "m", 2, 0)
         pair_wait(n_all, "m", 2, 6)
         z_send(n_all, "m", 2, 1)
-        for h in range(H):
-            ag_partner(dy_all, "e", (h,))
-        ag_fwd3(n_all, "m")
-        for h in range(H):
-            for j in range(2):
-                ag_fwd(dy_all, "e", 1, j, (h,))
+        ag_partner(dy_all, "e", (0,))
+        ag_partner(dy_all, "e", (1,))
+        ag_fwd(dy_all, "e", 1, 0, (1,))
+        ag_fwd(dy_all, "e", 1, 1, (0,))
+        ag_fwd(dy_all, "e", 1, 0, (0,))
         w_last("d")
         w_last("u")
         arrived(n_all, (zblk[7], ol), ("m", "z+", 1, 1))
         arrived(n_all, (zblk[1], ol), ("m", "z-", 1, 1))
         forward(0, 1, 7)
-        for h in range(H):
-            for j in range(2):
-                ag_fwd(dy_all, "e", 2, j, (h,))
+        ag_fwd(dy_all, "e", 1, 1, (1,))
+        ag_fwd(dy_all, "e", 2, 0, (1,))
+        ag_fwd(dy_all, "e", 2, 1, (0,))
+        ag_fwd(dy_all, "e", 2, 0, (0,))
+        ag_fwd(dy_all, "e", 2, 1, (1,))
+        ag_fwd3(n_all, "m")
         forward(2, 6, 3, 5)
+        ag_fwd3(dy_all, "e", (0,))
         for h in range(H):
             arrived(dy_all, (z, xl, h), ("e", "core", h))
         dhidden(0, 1, 7)
-        for h in range(H):
-            ag_fwd3(dy_all, "e", (h,))
+        ag_fwd3(dy_all, "e", (1,))
+        dhidden(2, 6, 3, 5)
         ag_last(n_all, "m")
         forward(4)
         hidden()
-        dhidden(2, 6, 3, 5)
-        for h in range(H):
-            ag_last(dy_all, "e", (h,))
+        ag_last(dy_all, "e", (0,))
+        ag_last(dy_all, "e", (1,))
         dhidden(4)
         dhidden_mid()
         cotangents()

time: 117 us -> 115 us (0.983)
  Pallas kernels: 116 us -> 114 us
    pallas_call x1, Pallas kernels: 114 us -> 112 us  [body(): pl.pallas_call(fused_kernel, name='fused', out_shape=[pltpu.VMEM(o.shape,...]
where the time goes in v7:
time: 115 us; the launch traced here: 114 us
  Pallas kernels  114 us (99%)
    pallas_call x1, Pallas kernels, body(): pl.pallas_call(fused_kernel, name='fused', out_shape=[pltpu.VMEM(o.shape,...  112 us

profile of v7, /device:TPU:2, one launch (start us, length us, event | category | flops | bytes accessed | tf_op | source)
XLA Modules:
  0.0 114.4 jit_solution(14378023041697179837)
XLA Ops:
  0.6 112.2 %fused.1 = (bf16[512,160]{1,0:T(8,128)(2,1)S(1)}, f32[320,432]{1,0:T(8,128)S(1)}, f32[320,432]{1,0:T(8,128)S(1)}, f32[320,432]{1,0:T(8,128)S(1)}, f32[1,160]{1,0:T(1,128)S(1)}) custom-call(bf16[512,160]{1,0:T(8,128)(2,1)} %bitcast.16, bf16[512,160]{1,0:T(8,128)(2,1)} %bitcast.17, f32[1,2560]{1,0:T(1,128)} %gain_hbm.1, bf16[320,432]{1,0:T(8,128)(2,1)} %bitcast.13, ...), custom_call_target="tpu_custom_call" | custom-call | tf_op jit(solution)/shard_map/fused/pallas_call | solution.py:934
  112.9 1.4 %put.1 = (bf16[512,160]{1,0:T(8,128)(2,1)}, f32[320,432]{1,0:T(8,128)}, f32[320,432]{1,0:T(8,128)}, f32[320,432]{1,0:T(8,128)}, f32[1,160]{1,0:T(1,128)}) custom-call(bf16[512,160]{1,0:T(8,128)(2,1)S(1)} %get-tuple-element.15.refs_0_, f32[320,432]{1,0:T(8,128)S(1)} %get-tuple-element.16.refs_1_, f32[320,432]{1,0:T(8,128)S(1)} %get-tuple-element.17.refs_2_, ...), custom_call_target="tpu_custom_call" | custom-call | tf_op jit(solution)/shard_map/put/pallas_call | solution.py:990

commit v8 on v7

--- a/solution.py
+++ b/solution.py
@@ -730,9 +730,9 @@
         pl.semaphore_signal(go, inc=1, device_id=dev["core"], device_id_type=MESH)
         norm_blocks(3, 5)
         dhidden(2, 6, 3, 5)
+        pl.semaphore_signal(go, inc=1, device_id=dev["core"], device_id_type=MESH)
         w_last("u")
         forward(0, 1, 7)
-        pl.semaphore_signal(go, inc=1, device_id=dev["core"], device_id_type=MESH)
         forward(2, 6, 3, 5)
         ag_last(x_all, "n")
         norm_blocks(4)
@@ -812,10 +812,10 @@
         ag_partner(n_all, "m")
         w_fwd("d")
         w_own_y("u", 1)
+        own_wait(n_all, "m", 1)
+        z_send(n_all, "m", 1, 0)
         w_fwd("u")
         w_pass("d")
-        own_wait(n_all, "m", 1)
-        z_send(n_all, "m", 1, 0)
         w_far("d")
         own_wait(n_all, "m", 2)
         pair_send(n_all, "m", 2, 6)
@@ -892,9 +892,9 @@
         g_near("d", False)
         rs_last(0)
         rs_last(1)
+        g_near("u", True)
         g_partner("d")
         g_kept("u", 4, 5)
-        g_near("u", True)
         g_near("d", True)
         take_stat()
         dx_part(0)

time: 115 us -> 114 us (level)
  Pallas kernels: 114 us -> 112 us
    pallas_call x1, Pallas kernels: 112 us -> 111 us  [body(): pl.pallas_call(fused_kernel, name='fused', out_shape=[pltpu.VMEM(o.shape,...]
where the time goes in v8:
time: 114 us; the launch traced here: 113 us
  Pallas kernels  112 us (98%)
    pallas_call x1, Pallas kernels, body(): pl.pallas_call(fused_kernel, name='fused', out_shape=[pltpu.VMEM(o.shape,...  111 us

profile of v8, /device:TPU:2, one launch (start us, length us, event | category | flops | bytes accessed | tf_op | source)
XLA Modules:
  0.0 113.0 jit_solution(252636598261840587)
XLA Ops:
  0.6 110.8 %fused.1 = (bf16[512,160]{1,0:T(8,128)(2,1)S(1)}, f32[320,432]{1,0:T(8,128)S(1)}, f32[320,432]{1,0:T(8,128)S(1)}, f32[320,432]{1,0:T(8,128)S(1)}, f32[1,160]{1,0:T(1,128)S(1)}) custom-call(bf16[512,160]{1,0:T(8,128)(2,1)} %bitcast.16, bf16[512,160]{1,0:T(8,128)(2,1)} %bitcast.17, f32[1,2560]{1,0:T(1,128)} %gain_hbm.1, bf16[320,432]{1,0:T(8,128)(2,1)} %bitcast.13, ...), custom_call_target="tpu_custom_call" | custom-call | tf_op jit(solution)/shard_map/fused/pallas_call | solution.py:934
  111.4 1.4 %put.1 = (bf16[512,160]{1,0:T(8,128)(2,1)}, f32[320,432]{1,0:T(8,128)}, f32[320,432]{1,0:T(8,128)}, f32[320,432]{1,0:T(8,128)}, f32[1,160]{1,0:T(1,128)}) custom-call(bf16[512,160]{1,0:T(8,128)(2,1)S(1)} %get-tuple-element.15.refs_0_, f32[320,432]{1,0:T(8,128)S(1)} %get-tuple-element.16.refs_1_, f32[320,432]{1,0:T(8,128)S(1)} %get-tuple-element.17.refs_2_, ...), custom_call_target="tpu_custom_call" | custom-call | tf_op jit(solution)/shard_map/put/pallas_call | solution.py:990

commit v9 on v8

--- a/solution.py
+++ b/solution.py
@@ -760,13 +760,13 @@
         rs_own()
         rs_step(4, (False,), (0,))
         rs_step(4, (False,), (1,))
+        rs_step(4, (True,), (1,))
         g_kept("d", 0, 1)
-        rs_step(4, (True,), (1,))
         rs_last(0)
+        pl.semaphore_signal(go, inc=1, device_id=dev["core"], device_id_type=MESH)
         g_first("d", 1, 2)
         g_kept("d", 1, 2)
         rs_last(1)
-        pl.semaphore_signal(go, inc=1, device_id=dev["core"], device_id_type=MESH)
         g_first("d", 0, 1)
         take_stat()
         dx_send(0)
@@ -827,31 +827,31 @@
         z_send(n_all, "m", 2, 1)
         ag_partner(dy_all, "e", (0,))
         ag_partner(dy_all, "e", (1,))
+        ag_fwd(dy_all, "e", 1, 0, (0,))
         ag_fwd(dy_all, "e", 1, 0, (1,))
         ag_fwd(dy_all, "e", 1, 1, (0,))
-        ag_fwd(dy_all, "e", 1, 0, (0,))
+        ag_fwd(dy_all, "e", 1, 1, (1,))
         w_last("d")
         w_last("u")
+        for h in range(H):
+            arrived(dy_all, (z, xl, h), ("e", "core", h))
+        dhidden(0, 1, 7)
+        ag_fwd(dy_all, "e", 2, 0, (0,))
+        ag_fwd(dy_all, "e", 2, 0, (1,))
+        ag_fwd(dy_all, "e", 2, 1, (0,))
+        ag_fwd(dy_all, "e", 2, 1, (1,))
+        ag_fwd3(n_all, "m")
         arrived(n_all, (zblk[7], ol), ("m", "z+", 1, 1))
         arrived(n_all, (zblk[1], ol), ("m", "z-", 1, 1))
         forward(0, 1, 7)
-        ag_fwd(dy_all, "e", 1, 1, (1,))
-        ag_fwd(dy_all, "e", 2, 0, (1,))
-        ag_fwd(dy_all, "e", 2, 1, (0,))
-        ag_fwd(dy_all, "e", 2, 0, (0,))
-        ag_fwd(dy_all, "e", 2, 1, (1,))
-        ag_fwd3(n_all, "m")
+        ag_fwd3(dy_all, "e", (0,))
+        ag_fwd3(dy_all, "e", (1,))
         forward(2, 6, 3, 5)
-        ag_fwd3(dy_all, "e", (0,))
-        for h in range(H):
-            arrived(dy_all, (z, xl, h), ("e", "core", h))
-        dhidden(0, 1, 7)
-        ag_fwd3(dy_all, "e", (1,))
-        dhidden(2, 6, 3, 5)
         ag_last(n_all, "m")
         forward(4)
         hidden()
         ag_last(dy_all, "e", (0,))
+        dhidden(2, 6, 3, 5)
         ag_last(dy_all, "e", (1,))
         dhidden(4)
         dhidden_mid()

time: 114 us -> 112 us (0.982)
    pallas_call x1, Pallas kernels: 111 us -> 109 us  [body(): pl.pallas_call(fused_kernel, name='fused', out_shape=[pltpu.VMEM(o.shape,...]
where the time goes in v9:
time: 112 us
  Pallas kernels  111 us (99%)
    pallas_call x1, Pallas kernels, body(): pl.pallas_call(fused_kernel, name='fused', out_shape=[pltpu.VMEM(o.shape,...  109 us

profile of v9, /device:TPU:2, one launch (start us, length us, event | category | flops | bytes accessed | tf_op | source)
XLA Modules:
  0.0 111.5 jit_solution(2417381535602975033)
XLA Ops:
  0.6 109.3 %fused.1 = (bf16[512,160]{1,0:T(8,128)(2,1)S(1)}, f32[320,432]{1,0:T(8,128)S(1)}, f32[320,432]{1,0:T(8,128)S(1)}, f32[320,432]{1,0:T(8,128)S(1)}, f32[1,160]{1,0:T(1,128)S(1)}) custom-call(bf16[512,160]{1,0:T(8,128)(2,1)} %bitcast.16, bf16[512,160]{1,0:T(8,128)(2,1)} %bitcast.17, f32[1,2560]{1,0:T(1,128)} %gain_hbm.1, bf16[320,432]{1,0:T(8,128)(2,1)} %bitcast.13, ...), custom_call_target="tpu_custom_call" | custom-call | tf_op jit(solution)/shard_map/fused/pallas_call | solution.py:934
  109.9 1.4 %put.1 = (bf16[512,160]{1,0:T(8,128)(2,1)}, f32[320,432]{1,0:T(8,128)}, f32[320,432]{1,0:T(8,128)}, f32[320,432]{1,0:T(8,128)}, f32[1,160]{1,0:T(1,128)}) custom-call(bf16[512,160]{1,0:T(8,128)(2,1)S(1)} %get-tuple-element.15.refs_0_, f32[320,432]{1,0:T(8,128)S(1)} %get-tuple-element.16.refs_1_, f32[320,432]{1,0:T(8,128)S(1)} %get-tuple-element.17.refs_2_, ...), custom_call_target="tpu_custom_call" | custom-call | tf_op jit(solution)/shard_map/put/pallas_call | solution.py:990

commit v10 on v9

--- a/solution.py
+++ b/solution.py
@@ -847,11 +847,11 @@
         ag_fwd3(dy_all, "e", (0,))
         ag_fwd3(dy_all, "e", (1,))
         forward(2, 6, 3, 5)
+        dhidden(2, 6, 3, 5)
         ag_last(n_all, "m")
         forward(4)
         hidden()
         ag_last(dy_all, "e", (0,))
-        dhidden(2, 6, 3, 5)
         ag_last(dy_all, "e", (1,))
         dhidden(4)
         dhidden_mid()

time: 112 us -> 112 us (level)
  no operation moved by 1% of the time
where the time goes in v10:
time: 112 us
  Pallas kernels  111 us (99%)
    pallas_call x1, Pallas kernels, body(): pl.pallas_call(fused_kernel, name='fused', out_shape=[pltpu.VMEM(o.shape,...  109 us

profile of v10, /device:TPU:2, one launch (start us, length us, event | category | flops | bytes accessed | tf_op | source)
XLA Modules:
  0.0 111.5 jit_solution(10494682595003200912)
XLA Ops:
  0.6 109.3 %fused.1 = (bf16[512,160]{1,0:T(8,128)(2,1)S(1)}, f32[320,432]{1,0:T(8,128)S(1)}, f32[320,432]{1,0:T(8,128)S(1)}, f32[320,432]{1,0:T(8,128)S(1)}, f32[1,160]{1,0:T(1,128)S(1)}) custom-call(bf16[512,160]{1,0:T(8,128)(2,1)} %bitcast.16, bf16[512,160]{1,0:T(8,128)(2,1)} %bitcast.17, f32[1,2560]{1,0:T(1,128)} %gain_hbm.1, bf16[320,432]{1,0:T(8,128)(2,1)} %bitcast.13, ...), custom_call_target="tpu_custom_call" | custom-call | tf_op jit(solution)/shard_map/fused/pallas_call | solution.py:934
  109.9 1.4 %put.1 = (bf16[512,160]{1,0:T(8,128)(2,1)}, f32[320,432]{1,0:T(8,128)}, f32[320,432]{1,0:T(8,128)}, f32[320,432]{1,0:T(8,128)}, f32[1,160]{1,0:T(1,128)}) custom-call(bf16[512,160]{1,0:T(8,128)(2,1)S(1)} %get-tuple-element.15.refs_0_, f32[320,432]{1,0:T(8,128)S(1)} %get-tuple-element.16.refs_1_, f32[320,432]{1,0:T(8,128)S(1)} %get-tuple-element.17.refs_2_, ...), custom_call_target="tpu_custom_call" | custom-call | tf_op jit(solution)/shard_map/put/pallas_call | solution.py:990
